TPU v7x, 32 devices: a whole 2x2x4 slice. The times are simulated.
32 devices in a mesh: owner: 8 (over z, y), rows: 4 (over x, core).
Axes of the slice: x: 2, y: 2, z: 4, core: 2. Of those that a mesh axis runs over, the one named last changes fastest.
Arguments:
- master_down: float32 [16, 6400, 4096], P('owner', None, 'rows'), may hold values from -0.109375 to 0.109375
- router_weight: float32 [4096, 16], P('rows', 'owner'), may hold values from -0.09375 to 0.09375
- router_gain: float32 [4096], P('rows'), may hold values from 0.25 to 1.75
Outputs:
- final_down: bfloat16 [16, 6400, 4096], P('owner', 'rows')
- scale_down: float32 [16, 6400], P('owner', 'rows')
- serve_router: bfloat16 [4096, 16], replicated
All inputs are finite; a program needn't handle non-finite values. Where the computation divides by a largest or mean magnitude, that divisor is 1e-20 or more.
Results may differ from a plain program's by a relative error of at most 0.001.
Values may be sent and summed in bfloat16 or wider, within the bound.
A program may use at most 192 MiB of HBM per device.

v0:
```python
import functools

import jax
import jax.numpy as jnp
from jax import lax
from jax.experimental import pallas as pl
from jax.experimental.pallas import tpu as pltpu
from jax.sharding import PartitionSpec as P

LANES = 128
SLOTS = 3


def rows_per_block(quota, n):
    fits = [r for r in range(16, quota + 1, 16) if quota % r == 0 and (n * r) % LANES == 0]
    small = [r for r in fits if r * n <= 1280 and r <= 160]
    return max(small) if small else (min(fits) if fits else quota)


def kernel(n, owners, steps, first, per, x_ref, weight_ref, gain_ref, out_ref, scale_ref, router_ref, fbuf, nbuf, acc, mine, peers,
           strip, load_sem, send_sem, recv_sem, own_sem, sum_send, sum_recv, strip_send, strip_recv,
           router_send, router_recv):
    me = lax.axis_index("rows")
    home = lax.axis_index("owner")
    rows, width = fbuf.shape[2], fbuf.shape[3]
    groups = width // LANES

    barrier = pltpu.get_barrier_semaphore()
    for d in range(1, n):
        pl.semaphore_signal(
            barrier, inc=1, device_id={"rows": lax.rem(me + d, n)},
            device_id_type=pl.DeviceIdType.MESH,
        )
    for d in range(1, owners):
        pl.semaphore_signal(
            barrier, inc=1, device_id={"owner": lax.rem(home + d, owners)},
            device_id_type=pl.DeviceIdType.MESH,
        )
    strip[me] = (weight_ref[...] * gain_ref[...]).astype(jnp.bfloat16)

    def row_strip(d):
        return pltpu.make_async_remote_copy(
            src_ref=strip.at[me],
            dst_ref=strip.at[me],
            send_sem=strip_send.at[d - 1],
            recv_sem=strip_recv.at[d - 1],
            device_id={"rows": lax.rem(me + d, n)},
            device_id_type=pl.DeviceIdType.MESH,
        )

    def owner_strips(d):
        return pltpu.make_async_remote_copy(
            src_ref=strip,
            dst_ref=router_ref.at[home],
            send_sem=router_send.at[d - 1],
            recv_sem=router_recv.at[d - 1],
            device_id={"owner": lax.rem(home + d, owners)},
            device_id_type=pl.DeviceIdType.MESH,
        )

    def load(t):
        slot = t % SLOTS
        return pltpu.make_async_copy(x_ref.at[t // per, :, t % per], fbuf.at[slot], load_sem.at[slot])

    def prefetch(lo, hi):
        for t in range(lo, min(lo + SLOTS - 1, hi)):
            load(t).start()

    def stream(lo, hi, body):
        def step(t, carry):
            @pl.when(t + SLOTS - 1 < hi)
            def _():
                load(t + SLOTS - 1).start()

            load(t).wait()
            body(t, t % SLOTS)
            return carry

        lax.fori_loop(lo, hi, step, 0)

    def add_up(t, slot):
        for j in range(n):
            part = jnp.abs(fbuf[slot, j, :, :LANES])
            for g in range(1, groups):
                part = part + jnp.abs(fbuf[slot, j, :, g * LANES:(g + 1) * LANES])
            acc[j * rows:(j + 1) * rows, :] = part
        mine[t] = jnp.sum(acc[...].T, axis=0, keepdims=True)

    def exchange(turn, lo, hi):
        return [
            pltpu.make_async_remote_copy(
                src_ref=mine.at[pl.ds(lo, hi - lo)],
                dst_ref=peers.at[d - 1, pl.ds(lo, hi - lo)],
                send_sem=sum_send.at[turn, d - 1],
                recv_sem=sum_recv.at[turn, d - 1],
                device_id={"rows": lax.rem(me + d, n)},
                device_id_type=pl.DeviceIdType.MESH,
            )
            for d in range(1, n)
        ]

    def block(t, d):
        there = lax.rem(me + d, n)
        return pltpu.make_async_remote_copy(
            src_ref=nbuf.at[t, there],
            dst_ref=out_ref.at[t // per, pl.ds(pl.multiple_of((t % per) * rows, rows), rows),
                               pl.ds(pl.multiple_of(me * width, width), width)],
            send_sem=send_sem.at[d - 1, t],
            recv_sem=recv_sem.at[d - 1, t],
            device_id={"rows": there},
            device_id_type=pl.DeviceIdType.MESH,
        )

    def own(t):
        return pltpu.make_async_copy(
            nbuf.at[t, me],
            out_ref.at[t // per, pl.ds(pl.multiple_of((t % per) * rows, rows), rows),
                       pl.ds(pl.multiple_of(me * width, width), width)],
            own_sem.at[t],
        )

    def send(t):
        for d in range(1, n):
            block(t, d).start()
        own(t).start()

    def narrow(t):
        total = mine[t]
        for d in range(1, n):
            total = total + peers[d - 1, t]
        scale = total / (n * width)
        scale_ref[pl.ds(t, 1), :] = scale
        acc[...] = jnp.broadcast_to(1.0 / scale, (LANES, n * rows)).T

    def scale_and_send(lo):
        def body(t, slot):
            narrow(t)
            for j in range(n):
                inverse = acc[j * rows:(j + 1) * rows, :]
                for g in range(groups):
                    cut = slice(g * LANES, (g + 1) * LANES)
                    nbuf[t, j, :, cut] = (fbuf[slot, j, :, cut] * inverse).astype(jnp.bfloat16)

            @pl.when(t > lo)
            def _():
                send(t - 1)

        return body

    prefetch(0, first)
    stream(0, first, add_up)
    prefetch(0, first)
    pl.semaphore_wait(barrier, n - 1 + owners - 1)
    sums = exchange(0, 0, first)
    for copy in sums:
        copy.start()
    for d in range(1, n):
        row_strip(d).start()
    for copy in sums:
        copy.wait()
    stream(0, first, scale_and_send(0))
    for d in range(1, n):
        row_strip(d).wait()
    for d in range(1, owners):
        owner_strips(d).start()
    router_ref[home] = strip[...]
    if first < steps:
        prefetch(first, steps)
        stream(first, steps, add_up)
        prefetch(first, steps)
        sums = exchange(1, first, steps)
        for copy in sums:
            copy.start()
        send(first - 1)
        for copy in sums:
            copy.wait()
        stream(first, steps, scale_and_send(first))
    send(steps - 1)

    def finish(t, carry):
        for d in range(1, n):
            block(t, d).wait()
        own(t).wait()
        return carry

    lax.fori_loop(0, steps, finish, 0)
    for d in range(1, owners):
        owner_strips(d).wait()


def per_device(n, owners, master_down, router_weight, router_gain):
    experts, height, width = master_down.shape
    quota = height // n
    rows = rows_per_block(quota, n)
    per = quota // rows
    steps = experts * per
    first = min(max(3, -(-steps // 8)), steps)
    cut = n * rows
    depth, mine = router_weight.shape
    final_down, scales, strips = pl.pallas_call(
        functools.partial(kernel, n, owners, steps, first, per),
        out_shape=(
            jax.ShapeDtypeStruct((experts, quota, n * width), jnp.bfloat16),
            jax.ShapeDtypeStruct((steps, cut), jnp.float32),
            jax.ShapeDtypeStruct((owners, n, mine, depth), jnp.bfloat16),
        ),
        in_specs=[
            pl.BlockSpec(memory_space=pl.ANY),
            pl.BlockSpec(memory_space=pltpu.VMEM),
            pl.BlockSpec(memory_space=pltpu.VMEM),
        ],
        out_specs=(
            pl.BlockSpec(memory_space=pl.ANY),
            pl.BlockSpec(memory_space=pltpu.VMEM),
            pl.BlockSpec(memory_space=pltpu.VMEM),
        ),
        scratch_shapes=[
            pltpu.VMEM((SLOTS, n, rows, width), jnp.float32),
            pltpu.VMEM((steps, n, rows, width), jnp.bfloat16),
            pltpu.VMEM((cut, LANES), jnp.float32),
            pltpu.VMEM((steps, 1, cut), jnp.float32),
            pltpu.VMEM((n - 1, steps, 1, cut), jnp.float32),
            pltpu.VMEM((n, mine, depth), jnp.bfloat16),
            pltpu.SemaphoreType.DMA((SLOTS,)),
            pltpu.SemaphoreType.DMA((n - 1, steps)),
            pltpu.SemaphoreType.DMA((n - 1, steps)),
            pltpu.SemaphoreType.DMA((steps,)),
            pltpu.SemaphoreType.DMA((2, n - 1)),
            pltpu.SemaphoreType.DMA((2, n - 1)),
            pltpu.SemaphoreType.DMA((n - 1,)),
            pltpu.SemaphoreType.DMA((n - 1,)),
            pltpu.SemaphoreType.DMA((owners - 1,)),
            pltpu.SemaphoreType.DMA((owners - 1,)),
        ],
        compiler_params=pltpu.CompilerParams(
            collective_id=0, has_side_effects=True, vmem_limit_bytes=48 * 1024 * 1024,
        ),
    )(master_down.reshape(experts, n, per, rows, width), router_weight.T, router_gain[None, :])
    by_device = scales.reshape(experts, per, n, rows)
    scale_down = lax.dynamic_index_in_dim(by_device, lax.axis_index("rows"), axis=2, keepdims=False)
    scale_down = scale_down.reshape(experts, quota)

    serve_router = strips.transpose(0, 2, 1, 3).reshape(owners * mine, n * depth).T
    return (final_down, scale_down, serve_router)


def solution(mesh):
    return jax.shard_map(
        functools.partial(per_device, mesh.shape["rows"], mesh.shape["owner"]),
        mesh=mesh,
        in_specs=(P("owner", None, "rows"), P("rows", "owner"), P("rows")),
        out_specs=(P("owner", "rows", None), P("owner", "rows"), P()),
        check_vma=False,
    )
```

profile of v0, /device:TPU:1, one launch (start us, length us, event | category | flops | bytes accessed | tf_op | source)
XLA Modules:
  0.0 320.4 jit_solution(8879563055414213338)
XLA Ops:
  0.6 0.0 copy-start
  0.6 0.7 copy-done
  1.3 0.0 copy-start.1
  1.3 0.7 copy-done.1
  2.0 295.1 %shard_map.58 = (bf16[2,1600,4096]{2,1,0:T(8,128)(2,1)}, f32[20,640]{1,0:T(8,128)S(1)}, bf16[8,4,2,1024]{3,2,1,0:T(2,128)(2,1)S(1)}) custom-call(f32[2,4,10,160,1024]{4,3,2,1,0:T(8,128)} %bitcast.12, f32[2,1024]{1,0:T(2,128)S(1)} %bitcast.10, f32[1,1024]{1,0:T(1,128)S(1)} %bitcast.11), custom_call_target="tpu_custom_call" | custom-call | tf_op jit(solution)/shard_map/pallas_call | solution.py:200
  297.1 0.1 reshape.20
  297.2 0.1 dynamic-slice_reduce_fusion
  297.3 0.7 reshape.21
  298.0 0.1 copy.6
  298.0 0.7 copy.7
  298.7 21.7 %copy.9 = bf16[2,1600,4096]{2,1,0:T(8,128)(2,1)} copy(bf16[2,1600,4096]{2,1,0:T(8,128)(2,1)} %get-tuple-element.12) | data formatting | bytes 52428800
Async XLA Ops:
  0.6 0.7 copy-start
  1.3 0.7 copy-start.1
where the time goes:
time: 321 us; the launch traced here: 320 us
  Pallas kernels  295 us (92%)
  local copies, waits for them, and re-layouts  24.6 us (8%)
    pallas_call x1, Pallas kernels, per_device(): pl.pallas_call(functools.partial(kernel, n, owners, steps, first, per), o...  295 us
    unnamed x6, local copies, waits for them, and re-layouts  23.7 us

commit v1 on v0

--- a/solution.py
+++ b/solution.py
@@ -18,7 +18,7 @@
 
 
 def kernel(n, owners, steps, first, per, x_ref, weight_ref, gain_ref, out_ref, scale_ref, router_ref, fbuf, nbuf, acc, mine, peers,
-           strip, load_sem, send_sem, recv_sem, own_sem, sum_send, sum_recv, strip_send, strip_recv,
+           strip, load_sem, send_sem, recv_sem, sum_send, sum_recv, strip_send, strip_recv,
            router_send, router_recv):
     me = lax.axis_index("rows")
     home = lax.axis_index("owner")
@@ -102,7 +102,7 @@
     def block(t, d):
         there = lax.rem(me + d, n)
         return pltpu.make_async_remote_copy(
-            src_ref=nbuf.at[t, there],
+            src_ref=nbuf.at[t, d - 1],
             dst_ref=out_ref.at[t // per, pl.ds(pl.multiple_of((t % per) * rows, rows), rows),
                                pl.ds(pl.multiple_of(me * width, width), width)],
             send_sem=send_sem.at[d - 1, t],
@@ -111,18 +111,9 @@
             device_id_type=pl.DeviceIdType.MESH,
         )
 
-    def own(t):
-        return pltpu.make_async_copy(
-            nbuf.at[t, me],
-            out_ref.at[t // per, pl.ds(pl.multiple_of((t % per) * rows, rows), rows),
-                       pl.ds(pl.multiple_of(me * width, width), width)],
-            own_sem.at[t],
-        )
-
     def send(t):
         for d in range(1, n):
             block(t, d).start()
-        own(t).start()
 
     def narrow(t):
         total = mine[t]
@@ -135,11 +126,17 @@
     def scale_and_send(lo):
         def body(t, slot):
             narrow(t)
-            for j in range(n):
-                inverse = acc[j * rows:(j + 1) * rows, :]
+            for d in range(n):
+                j = lax.rem(me + d, n)
+                inverse = acc[pl.ds(pl.multiple_of(j * rows, rows), rows), :]
                 for g in range(groups):
                     cut = slice(g * LANES, (g + 1) * LANES)
-                    nbuf[t, j, :, cut] = (fbuf[slot, j, :, cut] * inverse).astype(jnp.bfloat16)
+                    value = (fbuf[slot, j, :, cut] * inverse).astype(jnp.bfloat16)
+                    if d:
+                        nbuf[t, d - 1, :, cut] = value
+                    else:
+                        out_ref[t // per, pl.ds(pl.multiple_of((t % per) * rows, rows), rows),
+                                pl.ds(pl.multiple_of(me * width + g * LANES, LANES), LANES)] = value
 
             @pl.when(t > lo)
             def _():
@@ -180,12 +177,28 @@
     def finish(t, carry):
         for d in range(1, n):
             block(t, d).wait()
-        own(t).wait()
         return carry
 
     lax.fori_loop(0, steps, finish, 0)
     for d in range(1, owners):
         owner_strips(d).wait()
+
+
+CUTS = 10
+
+
+def store(x_ref, out_ref, sem):
+    height = x_ref.shape[1] // CUTS
+
+    def piece(t):
+        return pltpu.make_async_copy(
+            x_ref.at[:, pl.ds(t * height, height)], out_ref.at[:, pl.ds(t * height, height)], sem.at[t]
+        )
+
+    for t in range(CUTS):
+        piece(t).start()
+    for t in range(CUTS):
+        piece(t).wait()
 
 
 def per_device(n, owners, master_down, router_weight, router_gain):
@@ -200,7 +213,7 @@
     final_down, scales, strips = pl.pallas_call(
         functools.partial(kernel, n, owners, steps, first, per),
         out_shape=(
-            jax.ShapeDtypeStruct((experts, quota, n * width), jnp.bfloat16),
+            pltpu.VMEM((experts, quota, n * width), jnp.bfloat16),
             jax.ShapeDtypeStruct((steps, cut), jnp.float32),
             jax.ShapeDtypeStruct((owners, n, mine, depth), jnp.bfloat16),
         ),
@@ -210,13 +223,13 @@
             pl.BlockSpec(memory_space=pltpu.VMEM),
         ],
         out_specs=(
-            pl.BlockSpec(memory_space=pl.ANY),
+            pl.BlockSpec(memory_space=pltpu.VMEM),
             pl.BlockSpec(memory_space=pltpu.VMEM),
             pl.BlockSpec(memory_space=pltpu.VMEM),
         ),
         scratch_shapes=[
             pltpu.VMEM((SLOTS, n, rows, width), jnp.float32),
-            pltpu.VMEM((steps, n, rows, width), jnp.bfloat16),
+            pltpu.VMEM((steps, n - 1, rows, width), jnp.bfloat16),
             pltpu.VMEM((cut, LANES), jnp.float32),
             pltpu.VMEM((steps, 1, cut), jnp.float32),
             pltpu.VMEM((n - 1, steps, 1, cut), jnp.float32),
@@ -224,7 +237,6 @@
             pltpu.SemaphoreType.DMA((SLOTS,)),
             pltpu.SemaphoreType.DMA((n - 1, steps)),
             pltpu.SemaphoreType.DMA((n - 1, steps)),
-            pltpu.SemaphoreType.DMA((steps,)),
             pltpu.SemaphoreType.DMA((2, n - 1)),
             pltpu.SemaphoreType.DMA((2, n - 1)),
             pltpu.SemaphoreType.DMA((n - 1,)),
@@ -233,9 +245,18 @@
             pltpu.SemaphoreType.DMA((owners - 1,)),
         ],
         compiler_params=pltpu.CompilerParams(
-            collective_id=0, has_side_effects=True, vmem_limit_bytes=48 * 1024 * 1024,
+            collective_id=0, has_side_effects=True, vmem_limit_bytes=29 * 1024 * 1024,
         ),
     )(master_down.reshape(experts, n, per, rows, width), router_weight.T, router_gain[None, :])
+    final_down = pl.pallas_call(
+        store,
+        out_shape=jax.ShapeDtypeStruct(final_down.shape, final_down.dtype),
+        in_specs=[pl.BlockSpec(memory_space=pltpu.VMEM)],
+        out_specs=pl.BlockSpec(memory_space=pl.ANY),
+        scratch_shapes=[pltpu.SemaphoreType.DMA((CUTS,))],
+        compiler_params=pltpu.CompilerParams(vmem_limit_bytes=1024 * 1024),
+    )(final_down)
+    final_down, scales, strips = lax.optimization_barrier((final_down, scales, strips))
     by_device = scales.reshape(experts, per, n, rows)
     scale_down = lax.dynamic_index_in_dim(by_device, lax.axis_index("rows"), axis=2, keepdims=False)
     scale_down = scale_down.reshape(experts, quota)

time: 321 us -> 308 us (0.960)
  local copies, waits for them, and re-layouts: 24.6 us -> 1.62 us
  Pallas kernels: 295 us -> 305 us
    unnamed x6 -> x5, local copies, waits for them, and re-layouts: 23.7 us -> 0.71 us
    pallas_call x0 -> x1, Pallas kernels: none -> 8.82 us  [per_device(): pl.pallas_call(store, out_shape=jax.ShapeDtypeStruct(final_down.shape, fi...]
where the time goes in v1:
time: 308 us
  Pallas kernels  305 us (99%)
    pallas_call x1, Pallas kernels, per_device(): pl.pallas_call(functools.partial(kernel, n, owners, steps, first, per), o...  296 us
    pallas_call x1, Pallas kernels, per_device(): pl.pallas_call(store, out_shape=jax.ShapeDtypeStruct(final_down.shape, fi...  8.82 us

profile of v1, /device:TPU:1, one launch (start us, length us, event | category | flops | bytes accessed | tf_op | source)
XLA Modules:
  0.0 307.5 jit_solution(8715341243058257316)
XLA Ops:
  0.6 296.4 %shard_map.58 = (bf16[2,1600,4096]{2,1,0:T(8,128)(2,1)S(1)}, f32[20,640]{1,0:T(8,128)}, bf16[8,4,2,1024]{3,2,1,0:T(2,128)(2,1)}) custom-call(f32[2,4,10,160,1024]{4,3,2,1,0:T(8,128)} %bitcast.9, f32[2,1024]{1,0:T(2,128)} %bitcast.13, f32[1,1024]{1,0:T(1,128)} %bitcast.14), custom_call_target="tpu_custom_call" | custom-call | tf_op jit(solution)/shard_map/pallas_call | solution.py:213
  297.0 0.0 copy-start.1
  297.0 0.0 copy-start
  297.0 8.8 %shard_map.59 = bf16[2,1600,4096]{2,1,0:T(8,128)(2,1)} custom-call(bf16[2,1600,4096]{2,1,0:T(8,128)(2,1)S(1)} %get-tuple-element.9.x_ref), custom_call_target="tpu_custom_call" | custom-call | tf_op jit(solution)/shard_map/pallas_call | solution.py:251
  305.9 0.0 copy-done.1
  305.9 0.1 reshape.20
  306.0 0.1 dynamic-slice_reduce_fusion
  306.1 0.7 reshape.21
  306.8 0.0 copy-done
  306.8 0.1 copy.6
  306.8 0.7 copy.7
Async XLA Ops:
  297.0 8.9 %copy-start.1 = (f32[20,640]{1,0:T(8,128)S(1)}, f32[20,640]{1,0:T(8,128)}, u32[]{:S(2)}) copy-start(f32[20,640]{1,0:T(8,128)} %get-tuple-element.13) | copy-start | bytes 153604
  297.0 9.7 %copy-start = (bf16[8,4,2,1024]{3,2,1,0:T(2,128)(2,1)S(1)}, bf16[8,4,2,1024]{3,2,1,0:T(2,128)(2,1)}, u32[]{:S(2)}) copy-start(bf16[8,4,2,1024]{3,2,1,0:T(2,128)(2,1)} %get-tuple-element.14) | copy-start | bytes 393220

commit v2 on v0

v2 whole, which is shorter than its diff:
```python
import functools

import jax
import jax.numpy as jnp
from jax import lax
from jax.experimental import pallas as pl
from jax.experimental.pallas import tpu as pltpu
from jax.sharding import PartitionSpec as P


LANES = 128
MIB = 1024 * 1024
ANY = pl.BlockSpec(memory_space=pl.ANY)
VMEM = pl.BlockSpec(memory_space=pltpu.VMEM)
STAGES = ((1, 3, 5), (9, 14), (22, 30, 38, 45, 49, 50))


def block_rows(quota, count):
    fits = [r for r in (32, 16, 8) if quota % r == 0 and (count * r) % LANES == 0]
    return fits[0] if fits else quota


def partner(me, d, n):
    return me ^ d if n & (n - 1) == 0 else lax.rem(me + d, n)


def source(me, d, n):
    return me ^ d if n & (n - 1) == 0 else lax.rem(me + n - d, n)


def pairs(d, n):
    return [(i, i ^ d if n & (n - 1) == 0 else (i + d) % n) for i in range(n)]


def add_block(x, acc, rows):
    experts, n, _, width = x.shape
    for e in range(experts):
        for j in range(n):
            part = jnp.abs(x[e, j, :, :LANES])
            for g in range(1, width // LANES):
                part = part + jnp.abs(x[e, j, :, g * LANES:(g + 1) * LANES])
            at = (e * n + j) * rows
            acc[at:at + rows, :] = part
    return jnp.sum(acc[...].T, axis=0, keepdims=True)


def scale_block(x, total, acc, put, me, n, rows):
    experts, _, _, width = x.shape
    acc[...] = jnp.broadcast_to(1.0 / total, (LANES, acc.shape[0])).T
    for d in range(n):
        j = partner(me, d, n)
        for e in range(experts):
            inverse = acc[pl.ds(pl.multiple_of((e * n + j) * rows, rows), rows), :]
            for g in range(width // LANES):
                cut = slice(g * LANES, (g + 1) * LANES)
                put(d, e, cut, (x[e, j, :, cut] * inverse).astype(jnp.bfloat16))


def head(n, rows, x_ref, weight_ref, gain_ref, *refs):
    sent, (own_ref, mine, peers, scale_ref, strip) = refs[:n - 1], refs[n - 1:n + 4]
    (xbuf, acc, weight, gain, load_sem, small_sem, sum_send, sum_recv, strip_send, strip_recv) = refs[n + 4:]
    me = lax.axis_index("rows")
    blocks, width = xbuf.shape[0], xbuf.shape[-1]

    def load(b):
        return pltpu.make_async_copy(x_ref.at[:, :, pl.ds(b * rows, rows)], xbuf.at[b], load_sem.at[b])

    for b in range(blocks):
        load(b).start()
    smalls = [pltpu.make_async_copy(weight_ref, weight, small_sem.at[0]),
              pltpu.make_async_copy(gain_ref, gain, small_sem.at[1])]
    for copy in smalls:
        copy.start()
    barrier = pltpu.get_barrier_semaphore()
    for d in range(1, n):
        pl.semaphore_signal(barrier, inc=1, device_id={"rows": partner(me, d, n)},
                            device_id_type=pl.DeviceIdType.MESH)

    def remote(src, dst, send, recv, d):
        return pltpu.make_async_remote_copy(
            src_ref=src, dst_ref=dst, send_sem=send, recv_sem=recv,
            device_id={"rows": partner(me, d, n)}, device_id_type=pl.DeviceIdType.MESH)

    def sums(turn, lo, hi):
        return [
            remote(mine.at[pl.ds(lo, hi - lo)], peers.at[d - 1, pl.ds(lo, hi - lo)],
                   sum_send.at[turn, d - 1], sum_recv.at[turn, d - 1], d)
            for d in range(1, n)
        ]

    load(0).wait()
    mine[0] = add_block(xbuf.at[0], acc, rows)
    pl.semaphore_wait(barrier, n - 1)
    turns = [sums(0, 0, 1)] + ([sums(1, 1, blocks)] if blocks > 1 else [])
    for copy in turns[0]:
        copy.start()
    for copy in smalls:
        copy.wait()
    strip[me] = (weight[...] * gain[...]).astype(jnp.bfloat16)
    strips = [remote(strip.at[me], strip.at[me], strip_send.at[d - 1], strip_recv.at[d - 1], d)
              for d in range(1, n)]
    for copy in strips:
        copy.start()
    for b in range(1, blocks):
        load(b).wait()
        mine[b] = add_block(xbuf.at[b], acc, rows)
    for turn in turns[1:]:
        for copy in turn:
            copy.start()
    for copy in turns[0]:
        copy.wait()
    total = mine[0]
    for d in range(1, n):
        total = total + peers[d - 1, 0]
    scale = total / (n * width)
    scale_ref[0] = scale

    def put(d, e, cut, value):
        ref = sent[d - 1] if d else own_ref
        ref[e, :, cut] = value

    scale_block(xbuf.at[0], scale, acc, put, me, n, rows)
    for copy in strips:
        copy.wait()
    for turn in turns[1:]:
        for copy in turn:
            copy.wait()


def add_up(rows, *refs):
    mine_ref, acc = refs[-2:]
    for k in range(mine_ref.shape[0]):
        mine_ref[k] = add_block(refs[k], acc.at[k], rows)


def narrow(n, rows, held, x_ref, mine_ref, *refs):
    peers = refs[:n - 1]
    sent = refs[n - 1 + held:2 * n - 2 + held]
    out_ref, scale_ref, acc = refs[2 * n - 2 + held:]
    me = lax.axis_index("rows")
    total = mine_ref[0]
    for peer in peers:
        total = total + peer[0]
    scale = total / (n * x_ref.shape[-1])
    scale_ref[0] = scale

    def put(d, e, cut, value):
        ref = sent[d - 1] if d else out_ref
        ref[e, :, cut] = value

    scale_block(x_ref, scale, acc, put, me, n, rows)


def place(n, spots, *refs):
    count = len(spots)
    got, out_ref, bufs = refs[:count], refs[-3 - count], refs[-2 - count:-2]
    load_sem, store_sem = refs[-2:]
    me = lax.axis_index("rows")
    loads = [pltpu.make_async_copy(got[k], bufs[k], load_sem.at[k]) for k in range(count)]
    for copy in loads:
        copy.start()
    stores = []
    for k, (lo, d) in enumerate(spots):
        _, height, width = got[k].shape
        column = source(me, d, n) if d else me
        loads[k].wait()
        stores.append(pltpu.make_async_copy(
            bufs[k],
            out_ref.at[:, pl.ds(lo, height), pl.ds(pl.multiple_of(column * width, width), width)],
            store_sem.at[k]))
        stores[-1].start()
    for copy in stores:
        copy.wait()


def gather(owners, strip_ref, router_ref, send_sem, recv_sem):
    home = lax.axis_index("owner")
    barrier = pltpu.get_barrier_semaphore()
    for d in range(1, owners):
        pl.semaphore_signal(barrier, inc=1, device_id={"owner": lax.rem(home + d, owners)},
                            device_id_type=pl.DeviceIdType.MESH)
    pl.semaphore_wait(barrier, owners - 1)
    copies = [
        pltpu.make_async_remote_copy(
            src_ref=strip_ref, dst_ref=router_ref.at[home], send_sem=send_sem.at[d - 1],
            recv_sem=recv_sem.at[d - 1], device_id={"owner": lax.rem(home + d, owners)},
            device_id_type=pl.DeviceIdType.MESH)
        for d in range(1, owners)
    ]
    for copy in copies:
        copy.start()
    router_ref[home] = strip_ref[...]
    for copy in copies:
        copy.wait()


def cut(blocks):
    stages, done = [], 0
    for stage in STAGES:
        ends = sorted({-(-blocks * e // STAGES[-1][-1]) for e in stage} - set(range(done + 1)))
        if ends:
            stages.append([(lo, hi) for lo, hi in zip([done] + ends[:-1], ends)])
            done = ends[-1]
    return stages


def per_device(n, owners, master_down, router_weight, router_gain):
    experts, height, width = master_down.shape
    quota = height // n
    rows = block_rows(quota, experts * n)
    blocks = quota // rows
    wide = experts * n * rows
    bf16, f32 = jnp.bfloat16, jnp.float32
    x = master_down.reshape(experts, n, quota, width)
    depth, mine_e = router_weight.shape
    stages = cut(blocks)
    known = stages[0][-1][1]
    hbm = pl.BlockSpec(memory_space=pltpu.HBM)

    outs = pl.pallas_call(
        functools.partial(head, n, rows),
        out_shape=[pltpu.VMEM((experts, rows, width), bf16)] * n + [
            jax.ShapeDtypeStruct((known, 1, wide), f32),
            jax.ShapeDtypeStruct((n - 1, known, 1, wide), f32),
            jax.ShapeDtypeStruct((1, 1, wide), f32),
            jax.ShapeDtypeStruct((n, mine_e, depth), bf16),
        ],
        in_specs=[hbm, hbm, hbm],
        out_specs=[VMEM] * (n + 4),
        scratch_shapes=[
            pltpu.VMEM((known, experts, n, rows, width), f32),
            pltpu.VMEM((wide, LANES), f32),
            pltpu.VMEM((mine_e, depth), f32),
            pltpu.VMEM((1, depth), f32),
            pltpu.SemaphoreType.DMA((known,)),
            pltpu.SemaphoreType.DMA((2,)),
            pltpu.SemaphoreType.DMA((2, n - 1)),
            pltpu.SemaphoreType.DMA((2, n - 1)),
            pltpu.SemaphoreType.DMA((n - 1,)),
            pltpu.SemaphoreType.DMA((n - 1,)),
        ],
        compiler_params=pltpu.CompilerParams(
            collective_id=0, has_side_effects=True, vmem_limit_bytes=24 * MIB),
        name="head",
    )(x, router_weight.T, router_gain[None, :])
    own, mine, peers, scale0, strip = outs[n - 1:]
    peers = [peers[d] for d in range(n - 1)]
    scales = [scale0]

    def permute(arrays):
        got = []
        for d in range(1, n):
            got.append(lax.ppermute(arrays[d - 1], "rows", pairs(d, n)))
        return got

    def sums(lo, hi, after):
        step = max(k for k in (4, 3, 2, 1) if (hi - lo) % k == 0)
        return pl.pallas_call(
            functools.partial(add_up, rows),
            grid=((hi - lo) // step,),
            out_shape=jax.ShapeDtypeStruct((hi - lo, 1, wide), f32),
            in_specs=[
                pl.BlockSpec((experts, n, rows, width), lambda b, k=k: (0, 0, lo + b * step + k, 0))
                for k in range(step)
            ] + [ANY],
            out_specs=pl.BlockSpec((step, 1, wide), lambda b: (b, 0, 0)),
            scratch_shapes=[pltpu.VMEM((step, wide, LANES), f32)],
            compiler_params=pltpu.CompilerParams(vmem_limit_bytes=24 * MIB),
        )(*[x] * step, after)

    def scaled(lo, hi, base, mine, peers, out):
        part = pl.BlockSpec((1, 1, wide), lambda b: (lo - base + b, 0, 0))
        held = [] if out is None else [out]
        made = pl.pallas_call(
            functools.partial(narrow, n, rows, len(held)),
            grid=(hi - lo,),
            out_shape=[pltpu.HBM((experts, (hi - lo) * rows, width), bf16)] * (n - 1) + [
                jax.ShapeDtypeStruct((experts, quota, n * width), bf16),
                jax.ShapeDtypeStruct((hi - lo, 1, wide), f32),
            ],
            in_specs=[pl.BlockSpec((experts, n, rows, width), lambda b: (0, 0, lo + b, 0))]
            + [part] * n + [ANY] * len(held),
            out_specs=[pl.BlockSpec((experts, rows, width), lambda b: (0, b, 0))] * (n - 1) + [
                pl.BlockSpec((experts, rows, width), lambda b: (0, lo + b, lax.axis_index("rows"))),
                pl.BlockSpec((1, 1, wide), lambda b: (b, 0, 0)),
            ],
            scratch_shapes=[pltpu.VMEM((wide, LANES), f32)],
            input_output_aliases={n + 1: n - 1} if held else {},
            compiler_params=pltpu.CompilerParams(vmem_limit_bytes=16 * MIB),
        )(x, mine, *peers, *held)
        return made[:n - 1], made[n - 1], made[n]

    def placed(spots, got, out):
        count = len(got)
        return pl.pallas_call(
            functools.partial(place, n, spots),
            out_shape=jax.ShapeDtypeStruct((experts, quota, n * width), bf16),
            in_specs=[ANY] * (count + 1),
            out_specs=ANY,
            scratch_shapes=[pltpu.VMEM(a.shape, bf16) for a in got] + [
                pltpu.SemaphoreType.DMA((count,)),
                pltpu.SemaphoreType.DMA((count,)),
            ],
            input_output_aliases={count: 0},
            compiler_params=pltpu.CompilerParams(vmem_limit_bytes=24 * MIB),
        )(*got, out)

    out, got, p, base = None, [], 0, 0
    sent = list(outs[:n - 1])
    for s, stage in enumerate(stages):
        for k, (lo, hi) in enumerate(stage):
            if p:
                sent, out, part = scaled(lo, hi, base, mine, peers, out)
                scales.append(part)
            if k + 1 == len(stage) and s + 1 < len(stages):
                base, end = hi, stages[s + 1][-1][1]
                mine = sums(base, end, scales[-1])
                peers = permute([mine] * (n - 1))
            got.append(permute(sent))
            p += 1

    strips = pl.pallas_call(
        functools.partial(gather, owners),
        out_shape=jax.ShapeDtypeStruct((owners, n, mine_e, depth), bf16),
        in_specs=[VMEM],
        out_specs=VMEM,
        scratch_shapes=[pltpu.SemaphoreType.DMA((owners - 1,)), pltpu.SemaphoreType.DMA((owners - 1,))],
        compiler_params=pltpu.CompilerParams(
            collective_id=1, has_side_effects=True, vmem_limit_bytes=4 * MIB),
        name="router",
    )(strip)
    serve_router = strips.transpose(0, 2, 1, 3).reshape(owners * mine_e, n * depth).T
    held = jnp.concatenate(scales, axis=0).reshape(blocks, experts, n, rows)
    scale_down = lax.dynamic_index_in_dim(held, lax.axis_index("rows"), axis=2, keepdims=False)
    scale_down = scale_down.transpose(1, 0, 2).reshape(experts, quota)

    for p, (lo, _) in enumerate(piece for stage in stages for piece in stage):
        spots, arrays = [(lo * rows, d) for d in range(1, n)], got[p]
        if p == 0:
            spots, arrays = spots + [(0, 0)], arrays + [own]
        out = placed(tuple(spots), arrays, out)
    return out, scale_down, serve_router


def solution(mesh):
    n, owners = mesh.shape["rows"], mesh.shape["owner"]

    def body(*args):
        return per_device(n, owners, *args)

    return jax.shard_map(
        body,
        mesh=mesh,
        in_specs=(P("owner", None, "rows"), P("rows", "owner"), P("rows")),
        out_specs=(P("owner", "rows", None), P("owner", "rows"), P()),
        check_vma=False,
    )
```

time: 321 us -> 361 us (1.12)
  Pallas kernels: 295 us -> 110 us
  waiting for transfers between devices: 0 us -> 177 us
  starting transfers between devices: 0 us -> 32.5 us
  local copies, waits for them, and re-layouts: 24.6 us -> 37.4 us
    pallas_call x1 -> x25, Pallas kernels: 295 us -> 110 us  [the longest x10 55.1 us: scaled(): pl.pallas_call(functools.partial(narrow, n, rows, len(held)), grid=(hi -...]
    ppermute x0 -> x39, waiting for transfers between devices: none -> 177 us  [permute(): got.append(lax.ppermute(arrays[d - 1], 'rows', pairs(d, n)))]
    ppermute x0 -> x39, starting transfers between devices: none -> 32.5 us  [permute(): got.append(lax.ppermute(arrays[d - 1], 'rows', pairs(d, n)))]
    unnamed x6 -> x157, local copies, waits for them, and re-layouts: 23.7 us -> 33.7 us
  transfers between devices with their start and end apart: 0 -> 39, of which waited for: 0 -> 18; matrix products, arithmetic and copies ran while one was open for 0% -> 4% of each run, Pallas kernels for 0% -> 28%
where the time goes in v2:
time: 361 us; the launch traced here: 358 us
  waiting for transfers between devices  177 us (49%)
  Pallas kernels  110 us (30%)
  local copies, waits for them, and re-layouts  37.4 us (10%)
  starting transfers between devices  32.5 us (9%)
    ppermute x39, waiting for transfers between devices, permute(): got.append(lax.ppermute(arrays[d - 1], 'rows', pairs(d, n)))  177 us
    pallas_call x10, Pallas kernels, scaled(): pl.pallas_call(functools.partial(narrow, n, rows, len(held)), grid=(hi -...  55.1 us
    unnamed x157, local copies, waits for them, and re-layouts  33.7 us
    ppermute x39, starting transfers between devices, permute(): got.append(lax.ppermute(arrays[d - 1], 'rows', pairs(d, n)))  32.5 us
    pallas_call x11, Pallas kernels, placed(): pl.pallas_call(functools.partial(place, n, spots), out_shape=jax.ShapeDty...  21.3 us
    pallas_call x2, Pallas kernels, sums(): pl.pallas_call(functools.partial(add_up, rows), grid=((hi - lo) // step,)...  18.7 us
    pallas_call x1, Pallas kernels, per_device(): pl.pallas_call(functools.partial(head, n, rows), out_shape=[pltpu.VMEM((e...  7.69 us
  transfers between devices with their start and end apart: 39, of which 18 were waited for; matrix products, arithmetic and copies ran while one was open for 4% of the time, Pallas kernels for 28%

profile of v2, /device:TPU:1, one launch (start us, length us, event | category | flops | bytes accessed | tf_op | source)
XLA Modules:
  0.0 357.7 jit_solution(4071623942951599681)
XLA Ops:
  2.0 7.7 %head.1 = (bf16[2,32,1024]{2,1,0:T(8,128)(2,1)}, bf16[2,32,1024]{2,1,0:T(8,128)(2,1)S(1)}, bf16[2,32,1024]{2,1,0:T(8,128)(2,1)S(1)}, bf16[2,32,1024]{2,1,0:T(8,1...) custom-call(f32[2,4,1600,1024]{3,2,1,0:T(8,128)} %bitcast.23, ...), custom_call_target="tpu_custom_call" | custom-call | tf_op jit(solution)/shard_map/head/pallas_call | solution.py:220
  10.2 2.5 shard_map.58
  12.8 2.6 shard_map.59
  15.9 4.5 %shard_map.60.mine_ref = f32[9,1,256]{2,1,0:T(1,128)S(1)} custom-call(f32[2,4,1600,1024]{3,2,1,0:T(8,128)} %bitcast.26, f32[2,4,1600,1024]{3,2,1,0:T(8,128)} %bitcast.27, f32[2,4,1600,1024]{3,2,1,0:T(8,128)} %bitcast.28, f32[2,1,256]{2,1,0:T(1,128)S(1)} %get-tuple-element.64.refs_3_), custom_call_target="tpu_custom_call" | custom-call | tf_op jit(solution)/shard_map/pallas_call | solution.py:258
  20.6 1.6 collective-permute-start.1
  22.3 1.1 collective-permute-start.2
  23.7 1.6 collective-permute-done.2.refs_2_
  25.4 4.5 %shard_map.61 = (bf16[2,128,1024]{2,1,0:T(8,128)(2,1)}, bf16[2,128,1024]{2,1,0:T(8,128)(2,1)}, bf16[2,128,1024]{2,1,0:T(8,128)(2,1)}, bf16[2,1600,4096]{2,1,0:T(8,128)(2,1)}, f32[4,1,256]{2,1,0:T(1,128)S(1)}) custom-call(f32[2,4,1600,1024]{3,2,1,0:T(8,128)} %bitcast.29, f32[9,1,256]{2,1,0:T(1,128)S(1)} %shard_map.60.mine_ref, ...), custom_call_target="tpu_custom_call", output_to_operand_aliasing={{3}: (5, {})} | custom-call | tf_op jit(solution)/shard_map/pallas_call | solution.py:274
  29.9 5.9 %shard_map.62 = (bf16[2,160,1024]{2,1,0:T(8,128)(2,1)}, bf16[2,160,1024]{2,1,0:T(8,128)(2,1)}, bf16[2,160,1024]{2,1,0:T(8,128)(2,1)}, bf16[2,1600,4096]{2,1,0:T(8,128)(2,1)}, f32[5,1,256]{2,1,0:T(1,128)S(1)}) custom-call(f32[2,4,1600,1024]{3,2,1,0:T(8,128)} %bitcast.30, f32[9,1,256]{2,1,0:T(1,128)S(1)} %shard_map.60.mine_ref, ...), custom_call_target="tpu_custom_call", output_to_operand_aliasing={{3}: (5, {})} | custom-call | tf_op jit(solution)/shard_map/pallas_call | solution.py:274
  35.8 14.2 %shard_map.63.mine_ref = f32[36,1,256]{2,1,0:T(1,128)S(1)} custom-call(f32[2,4,1600,1024]{3,2,1,0:T(8,128)} %bitcast.31, f32[2,4,1600,1024]{3,2,1,0:T(8,128)} %bitcast.32, f32[2,4,1600,1024]{3,2,1,0:T(8,128)} %bitcast.33, f32[2,4,1600,1024]{3,2,1,0:T(8,128)} %bitcast.34, f32[5,1,256]{2,1,0:T(1,128)S(1)} %get-tuple-element.67.refs_4_), custom_call_target="tpu_custom_call" | custom-call | tf_op jit(solution)/shard_map/pallas_call | solution.py:258
  51.8 1.0 collective-permute-start.5
  55.3 1.4 collective-permute-start.38
  58.2 3.3 collective-permute-start.33
  61.5 1.8 collective-permute-done.38.refs_2_
  63.9 1.0 collective-permute-start.34
  65.6 3.0 collective-permute-done.32.refs_2_
  69.3 8.2 %shard_map.64 = (bf16[2,256,1024]{2,1,0:T(8,128)(2,1)}, bf16[2,256,1024]{2,1,0:T(8,128)(2,1)}, bf16[2,256,1024]{2,1,0:T(8,128)(2,1)}, bf16[2,1600,4096]{2,1,0:T(8,128)(2,1)}, f32[8,1,256]{2,1,0:T(1,128)S(1)}) custom-call(f32[2,4,1600,1024]{3,2,1,0:T(8,128)} %bitcast.35, f32[36,1,256]{2,1,0:T(1,128)S(1)} %shard_map.63.mine_ref, ...), custom_call_target="tpu_custom_call", output_to_operand_aliasing={{3}: (5, {})} | custom-call | tf_op jit(solution)/shard_map/pallas_call | solution.py:274
  78.1 8.1 %shard_map.65 = (bf16[2,256,1024]{2,1,0:T(8,128)(2,1)}, bf16[2,256,1024]{2,1,0:T(8,128)(2,1)}, bf16[2,256,1024]{2,1,0:T(8,128)(2,1)}, bf16[2,1600,4096]{2,1,0:T(8,128)(2,1)}, f32[8,1,256]{2,1,0:T(1,128)S(1)}) custom-call(f32[2,4,1600,1024]{3,2,1,0:T(8,128)} %bitcast.36, f32[36,1,256]{2,1,0:T(1,128)S(1)} %shard_map.63.mine_ref, ...), custom_call_target="tpu_custom_call", output_to_operand_aliasing={{3}: (5, {})} | custom-call | tf_op jit(solution)/shard_map/pallas_call | solution.py:274
  86.8 8.1 %shard_map.66 = (bf16[2,256,1024]{2,1,0:T(8,128)(2,1)}, bf16[2,256,1024]{2,1,0:T(8,128)(2,1)}, bf16[2,256,1024]{2,1,0:T(8,128)(2,1)}, bf16[2,1600,4096]{2,1,0:T(8,128)(2,1)}, f32[8,1,256]{2,1,0:T(1,128)S(1)}) custom-call(f32[2,4,1600,1024]{3,2,1,0:T(8,128)} %bitcast.37, f32[36,1,256]{2,1,0:T(1,128)S(1)} %shard_map.63.mine_ref, ...), custom_call_target="tpu_custom_call", output_to_operand_aliasing={{3}: (5, {})} | custom-call | tf_op jit(solution)/shard_map/pallas_call | solution.py:274
  95.5 7.6 %shard_map.67 = (bf16[2,224,1024]{2,1,0:T(8,128)(2,1)}, bf16[2,224,1024]{2,1,0:T(8,128)(2,1)}, bf16[2,224,1024]{2,1,0:T(8,128)(2,1)}, bf16[2,1600,4096]{2,1,0:T(8,128)(2,1)}, f32[7,1,256]{2,1,0:T(1,128)S(1)}) custom-call(f32[2,4,1600,1024]{3,2,1,0:T(8,128)} %bitcast.38, f32[36,1,256]{2,1,0:T(1,128)S(1)} %shard_map.63.mine_ref, ...), custom_call_target="tpu_custom_call", output_to_operand_aliasing={{3}: (5, {})} | custom-call | tf_op jit(solution)/shard_map/pallas_call | solution.py:274
  103.8 5.4 %shard_map.68 = (bf16[2,128,1024]{2,1,0:T(8,128)(2,1)}, bf16[2,128,1024]{2,1,0:T(8,128)(2,1)}, bf16[2,128,1024]{2,1,0:T(8,128)(2,1)}, bf16[2,1600,4096]{2,1,0:T(8,128)(2,1)}, f32[4,1,256]{2,1,0:T(1,128)S(1)}) custom-call(f32[2,4,1600,1024]{3,2,1,0:T(8,128)} %bitcast.39, f32[36,1,256]{2,1,0:T(1,128)S(1)} %shard_map.63.mine_ref, ...), custom_call_target="tpu_custom_call", output_to_operand_aliasing={{3}: (5, {})} | custom-call | tf_op jit(solution)/shard_map/pallas_call | solution.py:274
  109.8 1.7 collective-permute-start.35
  112.2 5.8 %collective-permute-done.35.refs_2_ = bf16[2,64,1024]{2,1,0:T(8,128)(2,1)S(1)} collective-permute-done((bf16[2,64,1024]{2,1,0:T(8,128)(2,1)S(1)}, bf16[2,64,1024]{2,1,0:T(8,128)(2,1)S(1)}, u32[]{:S(2)}, u32[]{:S(2)}) %collective-permute-start.35) | collective-permute-done | bytes 262176 | tf_op jit(solution)/shard_map/ppermute | solution.py:253
  118.7 1.1 collective-permute-start.24
  121.4 1.0 collective-permute-start.13
  124.5 2.0 collective-permute-start.26
  127.3 29.6 %collective-permute-done.25.refs_1_ = bf16[2,160,1024]{2,1,0:T(8,128)(2,1)S(1)} collective-permute-done((bf16[2,160,1024]{2,1,0:T(8,128)(2,1)S(1)}, bf16[2,160,1024]{2,1,0:T(8,128)(2,1)S(1)}, u32[]{:S(2)}, u32[]{:S(2)}) %collective-permute-start.25) | collective-permute-done | bytes 655392 | tf_op jit(solution)/shard_map/ppermute | solution.py:253
  157.7 3.2 collective-permute-start.14
  160.9 11.9 %collective-permute-done.26.refs_2_ = bf16[2,160,1024]{2,1,0:T(8,128)(2,1)S(1)} collective-permute-done((bf16[2,160,1024]{2,1,0:T(8,128)(2,1)S(1)}, bf16[2,160,1024]{2,1,0:T(8,128)(2,1)S(1)}, u32[]{:S(2)}, u32[]{:S(2)}) %collective-permute-start.26) | collective-permute-done | bytes 655392 | tf_op jit(solution)/shard_map/ppermute | solution.py:253
  173.7 1.0 collective-permute-start.16
  174.7 0.9 copy-done.2
  175.7 0.9 copy-done.4
  177.4 14.8 %collective-permute-done.14.refs_2_ = bf16[2,224,1024]{2,1,0:T(8,128)(2,1)S(1)} collective-permute-done((bf16[2,224,1024]{2,1,0:T(8,128)(2,1)S(1)}, bf16[2,224,1024]{2,1,0:T(8,128)(2,1)S(1)}, u32[]{:S(2)}, u32[]{:S(2)}) %collective-permute-start.14) | collective-permute-done | bytes 917536 | tf_op jit(solution)/shard_map/ppermute | solution.py:253
  192.2 0.9 copy-done.6
  193.1 1.0 collective-permute-start.19
  194.3 18.8 %collective-permute-done.16.refs_1_ = bf16[2,256,1024]{2,1,0:T(8,128)(2,1)S(1)} collective-permute-done((bf16[2,256,1024]{2,1,0:T(8,128)(2,1)S(1)}, bf16[2,256,1024]{2,1,0:T(8,128)(2,1)S(1)}, u32[]{:S(2)}, u32[]{:S(2)}) %collective-permute-start.16) | collective-permute-done | bytes 1048608 | tf_op jit(solution)/shard_map/ppermute | solution.py:253
  213.0 2.3 collective-permute-start.21
  215.4 21.8 %collective-permute-done.17.refs_2_ = bf16[2,256,1024]{2,1,0:T(8,128)(2,1)S(1)} collective-permute-done((bf16[2,256,1024]{2,1,0:T(8,128)(2,1)S(1)}, bf16[2,256,1024]{2,1,0:T(8,128)(2,1)S(1)}, u32[]{:S(2)}, u32[]{:S(2)}) %collective-permute-start.17) | collective-permute-done | bytes 1048608 | tf_op jit(solution)/shard_map/ppermute | solution.py:253
  237.1 1.0 collective-permute-start.22
  238.2 1.0 copy-done
  240.5 6.8 %router.1 = bf16[8,4,2,1024]{3,2,1,0:T(2,128)(2,1)S(1)} custom-call(bf16[4,2,1024]{2,1,0:T(2,128)(2,1)S(1)} %copy-done.40), custom_call_target="tpu_custom_call" | custom-call | tf_op jit(solution)/shard_map/router/pallas_call | solution.py:322
  248.1 1.3 constant_dynamic-update-slice_fusion.9
  249.3 1.3 constant_dynamic-update-slice_fusion.8
  250.6 1.3 constant_dynamic-update-slice_fusion.7
  251.9 1.3 constant_dynamic-update-slice_fusion.6
  253.2 2.2 shard_map.69
  256.6 1.5 collective-permute-done.19.refs_1_
  258.1 1.0 collective-permute-start.10
  259.1 23.1 %collective-permute-done.20.refs_2_ = bf16[2,256,1024]{2,1,0:T(8,128)(2,1)} collective-permute-done((bf16[2,256,1024]{2,1,0:T(8,128)(2,1)}, bf16[2,256,1024]{2,1,0:T(8,128)(2,1)}, u32[]{:S(2)}, u32[]{:S(2)}) %collective-permute-start.20) | collective-permute-done | bytes 1048608 | tf_op jit(solution)/shard_map/ppermute | solution.py:253
  284.0 1.4 collective-permute-start.6
  285.4 17.6 %collective-permute-done.22.refs_1_ = bf16[2,256,1024]{2,1,0:T(8,128)(2,1)} collective-permute-done((bf16[2,256,1024]{2,1,0:T(8,128)(2,1)}, bf16[2,256,1024]{2,1,0:T(8,128)(2,1)}, u32[]{:S(2)}, u32[]{:S(2)}) %collective-permute-start.22) | collective-permute-done | bytes 1048608 | tf_op jit(solution)/shard_map/ppermute | solution.py:253
  303.0 1.0 collective-permute-start.7
  304.0 23.1 %collective-permute-done.23.refs_2_ = bf16[2,256,1024]{2,1,0:T(8,128)(2,1)} collective-permute-done((bf16[2,256,1024]{2,1,0:T(8,128)(2,1)}, bf16[2,256,1024]{2,1,0:T(8,128)(2,1)}, u32[]{:S(2)}, u32[]{:S(2)}) %collective-permute-start.23) | collective-permute-done | bytes 1048608 | tf_op jit(solution)/shard_map/ppermute | solution.py:253
  333.5 1.8 shard_map.70.refs_3_
  335.4 1.0 shard_map.71.refs_3_
  336.7 1.0 shard_map.72.refs_3_
  338.4 1.3 shard_map.73.refs_3_
  340.4 1.9 shard_map.74.refs_3_
  342.4 3.0 shard_map.75.refs_3_
  345.4 3.0 shard_map.76.refs_3_
  348.5 1.9 shard_map.77.refs_3_
  351.3 2.2 shard_map.78.refs_3_
  353.6 2.3 shard_map.79.refs_3_
  356.0 1.7 shard_map.80
  (203 shorter events, 36.5 us)
Async XLA Ops:
  9.7 3.0 copy-start.32
  9.7 46.9 %collective-permute-start.36 = (bf16[2,32,1024]{2,1,0:T(8,128)(2,1)}, bf16[2,32,1024]{2,1,0:T(8,128)(2,1)}, u32[]{:S(2)}, u32[]{:S(2)}) collective-permute-start(bf16[2,32,1024]{2,1,0:T(8,128)(2,1)} %get-tuple-element.104), channel_id=1, source_target_pairs={{0,1},{1,0},{2,3},{3,2},{4,5},{5,4},{6,7},{7,6},{8,9},{9,8},{10,11... | collective-permute-start | bytes 393224 | tf_op jit(solution)/shard_map/ppermute | solution.py:253
  15.3 49.6 %collective-permute-start.30 = (bf16[2,64,1024]{2,1,0:T(8,128)(2,1)}, bf16[2,64,1024]{2,1,0:T(8,128)(2,1)S(1)}, u32[]{:S(2)}, u32[]{:S(2)}) collective-permute-start(bf16[2,64,1024]{2,1,0:T(8,128)(2,1)} %get-tuple-element.98), channel_id=1, source_target_pairs={{0,1},{1,0},{2,3},{3,2},{4,5},{5,4},{6,7},{7,6},{8,9},{9,8},{10,11... | collective-permute-start | bytes 786440 | tf_op jit(solution)/shard_map/ppermute | solution.py:253
  15.5 49.5 %collective-permute-start.31 = (bf16[2,64,1024]{2,1,0:T(8,128)(2,1)}, bf16[2,64,1024]{2,1,0:T(8,128)(2,1)S(1)}, u32[]{:S(2)}, u32[]{:S(2)}) collective-permute-start(bf16[2,64,1024]{2,1,0:T(8,128)(2,1)} %get-tuple-element.99), channel_id=1, source_target_pairs={{0,2},{1,3},{2,0},{3,1},{4,6},{5,7},{6,4},{7,5},{8,10},{9,11},{10,... | collective-permute-start | bytes 786440 | tf_op jit(solution)/shard_map/ppermute | solution.py:253
  20.4 1.8 collective-permute-start
  20.6 3.1 collective-permute-start.1
  22.3 3.1 collective-permute-start.2
  29.9 5.9 %copy-start.52 = (f32[4,1,256]{2,1,0:T(1,128)}, f32[4,1,256]{2,1,0:T(1,128)S(1)}, u32[]{:S(2)}) copy-start(f32[4,1,256]{2,1,0:T(1,128)S(1)} %get-tuple-element.111) | copy-start | bytes 12292
  35.8 20.9 %copy-start.72 = (bf16[2,64,1024]{2,1,0:T(8,128)(2,1)S(1)}, bf16[2,64,1024]{2,1,0:T(8,128)(2,1)}, u32[]{:S(2)}) copy-start(bf16[2,64,1024]{2,1,0:T(8,128)(2,1)} %get-tuple-element.100) | copy-start | bytes 786436
  35.8 22.4 %copy-start.71 = (bf16[2,64,1024]{2,1,0:T(8,128)(2,1)S(1)}, bf16[2,64,1024]{2,1,0:T(8,128)(2,1)}, u32[]{:S(2)}) copy-start(bf16[2,64,1024]{2,1,0:T(8,128)(2,1)} %get-tuple-element.101) | copy-start | bytes 786436
  35.8 28.2 %copy-start.70 = (bf16[2,64,1024]{2,1,0:T(8,128)(2,1)S(1)}, bf16[2,64,1024]{2,1,0:T(8,128)(2,1)}, u32[]{:S(2)}) copy-start(bf16[2,64,1024]{2,1,0:T(8,128)(2,1)} %get-tuple-element.102) | copy-start | bytes 786436
  35.8 29.2 %copy-start.68 = (bf16[2,128,1024]{2,1,0:T(8,128)(2,1)S(1)}, bf16[2,128,1024]{2,1,0:T(8,128)(2,1)}, u32[]{:S(2)}) copy-start(bf16[2,128,1024]{2,1,0:T(8,128)(2,1)} %get-tuple-element.95) | copy-start | bytes 1572868
  35.8 29.3 %copy-start.67 = (bf16[2,128,1024]{2,1,0:T(8,128)(2,1)S(1)}, bf16[2,128,1024]{2,1,0:T(8,128)(2,1)}, u32[]{:S(2)}) copy-start(bf16[2,128,1024]{2,1,0:T(8,128)(2,1)} %get-tuple-element.96) | copy-start | bytes 1572868
  35.8 33.5 %copy-start.66 = (bf16[2,128,1024]{2,1,0:T(8,128)(2,1)S(1)}, bf16[2,128,1024]{2,1,0:T(8,128)(2,1)}, u32[]{:S(2)}) copy-start(bf16[2,128,1024]{2,1,0:T(8,128)(2,1)} %get-tuple-element.97) | copy-start | bytes 1572868
  50.6 1.2 collective-permute-start.3
  50.9 2.8 collective-permute-start.4
  51.8 3.5 collective-permute-start.5
  53.7 3.8 %collective-permute-start.37 = (bf16[2,32,1024]{2,1,0:T(8,128)(2,1)S(1)}, bf16[2,32,1024]{2,1,0:T(8,128)(2,1)S(1)}, u32[]{:S(2)}, u32[]{:S(2)}) collective-permute-start(bf16[2,32,1024]{2,1,0:T(8,128)(2,1)S(1)} %get-tuple-element.105), channel_id=1, source_target_pairs={{0,2},{1,3},{2,0},{3,1},{4,6},{5,7},{6,4},{7,5},{8,10},{9,11},{10,... | collective-permute-start | bytes 393224 | tf_op jit(solution)/shard_map/ppermute | solution.py:253
  55.3 8.0 %collective-permute-start.38 = (bf16[2,32,1024]{2,1,0:T(8,128)(2,1)S(1)}, bf16[2,32,1024]{2,1,0:T(8,128)(2,1)S(1)}, u32[]{:S(2)}, u32[]{:S(2)}) collective-permute-start(bf16[2,32,1024]{2,1,0:T(8,128)(2,1)S(1)} %get-tuple-element.106), channel_id=1, source_target_pairs={{0,3},{1,2},{2,1},{3,0},{4,7},{5,6},{6,5},{7,4},{8,11},{9,10},{10,... | collective-permute-start | bytes 393224 | tf_op jit(solution)/shard_map/ppermute | solution.py:253
  56.7 11.9 %collective-permute-start.32 = (bf16[2,64,1024]{2,1,0:T(8,128)(2,1)S(1)}, bf16[2,64,1024]{2,1,0:T(8,128)(2,1)S(1)}, u32[]{:S(2)}, u32[]{:S(2)}) collective-permute-start(bf16[2,64,1024]{2,1,0:T(8,128)(2,1)S(1)} %copy-done.72), channel_id=1, source_target_pairs={{0,3},{1,2},{2,1},{3,0},{4,7},{5,6},{6,5},{7,4},{8,11},{9,10},{10,... | collective-permute-start | bytes 786440 | tf_op jit(solution)/shard_map/ppermute | solution.py:253
  58.2 51.6 %collective-permute-start.33 = (bf16[2,64,1024]{2,1,0:T(8,128)(2,1)S(1)}, bf16[2,64,1024]{2,1,0:T(8,128)(2,1)S(1)}, u32[]{:S(2)}, u32[]{:S(2)}) collective-permute-start(bf16[2,64,1024]{2,1,0:T(8,128)(2,1)S(1)} %copy-done.71), channel_id=1, source_target_pairs={{0,1},{1,0},{2,3},{3,2},{4,5},{5,4},{6,7},{7,6},{8,9},{9,8},{10,11... | collective-permute-start | bytes 786440 | tf_op jit(solution)/shard_map/ppermute | solution.py:253
  63.9 47.6 %collective-permute-start.34 = (bf16[2,64,1024]{2,1,0:T(8,128)(2,1)S(1)}, bf16[2,64,1024]{2,1,0:T(8,128)(2,1)S(1)}, u32[]{:S(2)}, u32[]{:S(2)}) collective-permute-start(bf16[2,64,1024]{2,1,0:T(8,128)(2,1)S(1)} %copy-done.70), channel_id=1, source_target_pairs={{0,2},{1,3},{2,0},{3,1},{4,6},{5,7},{6,4},{7,5},{8,10},{9,11},{10,... | collective-permute-start | bytes 786440 | tf_op jit(solution)/shard_map/ppermute | solution.py:253
  65.0 12.5 %copy-start.22 = (bf16[2,64,1024]{2,1,0:T(8,128)(2,1)}, bf16[2,64,1024]{2,1,0:T(8,128)(2,1)S(1)}, u32[]{:S(2)}) copy-start(bf16[2,64,1024]{2,1,0:T(8,128)(2,1)S(1)} %collective-permute-done.30.refs_0_) | copy-start | bytes 786436
  65.0 54.8 %collective-permute-start.27 = (bf16[2,128,1024]{2,1,0:T(8,128)(2,1)S(1)}, bf16[2,128,1024]{2,1,0:T(8,128)(2,1)S(1)}, u32[]{:S(2)}, u32[]{:S(2)}) collective-permute-start(bf16[2,128,1024]{2,1,0:T(8,128)(2,1)S(1)} %copy-done.68), channel_id=1, source_target_pairs={{0,1},{1,0},{2,3},{3,2},{4,5},{5,4},{6,7},{7,6},{8,9},{9,8},{10,11... | collective-permute-start | bytes 1572872 | tf_op jit(solution)/shard_map/ppermute | solution.py:253
  65.0 12.4 %copy-start.24 = (bf16[2,64,1024]{2,1,0:T(8,128)(2,1)}, bf16[2,64,1024]{2,1,0:T(8,128)(2,1)S(1)}, u32[]{:S(2)}) copy-start(bf16[2,64,1024]{2,1,0:T(8,128)(2,1)S(1)} %collective-permute-done.31.refs_1_) | copy-start | bytes 786436
  65.1 55.5 %collective-permute-start.28 = (bf16[2,128,1024]{2,1,0:T(8,128)(2,1)S(1)}, bf16[2,128,1024]{2,1,0:T(8,128)(2,1)S(1)}, u32[]{:S(2)}, u32[]{:S(2)}) collective-permute-start(bf16[2,128,1024]{2,1,0:T(8,128)(2,1)S(1)} %copy-done.67), channel_id=1, source_target_pairs={{0,2},{1,3},{2,0},{3,1},{4,6},{5,7},{6,4},{7,5},{8,10},{9,11},{10,... | collective-permute-start | bytes 1572872 | tf_op jit(solution)/shard_map/ppermute | solution.py:253
  69.3 53.1 %collective-permute-start.29 = (bf16[2,128,1024]{2,1,0:T(8,128)(2,1)S(1)}, bf16[2,128,1024]{2,1,0:T(8,128)(2,1)S(1)}, u32[]{:S(2)}, u32[]{:S(2)}) collective-permute-start(bf16[2,128,1024]{2,1,0:T(8,128)(2,1)S(1)} %copy-done.66), channel_id=1, source_target_pairs={{0,3},{1,2},{2,1},{3,0},{4,7},{5,6},{6,5},{7,4},{8,11},{9,10},{10,... | collective-permute-start | bytes 1572872 | tf_op jit(solution)/shard_map/ppermute | solution.py:253
  103.7 6.1 %copy-start.69 = (bf16[2,64,1024]{2,1,0:T(8,128)(2,1)S(1)}, bf16[2,64,1024]{2,1,0:T(8,128)(2,1)}, u32[]{:S(2)}) copy-start(bf16[2,64,1024]{2,1,0:T(8,128)(2,1)} %get-tuple-element.103) | copy-start | bytes 786436
  103.7 15.0 %copy-start.65 = (bf16[2,160,1024]{2,1,0:T(8,128)(2,1)S(1)}, bf16[2,160,1024]{2,1,0:T(8,128)(2,1)}, u32[]{:S(2)}) copy-start(bf16[2,160,1024]{2,1,0:T(8,128)(2,1)} %get-tuple-element.92) | copy-start | bytes 1966084
  103.7 16.9 %copy-start.62 = (bf16[2,224,1024]{2,1,0:T(8,128)(2,1)S(1)}, bf16[2,224,1024]{2,1,0:T(8,128)(2,1)}, u32[]{:S(2)}) copy-start(bf16[2,224,1024]{2,1,0:T(8,128)(2,1)} %get-tuple-element.80) | copy-start | bytes 2752516
  103.7 17.7 %copy-start.61 = (bf16[2,224,1024]{2,1,0:T(8,128)(2,1)S(1)}, bf16[2,224,1024]{2,1,0:T(8,128)(2,1)}, u32[]{:S(2)}) copy-start(bf16[2,224,1024]{2,1,0:T(8,128)(2,1)} %get-tuple-element.81) | copy-start | bytes 2752516
  103.7 19.5 %copy-start.64 = (bf16[2,160,1024]{2,1,0:T(8,128)(2,1)S(1)}, bf16[2,160,1024]{2,1,0:T(8,128)(2,1)}, u32[]{:S(2)}) copy-start(bf16[2,160,1024]{2,1,0:T(8,128)(2,1)} %get-tuple-element.93) | copy-start | bytes 1966084
  103.7 20.8 %copy-start.63 = (bf16[2,160,1024]{2,1,0:T(8,128)(2,1)S(1)}, bf16[2,160,1024]{2,1,0:T(8,128)(2,1)}, u32[]{:S(2)}) copy-start(bf16[2,160,1024]{2,1,0:T(8,128)(2,1)} %get-tuple-element.94) | copy-start | bytes 1966084
  103.7 23.6 %copy-start.59 = (bf16[2,256,1024]{2,1,0:T(8,128)(2,1)S(1)}, bf16[2,256,1024]{2,1,0:T(8,128)(2,1)}, u32[]{:S(2)}) copy-start(bf16[2,256,1024]{2,1,0:T(8,128)(2,1)} %get-tuple-element.83) | copy-start | bytes 3145732
  103.7 54.0 %copy-start.60 = (bf16[2,224,1024]{2,1,0:T(8,128)(2,1)S(1)}, bf16[2,224,1024]{2,1,0:T(8,128)(2,1)}, u32[]{:S(2)}) copy-start(bf16[2,224,1024]{2,1,0:T(8,128)(2,1)} %get-tuple-element.82) | copy-start | bytes 2752516
  103.8 69.9 %copy-start.58 = (bf16[2,256,1024]{2,1,0:T(8,128)(2,1)S(1)}, bf16[2,256,1024]{2,1,0:T(8,128)(2,1)}, u32[]{:S(2)}) copy-start(bf16[2,256,1024]{2,1,0:T(8,128)(2,1)} %get-tuple-element.84) | copy-start | bytes 3145732
  103.8 71.9 %copy-start.57 = (bf16[2,256,1024]{2,1,0:T(8,128)(2,1)S(1)}, bf16[2,256,1024]{2,1,0:T(8,128)(2,1)}, u32[]{:S(2)}) copy-start(bf16[2,256,1024]{2,1,0:T(8,128)(2,1)} %get-tuple-element.85) | copy-start | bytes 3145732
  103.8 72.8 %copy-start.56 = (bf16[2,256,1024]{2,1,0:T(8,128)(2,1)S(1)}, bf16[2,256,1024]{2,1,0:T(8,128)(2,1)}, u32[]{:S(2)}) copy-start(bf16[2,256,1024]{2,1,0:T(8,128)(2,1)} %get-tuple-element.86) | copy-start | bytes 3145732
  109.8 8.2 %collective-permute-start.35 = (bf16[2,64,1024]{2,1,0:T(8,128)(2,1)S(1)}, bf16[2,64,1024]{2,1,0:T(8,128)(2,1)S(1)}, u32[]{:S(2)}, u32[]{:S(2)}) collective-permute-start(bf16[2,64,1024]{2,1,0:T(8,128)(2,1)S(1)} %copy-done.69), channel_id=1, source_target_pairs={{0,3},{1,2},{2,1},{3,0},{4,7},{5,6},{6,5},{7,4},{8,11},{9,10},{10,... | collective-permute-start | bytes 786440 | tf_op jit(solution)/shard_map/ppermute | solution.py:253
  112.2 11.5 %collective-permute-start.9 = (bf16[2,128,1024]{2,1,0:T(8,128)(2,1)}, bf16[2,128,1024]{2,1,0:T(8,128)(2,1)S(1)}, u32[]{:S(2)}, u32[]{:S(2)}) collective-permute-start(bf16[2,128,1024]{2,1,0:T(8,128)(2,1)} %get-tuple-element.77), channel_id=1, source_target_pairs={{0,1},{1,0},{2,3},{3,2},{4,5},{5,4},{6,7},{7,6},{8,9},{9,8},{10,11... | collective-permute-start | bytes 1572872 | tf_op jit(solution)/shard_map/ppermute | solution.py:253
  118.7 7.7 %collective-permute-start.24 = (bf16[2,160,1024]{2,1,0:T(8,128)(2,1)S(1)}, bf16[2,160,1024]{2,1,0:T(8,128)(2,1)S(1)}, u32[]{:S(2)}, u32[]{:S(2)}) collective-permute-start(bf16[2,160,1024]{2,1,0:T(8,128)(2,1)S(1)} %copy-done.65), channel_id=1, source_target_pairs={{0,1},{1,0},{2,3},{3,2},{4,5},{5,4},{6,7},{7,6},{8,9},{9,8},{10,11... | collective-permute-start | bytes 1966088 | tf_op jit(solution)/shard_map/ppermute | solution.py:253
  120.6 54.1 %collective-permute-start.12 = (bf16[2,224,1024]{2,1,0:T(8,128)(2,1)S(1)}, bf16[2,224,1024]{2,1,0:T(8,128)(2,1)S(1)}, u32[]{:S(2)}, u32[]{:S(2)}) collective-permute-start(bf16[2,224,1024]{2,1,0:T(8,128)(2,1)S(1)} %copy-done.62), channel_id=1, source_target_pairs={{0,1},{1,0},{2,3},{3,2},{4,5},{5,4},{6,7},{7,6},{8,9},{9,8},{10,11... | collective-permute-start | bytes 2752520 | tf_op jit(solution)/shard_map/ppermute | solution.py:253
  121.4 54.2 %collective-permute-start.13 = (bf16[2,224,1024]{2,1,0:T(8,128)(2,1)S(1)}, bf16[2,224,1024]{2,1,0:T(8,128)(2,1)S(1)}, u32[]{:S(2)}, u32[]{:S(2)}) collective-permute-start(bf16[2,224,1024]{2,1,0:T(8,128)(2,1)S(1)} %copy-done.61), channel_id=1, source_target_pairs={{0,2},{1,3},{2,0},{3,1},{4,6},{5,7},{6,4},{7,5},{8,10},{9,11},{10,... | collective-permute-start | bytes 2752520 | tf_op jit(solution)/shard_map/ppermute | solution.py:253
  123.2 33.6 %collective-permute-start.25 = (bf16[2,160,1024]{2,1,0:T(8,128)(2,1)S(1)}, bf16[2,160,1024]{2,1,0:T(8,128)(2,1)S(1)}, u32[]{:S(2)}, u32[]{:S(2)}) collective-permute-start(bf16[2,160,1024]{2,1,0:T(8,128)(2,1)S(1)} %copy-done.64), channel_id=1, source_target_pairs={{0,2},{1,3},{2,0},{3,1},{4,6},{5,7},{6,4},{7,5},{8,10},{9,11},{10,... | collective-permute-start | bytes 1966088 | tf_op jit(solution)/shard_map/ppermute | solution.py:253
  124.5 48.3 %collective-permute-start.26 = (bf16[2,160,1024]{2,1,0:T(8,128)(2,1)S(1)}, bf16[2,160,1024]{2,1,0:T(8,128)(2,1)S(1)}, u32[]{:S(2)}, u32[]{:S(2)}) collective-permute-start(bf16[2,160,1024]{2,1,0:T(8,128)(2,1)S(1)} %copy-done.63), channel_id=1, source_target_pairs={{0,3},{1,2},{2,1},{3,0},{4,7},{5,6},{6,5},{7,4},{8,11},{9,10},{10,... | collective-permute-start | bytes 1966088 | tf_op jit(solution)/shard_map/ppermute | solution.py:253
  127.3 66.9 %collective-permute-start.15 = (bf16[2,256,1024]{2,1,0:T(8,128)(2,1)S(1)}, bf16[2,256,1024]{2,1,0:T(8,128)(2,1)S(1)}, u32[]{:S(2)}, u32[]{:S(2)}) collective-permute-start(bf16[2,256,1024]{2,1,0:T(8,128)(2,1)S(1)} %copy-done.59), channel_id=1, source_target_pairs={{0,1},{1,0},{2,3},{3,2},{4,5},{5,4},{6,7},{7,6},{8,9},{9,8},{10,11... | collective-permute-start | bytes 3145736 | tf_op jit(solution)/shard_map/ppermute | solution.py:253
  157.7 34.5 %collective-permute-start.14 = (bf16[2,224,1024]{2,1,0:T(8,128)(2,1)S(1)}, bf16[2,224,1024]{2,1,0:T(8,128)(2,1)S(1)}, u32[]{:S(2)}, u32[]{:S(2)}) collective-permute-start(bf16[2,224,1024]{2,1,0:T(8,128)(2,1)S(1)} %copy-done.60), channel_id=1, source_target_pairs={{0,3},{1,2},{2,1},{3,0},{4,7},{5,6},{6,5},{7,4},{8,11},{9,10},{10,... | collective-permute-start | bytes 2752520 | tf_op jit(solution)/shard_map/ppermute | solution.py:253
  173.7 39.4 %collective-permute-start.16 = (bf16[2,256,1024]{2,1,0:T(8,128)(2,1)S(1)}, bf16[2,256,1024]{2,1,0:T(8,128)(2,1)S(1)}, u32[]{:S(2)}, u32[]{:S(2)}) collective-permute-start(bf16[2,256,1024]{2,1,0:T(8,128)(2,1)S(1)} %copy-done.58), channel_id=1, source_target_pairs={{0,2},{1,3},{2,0},{3,1},{4,6},{5,7},{6,4},{7,5},{8,10},{9,11},{10,... | collective-permute-start | bytes 3145736 | tf_op jit(solution)/shard_map/ppermute | solution.py:253
  175.6 61.5 %collective-permute-start.17 = (bf16[2,256,1024]{2,1,0:T(8,128)(2,1)S(1)}, bf16[2,256,1024]{2,1,0:T(8,128)(2,1)S(1)}, u32[]{:S(2)}, u32[]{:S(2)}) collective-permute-start(bf16[2,256,1024]{2,1,0:T(8,128)(2,1)S(1)} %copy-done.57), channel_id=1, source_target_pairs={{0,3},{1,2},{2,1},{3,0},{4,7},{5,6},{6,5},{7,4},{8,11},{9,10},{10,... | collective-permute-start | bytes 3145736 | tf_op jit(solution)/shard_map/ppermute | solution.py:253
  176.6 61.6 %collective-permute-start.18 = (bf16[2,256,1024]{2,1,0:T(8,128)(2,1)S(1)}, bf16[2,256,1024]{2,1,0:T(8,128)(2,1)S(1)}, u32[]{:S(2)}, u32[]{:S(2)}) collective-permute-start(bf16[2,256,1024]{2,1,0:T(8,128)(2,1)S(1)} %copy-done.56), channel_id=1, source_target_pairs={{0,1},{1,0},{2,3},{3,2},{4,5},{5,4},{6,7},{7,6},{8,9},{9,8},{10,11... | collective-permute-start | bytes 3145736 | tf_op jit(solution)/shard_map/ppermute | solution.py:253
  193.1 65.0 %collective-permute-start.19 = (bf16[2,256,1024]{2,1,0:T(8,128)(2,1)}, bf16[2,256,1024]{2,1,0:T(8,128)(2,1)}, u32[]{:S(2)}, u32[]{:S(2)}) collective-permute-start(bf16[2,256,1024]{2,1,0:T(8,128)(2,1)} %get-tuple-element.87), channel_id=1, source_target_pairs={{0,2},{1,3},{2,0},{3,1},{4,6},{5,7},{6,4},{7,5},{8,10},{9,11},{10,... | collective-permute-start | bytes 3145736 | tf_op jit(solution)/shard_map/ppermute | solution.py:253
  194.1 88.0 %collective-permute-start.20 = (bf16[2,256,1024]{2,1,0:T(8,128)(2,1)}, bf16[2,256,1024]{2,1,0:T(8,128)(2,1)}, u32[]{:S(2)}, u32[]{:S(2)}) collective-permute-start(bf16[2,256,1024]{2,1,0:T(8,128)(2,1)} %get-tuple-element.88), channel_id=1, source_target_pairs={{0,3},{1,2},{2,1},{3,0},{4,7},{5,6},{6,5},{7,4},{8,11},{9,10},{10,... | collective-permute-start | bytes 3145736 | tf_op jit(solution)/shard_map/ppermute | solution.py:253
  213.0 71.0 %collective-permute-start.21 = (bf16[2,256,1024]{2,1,0:T(8,128)(2,1)}, bf16[2,256,1024]{2,1,0:T(8,128)(2,1)}, u32[]{:S(2)}, u32[]{:S(2)}) collective-permute-start(bf16[2,256,1024]{2,1,0:T(8,128)(2,1)} %get-tuple-element.89), channel_id=1, source_target_pairs={{0,1},{1,0},{2,3},{3,2},{4,5},{5,4},{6,7},{7,6},{8,9},{9,8},{10,11... | collective-permute-start | bytes 3145736 | tf_op jit(solution)/shard_map/ppermute | solution.py:253
  237.1 65.9 %collective-permute-start.22 = (bf16[2,256,1024]{2,1,0:T(8,128)(2,1)}, bf16[2,256,1024]{2,1,0:T(8,128)(2,1)}, u32[]{:S(2)}, u32[]{:S(2)}) collective-permute-start(bf16[2,256,1024]{2,1,0:T(8,128)(2,1)} %get-tuple-element.90), channel_id=1, source_target_pairs={{0,2},{1,3},{2,0},{3,1},{4,6},{5,7},{6,4},{7,5},{8,10},{9,11},{10,... | collective-permute-start | bytes 3145736 | tf_op jit(solution)/shard_map/ppermute | solution.py:253
  239.1 88.0 %collective-permute-start.23 = (bf16[2,256,1024]{2,1,0:T(8,128)(2,1)}, bf16[2,256,1024]{2,1,0:T(8,128)(2,1)}, u32[]{:S(2)}, u32[]{:S(2)}) collective-permute-start(bf16[2,256,1024]{2,1,0:T(8,128)(2,1)} %get-tuple-element.91), channel_id=1, source_target_pairs={{0,3},{1,2},{2,1},{3,0},{4,7},{5,6},{6,5},{7,4},{8,11},{9,10},{10,... | collective-permute-start | bytes 3145736 | tf_op jit(solution)/shard_map/ppermute | solution.py:253
  253.2 29.0 %copy-start.44 = (f32[8,1,256]{2,1,0:T(1,128)S(1)}, f32[8,1,256]{2,1,0:T(1,128)}, u32[]{:S(2)}) copy-start(f32[8,1,256]{2,1,0:T(1,128)} %copy-done.43) | copy-start | bytes 24580
  253.2 29.6 %copy-start.50 = (f32[7,1,256]{2,1,0:T(1,128)S(1)}, f32[7,1,256]{2,1,0:T(1,128)}, u32[]{:S(2)}) copy-start(f32[7,1,256]{2,1,0:T(1,128)} %copy-done.49) | copy-start | bytes 21508
  253.2 30.2 %copy-start.54 = (f32[4,1,256]{2,1,0:T(1,128)S(1)}, f32[4,1,256]{2,1,0:T(1,128)}, u32[]{:S(2)}) copy-start(f32[4,1,256]{2,1,0:T(1,128)} %copy-done.53) | copy-start | bytes 12292
  258.1 95.5 %collective-permute-start.10 = (bf16[2,128,1024]{2,1,0:T(8,128)(2,1)}, bf16[2,128,1024]{2,1,0:T(8,128)(2,1)}, u32[]{:S(2)}, u32[]{:S(2)}) collective-permute-start(bf16[2,128,1024]{2,1,0:T(8,128)(2,1)} %get-tuple-element.78), channel_id=1, source_target_pairs={{0,2},{1,3},{2,0},{3,1},{4,6},{5,7},{6,4},{7,5},{8,10},{9,11},{10,... | collective-permute-start | bytes 1572872 | tf_op jit(solution)/shard_map/ppermute | solution.py:253
  282.2 71.4 %collective-permute-start.11 = (bf16[2,128,1024]{2,1,0:T(8,128)(2,1)}, bf16[2,128,1024]{2,1,0:T(8,128)(2,1)}, u32[]{:S(2)}, u32[]{:S(2)}) collective-permute-start(bf16[2,128,1024]{2,1,0:T(8,128)(2,1)} %get-tuple-element.79), channel_id=1, source_target_pairs={{0,3},{1,2},{2,1},{3,0},{4,7},{5,6},{6,5},{7,4},{8,11},{9,10},{10,... | collective-permute-start | bytes 1572872 | tf_op jit(solution)/shard_map/ppermute | solution.py:253
  284.0 71.9 %collective-permute-start.6 = (bf16[2,32,1024]{2,1,0:T(8,128)(2,1)}, bf16[2,32,1024]{2,1,0:T(8,128)(2,1)}, u32[]{:S(2)}, u32[]{:S(2)}) collective-permute-start(bf16[2,32,1024]{2,1,0:T(8,128)(2,1)} %get-tuple-element.74), channel_id=1, source_target_pairs={{0,1},{1,0},{2,3},{3,2},{4,5},{5,4},{6,7},{7,6},{8,9},{9,8},{10,11... | collective-permute-start | bytes 393224 | tf_op jit(solution)/shard_map/ppermute | solution.py:253
  303.0 52.9 %collective-permute-start.7 = (bf16[2,32,1024]{2,1,0:T(8,128)(2,1)}, bf16[2,32,1024]{2,1,0:T(8,128)(2,1)}, u32[]{:S(2)}, u32[]{:S(2)}) collective-permute-start(bf16[2,32,1024]{2,1,0:T(8,128)(2,1)} %get-tuple-element.75), channel_id=1, source_target_pairs={{0,2},{1,3},{2,0},{3,1},{4,6},{5,7},{6,4},{7,5},{8,10},{9,11},{10,... | collective-permute-start | bytes 393224 | tf_op jit(solution)/shard_map/ppermute | solution.py:253
  327.1 28.8 %collective-permute-start.8 = (bf16[2,32,1024]{2,1,0:T(8,128)(2,1)}, bf16[2,32,1024]{2,1,0:T(8,128)(2,1)}, u32[]{:S(2)}, u32[]{:S(2)}) collective-permute-start(bf16[2,32,1024]{2,1,0:T(8,128)(2,1)} %get-tuple-element.76), channel_id=1, source_target_pairs={{0,3},{1,2},{2,1},{3,0},{4,7},{5,6},{6,5},{7,4},{8,11},{9,10},{10,... | collective-permute-start | bytes 393224 | tf_op jit(solution)/shard_map/ppermute | solution.py:253
  342.4 3.0 copy-start.1
  (48 other events, 58.5 us)

commit v3 on v2

--- a/solution.py
+++ b/solution.py
@@ -12,7 +12,7 @@
 MIB = 1024 * 1024
 ANY = pl.BlockSpec(memory_space=pl.ANY)
 VMEM = pl.BlockSpec(memory_space=pltpu.VMEM)
-STAGES = ((1, 3, 5), (9, 14), (22, 30, 38, 45, 49, 50))
+STAGES = ((1, 3, 5), (10, 15), (24, 34, 44, 49, 50))
 
 
 def block_rows(quota, count):
@@ -57,8 +57,9 @@
 
 
 def head(n, rows, x_ref, weight_ref, gain_ref, *refs):
-    sent, (own_ref, mine, peers, scale_ref, strip) = refs[:n - 1], refs[n - 1:n + 4]
-    (xbuf, acc, weight, gain, load_sem, small_sem, sum_send, sum_recv, strip_send, strip_recv) = refs[n + 4:]
+    sent, (own_ref, scale_ref, strip) = refs[:n - 1], refs[n - 1:n + 2]
+    (xbuf, acc, mine, peers, weight, gain, load_sem, small_sem, sum_send, sum_recv, strip_send,
+     strip_recv) = refs[n + 2:]
     me = lax.axis_index("rows")
     blocks, width = xbuf.shape[0], xbuf.shape[-1]
 
@@ -109,22 +110,27 @@
             copy.start()
     for copy in turns[0]:
         copy.wait()
-    total = mine[0]
-    for d in range(1, n):
-        total = total + peers[d - 1, 0]
-    scale = total / (n * width)
-    scale_ref[0] = scale
+
+    def average(b):
+        total = mine[b]
+        for d in range(1, n):
+            total = total + peers[d - 1, b]
+        scale_ref[b] = total / (n * width)
+
+    average(0)
 
     def put(d, e, cut, value):
         ref = sent[d - 1] if d else own_ref
         ref[e, :, cut] = value
 
-    scale_block(xbuf.at[0], scale, acc, put, me, n, rows)
-    for copy in strips:
-        copy.wait()
+    scale_block(xbuf.at[0], scale_ref[0], acc, put, me, n, rows)
     for turn in turns[1:]:
         for copy in turn:
             copy.wait()
+    for b in range(1, blocks):
+        average(b)
+    for copy in strips:
+        copy.wait()
 
 
 def add_up(rows, *refs):
@@ -133,15 +139,69 @@
         mine_ref[k] = add_block(refs[k], acc.at[k], rows)
 
 
-def narrow(n, rows, held, x_ref, mine_ref, *refs):
-    peers = refs[:n - 1]
-    sent = refs[n - 1 + held:2 * n - 2 + held]
-    out_ref, scale_ref, acc = refs[2 * n - 2 + held:]
+def signal_pair(me):
+    pl.semaphore_signal(pltpu.get_barrier_semaphore(), inc=1, device_id={"rows": me ^ 1},
+                        device_id_type=pl.DeviceIdType.MESH)
+
+
+def swap_pair(me, src, dst, send_sem, recv_sem):
+    pl.semaphore_wait(pltpu.get_barrier_semaphore(), 1)
+    copy = pltpu.make_async_remote_copy(
+        src_ref=src, dst_ref=dst, send_sem=send_sem, recv_sem=recv_sem,
+        device_id={"rows": me ^ 1}, device_id_type=pl.DeviceIdType.MESH)
+    copy.start()
+    copy.wait()
+
+
+def add_up_pair(rows, step, *refs):
+    half_ref, acc, mine, theirs, send_sem, recv_sem = refs[-6:]
+    me, at = lax.axis_index("rows"), pl.program_id(0)
+
+    @pl.when(at == 0)
+    def _():
+        signal_pair(me)
+
+    for k in range(step):
+        mine[at * step + k] = add_block(refs[k], acc.at[k], rows)
+
+    @pl.when(at == pl.num_programs(0) - 1)
+    def _():
+        swap_pair(me, mine, theirs, send_sem, recv_sem)
+        part = half_ref.shape[-1]
+        for core in range(2):
+            @pl.when(lax.rem(me, 2) == core)
+            def _():
+                cut = slice(core * part, (core + 1) * part)
+                half_ref[...] = mine[:, :, cut] + theirs[:, :, cut]
+
+
+def finish_pair(count, half_ref, *refs):
+    scale_ref, mine, theirs, send_sem, recv_sem = refs[-5:]
     me = lax.axis_index("rows")
-    total = mine_ref[0]
-    for peer in peers:
-        total = total + peer[0]
-    scale = total / (n * x_ref.shape[-1])
+    signal_pair(me)
+    total = half_ref[...]
+    for part in refs[:-5]:
+        total = total + part[...]
+    mine[...] = total / count
+    swap_pair(me, mine, theirs, send_sem, recv_sem)
+    part = half_ref.shape[-1]
+    for core in range(2):
+        @pl.when(lax.rem(me, 2) == core)
+        def _():
+            scale_ref[:, :, core * part:(core + 1) * part] = mine[...]
+            scale_ref[:, :, (1 - core) * part:(2 - core) * part] = theirs[...]
+
+
+def narrow(n, rows, counts, x_ref, *refs):
+    held, parts = counts
+    sent = refs[parts + held:parts + held + n - 1]
+    out_ref, scale_ref, acc = refs[parts + held + n - 1:]
+    me = lax.axis_index("rows")
+    scale = refs[0][0]
+    if parts > 1:
+        for part in refs[1:parts]:
+            scale = scale + part[0]
+        scale = scale / (n * x_ref.shape[-1])
     scale_ref[0] = scale
 
     def put(d, e, cut, value):
@@ -204,6 +264,10 @@
     return stages
 
 
+def in_pairs(s, stages, n, wide):
+    return s + 2 == stages and n > 2 and n & (n - 1) == 0 and wide % (2 * LANES) == 0
+
+
 def per_device(n, owners, master_down, router_weight, router_gain):
     experts, height, width = master_down.shape
     quota = height // n
@@ -221,15 +285,15 @@
         functools.partial(head, n, rows),
         out_shape=[pltpu.VMEM((experts, rows, width), bf16)] * n + [
             jax.ShapeDtypeStruct((known, 1, wide), f32),
-            jax.ShapeDtypeStruct((n - 1, known, 1, wide), f32),
-            jax.ShapeDtypeStruct((1, 1, wide), f32),
             jax.ShapeDtypeStruct((n, mine_e, depth), bf16),
         ],
         in_specs=[hbm, hbm, hbm],
-        out_specs=[VMEM] * (n + 4),
+        out_specs=[VMEM] * (n + 2),
         scratch_shapes=[
             pltpu.VMEM((known, experts, n, rows, width), f32),
             pltpu.VMEM((wide, LANES), f32),
+            pltpu.VMEM((known, 1, wide), f32),
+            pltpu.VMEM((n - 1, known, 1, wide), f32),
             pltpu.VMEM((mine_e, depth), f32),
             pltpu.VMEM((1, depth), f32),
             pltpu.SemaphoreType.DMA((known,)),
@@ -240,18 +304,17 @@
             pltpu.SemaphoreType.DMA((n - 1,)),
         ],
         compiler_params=pltpu.CompilerParams(
-            collective_id=0, has_side_effects=True, vmem_limit_bytes=24 * MIB),
+            collective_id=0, has_side_effects=True, vmem_limit_bytes=62 * MIB),
         name="head",
     )(x, router_weight.T, router_gain[None, :])
-    own, mine, peers, scale0, strip = outs[n - 1:]
-    peers = [peers[d] for d in range(n - 1)]
-    scales = [scale0]
+    own, scale, strip = outs[n - 1:]
+    scales, parts, after = [scale], [scale], scale
+
+    def move(array, d):
+        return lax.ppermute(array, "rows", pairs(d, n))
 
     def permute(arrays):
-        got = []
-        for d in range(1, n):
-            got.append(lax.ppermute(arrays[d - 1], "rows", pairs(d, n)))
-        return got
+        return [move(arrays[d - 1], d) for d in range(1, n)]
 
     def sums(lo, hi, after):
         step = max(k for k in (4, 3, 2, 1) if (hi - lo) % k == 0)
@@ -268,26 +331,62 @@
             compiler_params=pltpu.CompilerParams(vmem_limit_bytes=24 * MIB),
         )(*[x] * step, after)
 
-    def scaled(lo, hi, base, mine, peers, out):
+    def sums_pair(lo, hi, after):
+        step = max(k for k in (5, 4, 3, 2, 1) if (hi - lo) % k == 0)
+        part = (hi - lo, 1, wide // 2)
+        sems = [pltpu.SemaphoreType.DMA, pltpu.SemaphoreType.DMA]
+        half = pl.pallas_call(
+            functools.partial(add_up_pair, rows, step),
+            grid=((hi - lo) // step,),
+            out_shape=jax.ShapeDtypeStruct(part, f32),
+            in_specs=[
+                pl.BlockSpec((experts, n, rows, width), lambda b, k=k: (0, 0, lo + b * step + k, 0))
+                for k in range(step)
+            ] + [ANY],
+            out_specs=pl.BlockSpec(part, lambda b: (0, 0, 0)),
+            scratch_shapes=[
+                pltpu.VMEM((step, wide, LANES), f32),
+                pltpu.VMEM((hi - lo, 1, wide), f32),
+                pltpu.VMEM((hi - lo, 1, wide), f32),
+            ] + sems,
+            compiler_params=pltpu.CompilerParams(
+                collective_id=2, has_side_effects=True, vmem_limit_bytes=24 * MIB),
+        )(*[x] * step, after)
+        got = [move(half, d) for d in range(2, n, 2)]
+
+        def finish():
+            return pl.pallas_call(
+                functools.partial(finish_pair, n * width),
+                out_shape=jax.ShapeDtypeStruct((hi - lo, 1, wide), f32),
+                in_specs=[VMEM] * (1 + len(got)),
+                out_specs=VMEM,
+                scratch_shapes=[pltpu.VMEM(part, f32), pltpu.VMEM(part, f32)] + sems,
+                compiler_params=pltpu.CompilerParams(
+                    collective_id=3, has_side_effects=True, vmem_limit_bytes=4 * MIB),
+            )(half, *got)
+
+        return finish
+
+    def scaled(lo, hi, base, parts, out, limit=16):
         part = pl.BlockSpec((1, 1, wide), lambda b: (lo - base + b, 0, 0))
         held = [] if out is None else [out]
         made = pl.pallas_call(
-            functools.partial(narrow, n, rows, len(held)),
+            functools.partial(narrow, n, rows, (len(held), len(parts))),
             grid=(hi - lo,),
             out_shape=[pltpu.HBM((experts, (hi - lo) * rows, width), bf16)] * (n - 1) + [
                 jax.ShapeDtypeStruct((experts, quota, n * width), bf16),
                 jax.ShapeDtypeStruct((hi - lo, 1, wide), f32),
             ],
             in_specs=[pl.BlockSpec((experts, n, rows, width), lambda b: (0, 0, lo + b, 0))]
-            + [part] * n + [ANY] * len(held),
+            + [part] * len(parts) + [ANY] * len(held),
             out_specs=[pl.BlockSpec((experts, rows, width), lambda b: (0, b, 0))] * (n - 1) + [
                 pl.BlockSpec((experts, rows, width), lambda b: (0, lo + b, lax.axis_index("rows"))),
                 pl.BlockSpec((1, 1, wide), lambda b: (b, 0, 0)),
             ],
             scratch_shapes=[pltpu.VMEM((wide, LANES), f32)],
-            input_output_aliases={n + 1: n - 1} if held else {},
-            compiler_params=pltpu.CompilerParams(vmem_limit_bytes=16 * MIB),
-        )(x, mine, *peers, *held)
+            input_output_aliases={len(parts) + 1: n - 1} if held else {},
+            compiler_params=pltpu.CompilerParams(vmem_limit_bytes=limit * MIB),
+        )(x, *parts, *held)
         return made[:n - 1], made[n - 1], made[n]
 
     def placed(spots, got, out):
@@ -310,14 +409,21 @@
     for s, stage in enumerate(stages):
         for k, (lo, hi) in enumerate(stage):
             if p:
-                sent, out, part = scaled(lo, hi, base, mine, peers, out)
-                scales.append(part)
+                sent, out, after = scaled(lo, hi, base, parts, out, 16 if s else 62)
+                if len(parts) > 1:
+                    scales.append(after)
             if k + 1 == len(stage) and s + 1 < len(stages):
                 base, end = hi, stages[s + 1][-1][1]
-                mine = sums(base, end, scales[-1])
-                peers = permute([mine] * (n - 1))
+                if in_pairs(s, len(stages), n, wide):
+                    finish = sums_pair(base, end, after)
+                else:
+                    mine = sums(base, end, after)
+                    parts = [mine] + permute([mine] * (n - 1))
             got.append(permute(sent))
             p += 1
+        if in_pairs(s, len(stages), n, wide):
+            parts = [finish()]
+            scales.append(parts[0])
 
     strips = pl.pallas_call(
         functools.partial(gather, owners),

time: 361 us -> 341 us (0.945)
  local copies, waits for them, and re-layouts: 37.4 us -> 17.8 us
  starting transfers between devices: 32.5 us -> 28.8 us
    unnamed x157 -> x101, local copies, waits for them, and re-layouts: 33.7 us -> 15.4 us
    pallas_call x10 -> x11, Pallas kernels: 55.1 us -> 70.7 us  [the longest x9 54.4 us: scaled(): pl.pallas_call(functools.partial(narrow, n, rows, (len(held), len(parts))...]
    pallas_call x2 -> x1, Pallas kernels: 18.7 us -> 5.58 us  [sums(): pl.pallas_call(functools.partial(add_up, rows), grid=((hi - lo) // step,)...]
    ppermute x39 -> x34, starting transfers between devices: 32.5 us -> 28.8 us  [move(): return lax.ppermute(array, 'rows', pairs(d, n))]
    ppermute x39 -> x34, waiting for transfers between devices: 177 us -> 177 us  [move(): return lax.ppermute(array, 'rows', pairs(d, n))]
    pallas_call x11 -> x10, Pallas kernels: 21.3 us -> 21.2 us  [placed(): pl.pallas_call(functools.partial(place, n, spots), out_shape=jax.ShapeDty...]
  transfers between devices with their start and end apart: 39 -> 34, of which waited for: 18 -> 18; matrix products, arithmetic and copies ran while one was open for 4% -> 1% of each run, Pallas kernels for 28% -> 31%
where the time goes in v3:
time: 341 us; the launch traced here: 338 us
  waiting for transfers between devices  177 us (52%)
  Pallas kernels  113 us (33%)
  starting transfers between devices  28.8 us (8%)
  local copies, waits for them, and re-layouts  17.8 us (5%)
    ppermute x34, waiting for transfers between devices, move(): return lax.ppermute(array, 'rows', pairs(d, n))  177 us
    pallas_call x9, Pallas kernels, scaled(): pl.pallas_call(functools.partial(narrow, n, rows, (len(held), len(parts))...  54.4 us
    ppermute x34, starting transfers between devices, move(): return lax.ppermute(array, 'rows', pairs(d, n))  28.8 us
    pallas_call x10, Pallas kernels, placed(): pl.pallas_call(functools.partial(place, n, spots), out_shape=jax.ShapeDty...  21.2 us
    unnamed x101, local copies, waits for them, and re-layouts  15.4 us
    pallas_call x1, Pallas kernels, sums_pair(): pl.pallas_call(functools.partial(add_up_pair, rows, step), grid=((hi - lo...  15 us
    pallas_call x1, Pallas kernels, per_device(): pl.pallas_call(functools.partial(head, n, rows), out_shape=[pltpu.VMEM((e...  8.08 us
    pallas_call x1, Pallas kernels, per_device(): pl.pallas_call(functools.partial(gather, owners), out_shape=jax.ShapeDtyp...  7.59 us
  transfers between devices with their start and end apart: 34, of which 18 were waited for; matrix products, arithmetic and copies ran while one was open for 1% of the time, Pallas kernels for 31%

profile of v3, /device:TPU:1, one launch (start us, length us, event | category | flops | bytes accessed | tf_op | source)
XLA Modules:
  0.0 338.3 jit_solution(6741847363753314564)
XLA Ops:
  0.6 8.1 %head.1 = (bf16[2,32,1024]{2,1,0:T(8,128)(2,1)}, bf16[2,32,1024]{2,1,0:T(8,128)(2,1)}, bf16[2,32,1024]{2,1,0:T(8,128)(2,1)S(1)}, bf16[2,32,1024]{2,1,0:T(8,128)(...) custom-call(f32[2,4,1600,1024]{3,2,1,0:T(8,128)} %bitcast.15, f32[2,1024]{1,0:T(2,128)} %bitcast.35, ...), custom_call_target="tpu_custom_call" | custom-call | tf_op jit(solution)/shard_map/head/pallas_call | solution.py:284
  9.2 2.6 shard_map.58
  11.9 2.5 shard_map.59
  15.1 5.6 %shard_map.60.refs_0_ = f32[10,1,256]{2,1,0:T(1,128)S(1)} custom-call(f32[2,4,1600,1024]{3,2,1,0:T(8,128)} %bitcast.18, f32[2,4,1600,1024]{3,2,1,0:T(8,128)} %bitcast.19, f32[2,1,256]{2,1,0:T(1,128)S(1)} %copy-done.33), custom_call_target="tpu_custom_call" | custom-call | tf_op jit(solution)/shard_map/pallas_call | solution.py:321
  21.1 1.4 collective-permute-start.1
  22.6 1.1 collective-permute-start.2
  23.7 2.4 collective-permute-done.2.refs_3_
  26.0 5.9 %shard_map.61 = (bf16[2,160,1024]{2,1,0:T(8,128)(2,1)}, bf16[2,160,1024]{2,1,0:T(8,128)(2,1)}, bf16[2,160,1024]{2,1,0:T(8,128)(2,1)}, bf16[2,1600,4096]{2,1,0:T(8,128)(2,1)}, f32[5,1,256]{2,1,0:T(1,128)S(1)}) custom-call(f32[2,4,1600,1024]{3,2,1,0:T(8,128)} %bitcast.20, f32[10,1,256]{2,1,0:T(1,128)S(1)} %shard_map.60.refs_0_, ...), custom_call_target="tpu_custom_call", output_to_operand_aliasing={{3}: (5, {})} | custom-call | tf_op jit(solution)/shard_map/pallas_call | solution.py:373
  31.9 5.9 %shard_map.62 = (bf16[2,160,1024]{2,1,0:T(8,128)(2,1)}, bf16[2,160,1024]{2,1,0:T(8,128)(2,1)}, bf16[2,160,1024]{2,1,0:T(8,128)(2,1)}, bf16[2,1600,4096]{2,1,0:T(8,128)(2,1)}, f32[5,1,256]{2,1,0:T(1,128)S(1)}) custom-call(f32[2,4,1600,1024]{3,2,1,0:T(8,128)} %bitcast.21, f32[10,1,256]{2,1,0:T(1,128)S(1)} %shard_map.60.refs_0_, ...), custom_call_target="tpu_custom_call", output_to_operand_aliasing={{3}: (5, {})} | custom-call | tf_op jit(solution)/shard_map/pallas_call | solution.py:373
  37.9 15.0 %shard_map.63.half_ref = f32[35,1,128]{2,1,0:T(1,128)S(1)} custom-call(f32[2,4,1600,1024]{3,2,1,0:T(8,128)} %bitcast.22, f32[2,4,1600,1024]{3,2,1,0:T(8,128)} %bitcast.23, f32[2,4,1600,1024]{3,2,1,0:T(8,128)} %bitcast.24, f32[2,4,1600,1024]{3,2,1,0:T(8,128)} %bitcast.25, f32[2,4,1600,1024]{3,2,1,0:T(8,128)} %bitcast.26, ...), custom_call_target="tpu_custom_call" | custom-call | tf_op jit(solution)/shard_map/pallas_call | solution.py:338
  54.0 1.5 collective-permute-done.3.refs_0_
  55.6 1.8 collective-permute-start.33
  57.4 0.8 collective-permute-start.29
  58.6 2.6 collective-permute-done.33.refs_2_
  61.9 1.0 collective-permute-start.23
  62.9 1.4 collective-permute-start.25
  64.3 3.3 collective-permute-done.29.refs_1_
  68.9 3.5 %collective-permute-done.30.refs_2_ = bf16[2,64,1024]{2,1,0:T(8,128)(2,1)S(1)} collective-permute-done((bf16[2,64,1024]{2,1,0:T(8,128)(2,1)S(1)}, bf16[2,64,1024]{2,1,0:T(8,128)(2,1)S(1)}, u32[]{:S(2)}, u32[]{:S(2)}) %collective-permute-start.30) | collective-permute-done | bytes 262176 | tf_op jit(solution)/shard_map/ppermute | solution.py:314
  73.2 2.0 collective-permute-start.27
  75.9 17.0 %collective-permute-done.26.refs_1_ = bf16[2,64,1024]{2,1,0:T(8,128)(2,1)S(1)} collective-permute-done((bf16[2,64,1024]{2,1,0:T(8,128)(2,1)S(1)}, bf16[2,64,1024]{2,1,0:T(8,128)(2,1)S(1)}, u32[]{:S(2)}, u32[]{:S(2)}) %collective-permute-start.26) | collective-permute-done | bytes 262176 | tf_op jit(solution)/shard_map/ppermute | solution.py:314
  93.6 4.1 %collective-permute-done.27.refs_2_ = bf16[2,64,1024]{2,1,0:T(8,128)(2,1)S(1)} collective-permute-done((bf16[2,64,1024]{2,1,0:T(8,128)(2,1)S(1)}, bf16[2,64,1024]{2,1,0:T(8,128)(2,1)S(1)}, u32[]{:S(2)}, u32[]{:S(2)}) %collective-permute-start.27) | collective-permute-done | bytes 262176 | tf_op jit(solution)/shard_map/ppermute | solution.py:314
  98.4 1.0 collective-permute-start.20
  99.5 0.8 copy-done.8
  100.3 2.1 collective-permute-start.21
  102.4 1.2 shard_map.64.refs_0_
  103.6 9.4 %shard_map.65 = (bf16[2,288,1024]{2,1,0:T(8,128)(2,1)}, bf16[2,288,1024]{2,1,0:T(8,128)(2,1)}, bf16[2,288,1024]{2,1,0:T(8,128)(2,1)}, bf16[2,1600,4096]{2,1,0:T(8,128)(2,1)}, f32[9,1,256]{2,1,0:T(1,128)}) custom-call(f32[2,4,1600,1024]{3,2,1,0:T(8,128)} %bitcast.27, f32[35,1,256]{2,1,0:T(1,128)S(1)} %shard_map.64.refs_0_, ...), custom_call_target="tpu_custom_call", output_to_operand_aliasing={{3}: (2, {})} | custom-call | tf_op jit(solution)/shard_map/pallas_call | solution.py:373
  113.2 10.1 %shard_map.66 = (bf16[2,320,1024]{2,1,0:T(8,128)(2,1)}, bf16[2,320,1024]{2,1,0:T(8,128)(2,1)}, bf16[2,320,1024]{2,1,0:T(8,128)(2,1)}, bf16[2,1600,4096]{2,1,0:T(8,128)(2,1)}, f32[10,1,256]{2,1,0:T(1,128)}) custom-call(f32[2,4,1600,1024]{3,2,1,0:T(8,128)} %bitcast.28, f32[35,1,256]{2,1,0:T(1,128)S(1)} %shard_map.64.refs_0_, ...), custom_call_target="tpu_custom_call", output_to_operand_aliasing={{3}: (2, {})} | custom-call | tf_op jit(solution)/shard_map/pallas_call | solution.py:373
  125.2 1.4 collective-permute-done.20.refs_1_
  127.1 9.9 %shard_map.67 = (bf16[2,320,1024]{2,1,0:T(8,128)(2,1)}, bf16[2,320,1024]{2,1,0:T(8,128)(2,1)}, bf16[2,320,1024]{2,1,0:T(8,128)(2,1)}, bf16[2,1600,4096]{2,1,0:T(8,128)(2,1)}, f32[10,1,256]{2,1,0:T(1,128)}) custom-call(f32[2,4,1600,1024]{3,2,1,0:T(8,128)} %bitcast.29, f32[35,1,256]{2,1,0:T(1,128)S(1)} %shard_map.64.refs_0_, ...), custom_call_target="tpu_custom_call", output_to_operand_aliasing={{3}: (2, {})} | custom-call | tf_op jit(solution)/shard_map/pallas_call | solution.py:373
  137.1 6.0 %shard_map.68 = (bf16[2,160,1024]{2,1,0:T(8,128)(2,1)}, bf16[2,160,1024]{2,1,0:T(8,128)(2,1)}, bf16[2,160,1024]{2,1,0:T(8,128)(2,1)}, bf16[2,1600,4096]{2,1,0:T(8,128)(2,1)}, f32[5,1,256]{2,1,0:T(1,128)}) custom-call(f32[2,4,1600,1024]{3,2,1,0:T(8,128)} %bitcast.30, f32[35,1,256]{2,1,0:T(1,128)S(1)} %shard_map.64.refs_0_, ...), custom_call_target="tpu_custom_call", output_to_operand_aliasing={{3}: (2, {})} | custom-call | tf_op jit(solution)/shard_map/pallas_call | solution.py:373
  144.5 1.9 collective-permute-done.7.refs_0_
  146.4 0.8 copy-done.18
  147.2 0.8 collective-permute-start.14
  148.1 1.0 copy-done.2
  149.1 1.2 collective-permute-start.15
  150.3 15.6 %collective-permute-done.17.refs_1_ = bf16[2,288,1024]{2,1,0:T(8,128)(2,1)S(1)} collective-permute-done((bf16[2,288,1024]{2,1,0:T(8,128)(2,1)S(1)}, bf16[2,288,1024]{2,1,0:T(8,128)(2,1)S(1)}, u32[]{:S(2)}, u32[]{:S(2)}) %collective-permute-start.17) | collective-permute-done | bytes 1179680 | tf_op jit(solution)/shard_map/ppermute | solution.py:314
  165.9 1.1 copy-done.4
  167.0 23.5 %collective-permute-done.18.refs_2_ = bf16[2,288,1024]{2,1,0:T(8,128)(2,1)S(1)} collective-permute-done((bf16[2,288,1024]{2,1,0:T(8,128)(2,1)S(1)}, bf16[2,288,1024]{2,1,0:T(8,128)(2,1)S(1)}, u32[]{:S(2)}, u32[]{:S(2)}) %collective-permute-start.18) | collective-permute-done | bytes 1179680 | tf_op jit(solution)/shard_map/ppermute | solution.py:314
  190.4 1.0 copy-done.6
  191.5 1.0 collective-permute-start.11
  192.5 2.1 collective-permute-start.12
  194.6 24.7 %collective-permute-done.14.refs_1_ = bf16[2,320,1024]{2,1,0:T(8,128)(2,1)S(1)} collective-permute-done((bf16[2,320,1024]{2,1,0:T(8,128)(2,1)S(1)}, bf16[2,320,1024]{2,1,0:T(8,128)(2,1)S(1)}, u32[]{:S(2)}, u32[]{:S(2)}) %collective-permute-start.14) | collective-permute-done | bytes 1310752 | tf_op jit(solution)/shard_map/ppermute | solution.py:314
  219.9 26.7 %collective-permute-done.15.refs_2_ = bf16[2,320,1024]{2,1,0:T(8,128)(2,1)S(1)} collective-permute-done((bf16[2,320,1024]{2,1,0:T(8,128)(2,1)S(1)}, bf16[2,320,1024]{2,1,0:T(8,128)(2,1)S(1)}, u32[]{:S(2)}, u32[]{:S(2)}) %collective-permute-start.15) | collective-permute-done | bytes 1310752 | tf_op jit(solution)/shard_map/ppermute | solution.py:314
  246.6 1.1 copy-done
  247.7 2.0 collective-permute-start.9
  249.7 7.6 %router.1 = bf16[8,4,2,1024]{3,2,1,0:T(2,128)(2,1)S(1)} custom-call(bf16[4,2,1024]{2,1,0:T(2,128)(2,1)S(1)} %copy-done.32), custom_call_target="tpu_custom_call" | custom-call | tf_op jit(solution)/shard_map/router/pallas_call | solution.py:428
  258.0 2.2 shard_map.69
  260.6 14.9 %collective-permute-done.11.refs_1_ = bf16[2,320,1024]{2,1,0:T(8,128)(2,1)} collective-permute-done((bf16[2,320,1024]{2,1,0:T(8,128)(2,1)}, bf16[2,320,1024]{2,1,0:T(8,128)(2,1)}, u32[]{:S(2)}, u32[]{:S(2)}) %collective-permute-start.11) | collective-permute-done | bytes 1310752 | tf_op jit(solution)/shard_map/ppermute | solution.py:314
  276.2 26.7 %collective-permute-done.12.refs_2_ = bf16[2,320,1024]{2,1,0:T(8,128)(2,1)} collective-permute-done((bf16[2,320,1024]{2,1,0:T(8,128)(2,1)}, bf16[2,320,1024]{2,1,0:T(8,128)(2,1)}, u32[]{:S(2)}, u32[]{:S(2)}) %collective-permute-start.12) | collective-permute-done | bytes 1310752 | tf_op jit(solution)/shard_map/ppermute | solution.py:314
  302.9 2.0 collective-permute-start.6
  307.2 0.9 copy-done.31
  308.1 1.8 shard_map.70.refs_3_
  310.0 1.9 shard_map.71.refs_3_
  312.0 1.0 shard_map.72.refs_3_
  313.6 1.9 shard_map.73.refs_3_
  315.6 1.9 shard_map.74.refs_3_
  318.3 2.6 shard_map.75.refs_3_
  320.8 2.3 shard_map.76.refs_3_
  323.1 3.4 shard_map.77.refs_3_
  326.5 4.5 %collective-permute-done.9.refs_2_ = bf16[2,160,1024]{2,1,0:T(8,128)(2,1)} collective-permute-done((bf16[2,160,1024]{2,1,0:T(8,128)(2,1)}, bf16[2,160,1024]{2,1,0:T(8,128)(2,1)}, u32[]{:S(2)}, u32[]{:S(2)}) %collective-permute-start.9) | collective-permute-done | bytes 655392 | tf_op jit(solution)/shard_map/ppermute | solution.py:314
  331.0 2.6 shard_map.78.refs_3_
  333.6 0.9 collective-permute-done.5.refs_1_
  334.5 2.0 collective-permute-done.6.refs_2_
  336.6 1.7 shard_map.79
  (135 shorter events, 18.2 us)
Async XLA Ops:
  8.7 48.7 %collective-permute-start.31 = (bf16[2,32,1024]{2,1,0:T(8,128)(2,1)}, bf16[2,32,1024]{2,1,0:T(8,128)(2,1)}, u32[]{:S(2)}, u32[]{:S(2)}) collective-permute-start(bf16[2,32,1024]{2,1,0:T(8,128)(2,1)} %get-tuple-element.86), channel_id=1, source_target_pairs={{0,1},{1,0},{2,3},{3,2},{4,5},{5,4},{6,7},{7,6},{8,9},{9,8},{10,11... | collective-permute-start | bytes 393224 | tf_op jit(solution)/shard_map/ppermute | solution.py:314
  9.2 49.1 %collective-permute-start.32 = (bf16[2,32,1024]{2,1,0:T(8,128)(2,1)}, bf16[2,32,1024]{2,1,0:T(8,128)(2,1)}, u32[]{:S(2)}, u32[]{:S(2)}) collective-permute-start(bf16[2,32,1024]{2,1,0:T(8,128)(2,1)} %get-tuple-element.87), channel_id=1, source_target_pairs={{0,2},{1,3},{2,0},{3,1},{4,6},{5,7},{6,4},{7,5},{8,10},{9,11},{10,... | collective-permute-start | bytes 393224 | tf_op jit(solution)/shard_map/ppermute | solution.py:314
  11.7 51.2 %collective-permute-start.28 = (bf16[2,64,1024]{2,1,0:T(8,128)(2,1)}, bf16[2,64,1024]{2,1,0:T(8,128)(2,1)}, u32[]{:S(2)}, u32[]{:S(2)}) collective-permute-start(bf16[2,64,1024]{2,1,0:T(8,128)(2,1)} %get-tuple-element.83), channel_id=1, source_target_pairs={{0,1},{1,0},{2,3},{3,2},{4,5},{5,4},{6,7},{7,6},{8,9},{9,8},{10,11... | collective-permute-start | bytes 786440 | tf_op jit(solution)/shard_map/ppermute | solution.py:314
  20.7 1.9 collective-permute-start
  21.1 2.5 collective-permute-start.1
  22.6 3.5 %collective-permute-start.2 = (f32[10,1,256]{2,1,0:T(1,128)S(1)}, f32[10,1,256]{2,1,0:T(1,128)S(1)}, u32[]{:S(2)}, u32[]{:S(2)}) collective-permute-start(f32[10,1,256]{2,1,0:T(1,128)S(1)} %shard_map.60.refs_0_), channel_id=1, source_target_pairs={{0,3},{1,2},{2,1},{3,0},{4,7},{5,6},{6,5},{7,4},{8,11},{9,10},{10,... | collective-permute-start | bytes 30728 | tf_op jit(solution)/shard_map/ppermute | solution.py:314
  37.8 15.6 %copy-start.44 = (bf16[2,160,1024]{2,1,0:T(8,128)(2,1)S(1)}, bf16[2,160,1024]{2,1,0:T(8,128)(2,1)}, u32[]{:S(2)}) copy-start(bf16[2,160,1024]{2,1,0:T(8,128)(2,1)} %get-tuple-element.77) | copy-start | bytes 1966084
  37.8 19.6 %copy-start.49 = (bf16[2,64,1024]{2,1,0:T(8,128)(2,1)S(1)}, bf16[2,64,1024]{2,1,0:T(8,128)(2,1)}, u32[]{:S(2)}) copy-start(bf16[2,64,1024]{2,1,0:T(8,128)(2,1)} %get-tuple-element.84) | copy-start | bytes 786436
  37.8 20.5 %copy-start.47 = (bf16[2,64,1024]{2,1,0:T(8,128)(2,1)S(1)}, bf16[2,64,1024]{2,1,0:T(8,128)(2,1)}, u32[]{:S(2)}) copy-start(bf16[2,64,1024]{2,1,0:T(8,128)(2,1)} %get-tuple-element.85) | copy-start | bytes 786436
  37.8 24.1 %copy-start.43 = (bf16[2,160,1024]{2,1,0:T(8,128)(2,1)S(1)}, bf16[2,160,1024]{2,1,0:T(8,128)(2,1)}, u32[]{:S(2)}) copy-start(bf16[2,160,1024]{2,1,0:T(8,128)(2,1)} %get-tuple-element.78) | copy-start | bytes 1966084
  37.8 25.1 %copy-start.48 = (bf16[2,64,1024]{2,1,0:T(8,128)(2,1)S(1)}, bf16[2,64,1024]{2,1,0:T(8,128)(2,1)}, u32[]{:S(2)}) copy-start(bf16[2,64,1024]{2,1,0:T(8,128)(2,1)} %get-tuple-element.80) | copy-start | bytes 786436
  37.8 30.5 %copy-start.46 = (bf16[2,64,1024]{2,1,0:T(8,128)(2,1)S(1)}, bf16[2,64,1024]{2,1,0:T(8,128)(2,1)}, u32[]{:S(2)}) copy-start(bf16[2,64,1024]{2,1,0:T(8,128)(2,1)} %get-tuple-element.81) | copy-start | bytes 786436
  37.8 35.4 %copy-start.45 = (bf16[2,64,1024]{2,1,0:T(8,128)(2,1)S(1)}, bf16[2,64,1024]{2,1,0:T(8,128)(2,1)}, u32[]{:S(2)}) copy-start(bf16[2,64,1024]{2,1,0:T(8,128)(2,1)} %get-tuple-element.82) | copy-start | bytes 786436
  37.8 38.0 %copy-start.42 = (bf16[2,160,1024]{2,1,0:T(8,128)(2,1)S(1)}, bf16[2,160,1024]{2,1,0:T(8,128)(2,1)}, u32[]{:S(2)}) copy-start(bf16[2,160,1024]{2,1,0:T(8,128)(2,1)} %get-tuple-element.79) | copy-start | bytes 1966084
  37.8 55.8 %copy-start.41 = (bf16[2,160,1024]{2,1,0:T(8,128)(2,1)S(1)}, bf16[2,160,1024]{2,1,0:T(8,128)(2,1)}, u32[]{:S(2)}) copy-start(bf16[2,160,1024]{2,1,0:T(8,128)(2,1)} %get-tuple-element.74) | copy-start | bytes 1966084
  37.8 60.6 %copy-start.40 = (bf16[2,160,1024]{2,1,0:T(8,128)(2,1)S(1)}, bf16[2,160,1024]{2,1,0:T(8,128)(2,1)}, u32[]{:S(2)}) copy-start(bf16[2,160,1024]{2,1,0:T(8,128)(2,1)} %get-tuple-element.75) | copy-start | bytes 1966084
  37.9 62.4 %copy-start.39 = (bf16[2,160,1024]{2,1,0:T(8,128)(2,1)S(1)}, bf16[2,160,1024]{2,1,0:T(8,128)(2,1)}, u32[]{:S(2)}) copy-start(bf16[2,160,1024]{2,1,0:T(8,128)(2,1)} %get-tuple-element.76) | copy-start | bytes 1966084
  52.9 2.7 collective-permute-start.3
  53.4 46.0 %collective-permute-start.22 = (bf16[2,160,1024]{2,1,0:T(8,128)(2,1)S(1)}, bf16[2,160,1024]{2,1,0:T(8,128)(2,1)S(1)}, u32[]{:S(2)}, u32[]{:S(2)}) collective-permute-start(bf16[2,160,1024]{2,1,0:T(8,128)(2,1)S(1)} %copy-done.44), channel_id=1, source_target_pairs={{0,1},{1,0},{2,3},{3,2},{4,5},{5,4},{6,7},{7,6},{8,9},{9,8},{10,11... | collective-permute-start | bytes 1966088 | tf_op jit(solution)/shard_map/ppermute | solution.py:314
  55.6 5.7 %collective-permute-start.33 = (bf16[2,32,1024]{2,1,0:T(8,128)(2,1)S(1)}, bf16[2,32,1024]{2,1,0:T(8,128)(2,1)S(1)}, u32[]{:S(2)}, u32[]{:S(2)}) collective-permute-start(bf16[2,32,1024]{2,1,0:T(8,128)(2,1)S(1)} %get-tuple-element.88), channel_id=1, source_target_pairs={{0,3},{1,2},{2,1},{3,0},{4,7},{5,6},{6,5},{7,4},{8,11},{9,10},{10,... | collective-permute-start | bytes 393224 | tf_op jit(solution)/shard_map/ppermute | solution.py:314
  57.4 10.2 %collective-permute-start.29 = (bf16[2,64,1024]{2,1,0:T(8,128)(2,1)S(1)}, bf16[2,64,1024]{2,1,0:T(8,128)(2,1)S(1)}, u32[]{:S(2)}, u32[]{:S(2)}) collective-permute-start(bf16[2,64,1024]{2,1,0:T(8,128)(2,1)S(1)} %copy-done.49), channel_id=1, source_target_pairs={{0,2},{1,3},{2,0},{3,1},{4,6},{5,7},{6,4},{7,5},{8,10},{9,11},{10,... | collective-permute-start | bytes 786440 | tf_op jit(solution)/shard_map/ppermute | solution.py:314
  58.2 14.2 %collective-permute-start.30 = (bf16[2,64,1024]{2,1,0:T(8,128)(2,1)S(1)}, bf16[2,64,1024]{2,1,0:T(8,128)(2,1)S(1)}, u32[]{:S(2)}, u32[]{:S(2)}) collective-permute-start(bf16[2,64,1024]{2,1,0:T(8,128)(2,1)S(1)} %copy-done.47), channel_id=1, source_target_pairs={{0,3},{1,2},{2,1},{3,0},{4,7},{5,6},{6,5},{7,4},{8,11},{9,10},{10,... | collective-permute-start | bytes 786440 | tf_op jit(solution)/shard_map/ppermute | solution.py:314
  61.9 51.1 %collective-permute-start.23 = (bf16[2,160,1024]{2,1,0:T(8,128)(2,1)S(1)}, bf16[2,160,1024]{2,1,0:T(8,128)(2,1)S(1)}, u32[]{:S(2)}, u32[]{:S(2)}) collective-permute-start(bf16[2,160,1024]{2,1,0:T(8,128)(2,1)S(1)} %copy-done.43), channel_id=1, source_target_pairs={{0,2},{1,3},{2,0},{3,1},{4,6},{5,7},{6,4},{7,5},{8,10},{9,11},{10,... | collective-permute-start | bytes 1966088 | tf_op jit(solution)/shard_map/ppermute | solution.py:314
  62.9 12.2 %collective-permute-start.25 = (bf16[2,64,1024]{2,1,0:T(8,128)(2,1)S(1)}, bf16[2,64,1024]{2,1,0:T(8,128)(2,1)S(1)}, u32[]{:S(2)}, u32[]{:S(2)}) collective-permute-start(bf16[2,64,1024]{2,1,0:T(8,128)(2,1)S(1)} %copy-done.48), channel_id=1, source_target_pairs={{0,1},{1,0},{2,3},{3,2},{4,5},{5,4},{6,7},{7,6},{8,9},{9,8},{10,11... | collective-permute-start | bytes 786440 | tf_op jit(solution)/shard_map/ppermute | solution.py:314
  68.3 24.6 %collective-permute-start.26 = (bf16[2,64,1024]{2,1,0:T(8,128)(2,1)S(1)}, bf16[2,64,1024]{2,1,0:T(8,128)(2,1)S(1)}, u32[]{:S(2)}, u32[]{:S(2)}) collective-permute-start(bf16[2,64,1024]{2,1,0:T(8,128)(2,1)S(1)} %copy-done.46), channel_id=1, source_target_pairs={{0,2},{1,3},{2,0},{3,1},{4,6},{5,7},{6,4},{7,5},{8,10},{9,11},{10,... | collective-permute-start | bytes 786440 | tf_op jit(solution)/shard_map/ppermute | solution.py:314
  73.2 24.6 %collective-permute-start.27 = (bf16[2,64,1024]{2,1,0:T(8,128)(2,1)S(1)}, bf16[2,64,1024]{2,1,0:T(8,128)(2,1)S(1)}, u32[]{:S(2)}, u32[]{:S(2)}) collective-permute-start(bf16[2,64,1024]{2,1,0:T(8,128)(2,1)S(1)} %copy-done.45), channel_id=1, source_target_pairs={{0,3},{1,2},{2,1},{3,0},{4,7},{5,6},{6,5},{7,4},{8,11},{9,10},{10,... | collective-permute-start | bytes 786440 | tf_op jit(solution)/shard_map/ppermute | solution.py:314
  75.9 47.4 %collective-permute-start.24 = (bf16[2,160,1024]{2,1,0:T(8,128)(2,1)S(1)}, bf16[2,160,1024]{2,1,0:T(8,128)(2,1)S(1)}, u32[]{:S(2)}, u32[]{:S(2)}) collective-permute-start(bf16[2,160,1024]{2,1,0:T(8,128)(2,1)S(1)} %copy-done.42), channel_id=1, source_target_pairs={{0,3},{1,2},{2,1},{3,0},{4,7},{5,6},{6,5},{7,4},{8,11},{9,10},{10,... | collective-permute-start | bytes 1966088 | tf_op jit(solution)/shard_map/ppermute | solution.py:314
  93.6 30.9 %collective-permute-start.19 = (bf16[2,160,1024]{2,1,0:T(8,128)(2,1)S(1)}, bf16[2,160,1024]{2,1,0:T(8,128)(2,1)S(1)}, u32[]{:S(2)}, u32[]{:S(2)}) collective-permute-start(bf16[2,160,1024]{2,1,0:T(8,128)(2,1)S(1)} %copy-done.41), channel_id=1, source_target_pairs={{0,1},{1,0},{2,3},{3,2},{4,5},{5,4},{6,7},{7,6},{8,9},{9,8},{10,11... | collective-permute-start | bytes 1966088 | tf_op jit(solution)/shard_map/ppermute | solution.py:314
  98.4 28.2 %collective-permute-start.20 = (bf16[2,160,1024]{2,1,0:T(8,128)(2,1)S(1)}, bf16[2,160,1024]{2,1,0:T(8,128)(2,1)S(1)}, u32[]{:S(2)}, u32[]{:S(2)}) collective-permute-start(bf16[2,160,1024]{2,1,0:T(8,128)(2,1)S(1)} %copy-done.40), channel_id=1, source_target_pairs={{0,2},{1,3},{2,0},{3,1},{4,6},{5,7},{6,4},{7,5},{8,10},{9,11},{10,... | collective-permute-start | bytes 1966088 | tf_op jit(solution)/shard_map/ppermute | solution.py:314
  100.3 42.8 %collective-permute-start.21 = (bf16[2,160,1024]{2,1,0:T(8,128)(2,1)S(1)}, bf16[2,160,1024]{2,1,0:T(8,128)(2,1)S(1)}, u32[]{:S(2)}, u32[]{:S(2)}) collective-permute-start(bf16[2,160,1024]{2,1,0:T(8,128)(2,1)S(1)} %copy-done.39), channel_id=1, source_target_pairs={{0,3},{1,2},{2,1},{3,0},{4,7},{5,6},{6,5},{7,4},{8,11},{9,10},{10,... | collective-permute-start | bytes 1966088 | tf_op jit(solution)/shard_map/ppermute | solution.py:314
  113.0 35.1 %collective-permute-start.16 = (bf16[2,288,1024]{2,1,0:T(8,128)(2,1)}, bf16[2,288,1024]{2,1,0:T(8,128)(2,1)S(1)}, u32[]{:S(2)}, u32[]{:S(2)}) collective-permute-start(bf16[2,288,1024]{2,1,0:T(8,128)(2,1)} %get-tuple-element.71), channel_id=1, source_target_pairs={{0,1},{1,0},{2,3},{3,2},{4,5},{5,4},{6,7},{7,6},{8,9},{9,8},{10,11... | collective-permute-start | bytes 3538952 | tf_op jit(solution)/shard_map/ppermute | solution.py:314
  113.2 11.3 %copy-start.38 = (bf16[2,288,1024]{2,1,0:T(8,128)(2,1)S(1)}, bf16[2,288,1024]{2,1,0:T(8,128)(2,1)}, u32[]{:S(2)}) copy-start(bf16[2,288,1024]{2,1,0:T(8,128)(2,1)} %get-tuple-element.72) | copy-start | bytes 3538948
  113.2 13.4 %copy-start.37 = (bf16[2,288,1024]{2,1,0:T(8,128)(2,1)S(1)}, bf16[2,288,1024]{2,1,0:T(8,128)(2,1)}, u32[]{:S(2)}) copy-start(bf16[2,288,1024]{2,1,0:T(8,128)(2,1)} %get-tuple-element.73) | copy-start | bytes 3538948
  124.1 68.4 %collective-permute-start.13 = (bf16[2,320,1024]{2,1,0:T(8,128)(2,1)}, bf16[2,320,1024]{2,1,0:T(8,128)(2,1)S(1)}, u32[]{:S(2)}, u32[]{:S(2)}) collective-permute-start(bf16[2,320,1024]{2,1,0:T(8,128)(2,1)} %get-tuple-element.68), channel_id=1, source_target_pairs={{0,1},{1,0},{2,3},{3,2},{4,5},{5,4},{6,7},{7,6},{8,9},{9,8},{10,11... | collective-permute-start | bytes 3932168 | tf_op jit(solution)/shard_map/ppermute | solution.py:314
  124.5 12.6 %copy-start.12 = (bf16[2,160,1024]{2,1,0:T(8,128)(2,1)}, bf16[2,160,1024]{2,1,0:T(8,128)(2,1)S(1)}, u32[]{:S(2)}) copy-start(bf16[2,160,1024]{2,1,0:T(8,128)(2,1)S(1)} %collective-permute-done.19.refs_0_) | copy-start | bytes 1966084
  124.5 41.4 %collective-permute-start.17 = (bf16[2,288,1024]{2,1,0:T(8,128)(2,1)S(1)}, bf16[2,288,1024]{2,1,0:T(8,128)(2,1)S(1)}, u32[]{:S(2)}, u32[]{:S(2)}) collective-permute-start(bf16[2,288,1024]{2,1,0:T(8,128)(2,1)S(1)} %copy-done.38), channel_id=1, source_target_pairs={{0,2},{1,3},{2,0},{3,1},{4,6},{5,7},{6,4},{7,5},{8,10},{9,11},{10,... | collective-permute-start | bytes 3538952 | tf_op jit(solution)/shard_map/ppermute | solution.py:314
  126.6 10.5 %copy-start.14 = (bf16[2,160,1024]{2,1,0:T(8,128)(2,1)}, bf16[2,160,1024]{2,1,0:T(8,128)(2,1)S(1)}, u32[]{:S(2)}) copy-start(bf16[2,160,1024]{2,1,0:T(8,128)(2,1)S(1)} %collective-permute-done.20.refs_1_) | copy-start | bytes 1966084
  126.6 63.8 %collective-permute-start.18 = (bf16[2,288,1024]{2,1,0:T(8,128)(2,1)S(1)}, bf16[2,288,1024]{2,1,0:T(8,128)(2,1)S(1)}, u32[]{:S(2)}, u32[]{:S(2)}) collective-permute-start(bf16[2,288,1024]{2,1,0:T(8,128)(2,1)S(1)} %copy-done.37), channel_id=1, source_target_pairs={{0,3},{1,2},{2,1},{3,0},{4,7},{5,6},{6,5},{7,4},{8,11},{9,10},{10,... | collective-permute-start | bytes 3538952 | tf_op jit(solution)/shard_map/ppermute | solution.py:314
  137.1 10.2 %copy-start.36 = (bf16[2,320,1024]{2,1,0:T(8,128)(2,1)S(1)}, bf16[2,320,1024]{2,1,0:T(8,128)(2,1)}, u32[]{:S(2)}) copy-start(bf16[2,320,1024]{2,1,0:T(8,128)(2,1)} %get-tuple-element.69) | copy-start | bytes 3932164
  137.1 12.0 %copy-start.35 = (bf16[2,320,1024]{2,1,0:T(8,128)(2,1)S(1)}, bf16[2,320,1024]{2,1,0:T(8,128)(2,1)}, u32[]{:S(2)}) copy-start(bf16[2,320,1024]{2,1,0:T(8,128)(2,1)} %get-tuple-element.70) | copy-start | bytes 3932164
  137.1 112.6 %copy-start.32 = (bf16[4,2,1024]{2,1,0:T(2,128)(2,1)S(1)}, bf16[4,2,1024]{2,1,0:T(2,128)(2,1)}, u32[]{:S(2)}) copy-start(bf16[4,2,1024]{2,1,0:T(2,128)(2,1)} %get-tuple-element.92.strip_ref) | copy-start | bytes 49156
  144.0 2.4 collective-permute-start.7
  147.2 72.0 %collective-permute-start.14 = (bf16[2,320,1024]{2,1,0:T(8,128)(2,1)S(1)}, bf16[2,320,1024]{2,1,0:T(8,128)(2,1)S(1)}, u32[]{:S(2)}, u32[]{:S(2)}) collective-permute-start(bf16[2,320,1024]{2,1,0:T(8,128)(2,1)S(1)} %copy-done.36), channel_id=1, source_target_pairs={{0,2},{1,3},{2,0},{3,1},{4,6},{5,7},{6,4},{7,5},{8,10},{9,11},{10,... | collective-permute-start | bytes 3932168 | tf_op jit(solution)/shard_map/ppermute | solution.py:314
  149.1 97.5 %collective-permute-start.15 = (bf16[2,320,1024]{2,1,0:T(8,128)(2,1)S(1)}, bf16[2,320,1024]{2,1,0:T(8,128)(2,1)S(1)}, u32[]{:S(2)}, u32[]{:S(2)}) collective-permute-start(bf16[2,320,1024]{2,1,0:T(8,128)(2,1)S(1)} %copy-done.35), channel_id=1, source_target_pairs={{0,3},{1,2},{2,1},{3,0},{4,7},{5,6},{6,5},{7,4},{8,11},{9,10},{10,... | collective-permute-start | bytes 3932168 | tf_op jit(solution)/shard_map/ppermute | solution.py:314
  167.0 93.3 %collective-permute-start.10 = (bf16[2,320,1024]{2,1,0:T(8,128)(2,1)}, bf16[2,320,1024]{2,1,0:T(8,128)(2,1)}, u32[]{:S(2)}, u32[]{:S(2)}) collective-permute-start(bf16[2,320,1024]{2,1,0:T(8,128)(2,1)} %get-tuple-element.65), channel_id=1, source_target_pairs={{0,1},{1,0},{2,3},{3,2},{4,5},{5,4},{6,7},{7,6},{8,9},{9,8},{10,11... | collective-permute-start | bytes 3932168 | tf_op jit(solution)/shard_map/ppermute | solution.py:314
  191.5 84.1 %collective-permute-start.11 = (bf16[2,320,1024]{2,1,0:T(8,128)(2,1)}, bf16[2,320,1024]{2,1,0:T(8,128)(2,1)}, u32[]{:S(2)}, u32[]{:S(2)}) collective-permute-start(bf16[2,320,1024]{2,1,0:T(8,128)(2,1)} %get-tuple-element.66), channel_id=1, source_target_pairs={{0,2},{1,3},{2,0},{3,1},{4,6},{5,7},{6,4},{7,5},{8,10},{9,11},{10,... | collective-permute-start | bytes 3932168 | tf_op jit(solution)/shard_map/ppermute | solution.py:314
  192.5 110.4 %collective-permute-start.12 = (bf16[2,320,1024]{2,1,0:T(8,128)(2,1)}, bf16[2,320,1024]{2,1,0:T(8,128)(2,1)}, u32[]{:S(2)}, u32[]{:S(2)}) collective-permute-start(bf16[2,320,1024]{2,1,0:T(8,128)(2,1)} %get-tuple-element.67), channel_id=1, source_target_pairs={{0,3},{1,2},{2,1},{3,0},{4,7},{5,6},{6,5},{7,4},{8,11},{9,10},{10,... | collective-permute-start | bytes 3932168 | tf_op jit(solution)/shard_map/ppermute | solution.py:314
  219.3 107.2 %collective-permute-start.8 = (bf16[2,160,1024]{2,1,0:T(8,128)(2,1)}, bf16[2,160,1024]{2,1,0:T(8,128)(2,1)}, u32[]{:S(2)}, u32[]{:S(2)}) collective-permute-start(bf16[2,160,1024]{2,1,0:T(8,128)(2,1)} %get-tuple-element.63), channel_id=1, source_target_pairs={{0,2},{1,3},{2,0},{3,1},{4,6},{5,7},{6,4},{7,5},{8,10},{9,11},{10,... | collective-permute-start | bytes 1966088 | tf_op jit(solution)/shard_map/ppermute | solution.py:314
  247.7 83.3 %collective-permute-start.9 = (bf16[2,160,1024]{2,1,0:T(8,128)(2,1)}, bf16[2,160,1024]{2,1,0:T(8,128)(2,1)}, u32[]{:S(2)}, u32[]{:S(2)}) collective-permute-start(bf16[2,160,1024]{2,1,0:T(8,128)(2,1)} %get-tuple-element.64), channel_id=1, source_target_pairs={{0,3},{1,2},{2,1},{3,0},{4,7},{5,6},{6,5},{7,4},{8,11},{9,10},{10,... | collective-permute-start | bytes 1966088 | tf_op jit(solution)/shard_map/ppermute | solution.py:314
  258.0 46.8 %copy-start.34 = (f32[5,1,256]{2,1,0:T(1,128)S(1)}, f32[5,1,256]{2,1,0:T(1,128)}, u32[]{:S(2)}) copy-start(f32[5,1,256]{2,1,0:T(1,128)} %get-tuple-element.48.refs_0_) | copy-start | bytes 15364
  260.2 73.4 %collective-permute-start.4 = (bf16[2,32,1024]{2,1,0:T(8,128)(2,1)}, bf16[2,32,1024]{2,1,0:T(8,128)(2,1)}, u32[]{:S(2)}, u32[]{:S(2)}) collective-permute-start(bf16[2,32,1024]{2,1,0:T(8,128)(2,1)} %get-tuple-element.59), channel_id=1, source_target_pairs={{0,1},{1,0},{2,3},{3,2},{4,5},{5,4},{6,7},{7,6},{8,9},{9,8},{10,11... | collective-permute-start | bytes 393224 | tf_op jit(solution)/shard_map/ppermute | solution.py:314
  275.6 59.0 %collective-permute-start.5 = (bf16[2,32,1024]{2,1,0:T(8,128)(2,1)}, bf16[2,32,1024]{2,1,0:T(8,128)(2,1)}, u32[]{:S(2)}, u32[]{:S(2)}) collective-permute-start(bf16[2,32,1024]{2,1,0:T(8,128)(2,1)} %get-tuple-element.60), channel_id=1, source_target_pairs={{0,2},{1,3},{2,0},{3,1},{4,6},{5,7},{6,4},{7,5},{8,10},{9,11},{10,... | collective-permute-start | bytes 393224 | tf_op jit(solution)/shard_map/ppermute | solution.py:314
  302.9 33.7 %collective-permute-start.6 = (bf16[2,32,1024]{2,1,0:T(8,128)(2,1)}, bf16[2,32,1024]{2,1,0:T(8,128)(2,1)}, u32[]{:S(2)}, u32[]{:S(2)}) collective-permute-start(bf16[2,32,1024]{2,1,0:T(8,128)(2,1)} %get-tuple-element.61), channel_id=1, source_target_pairs={{0,3},{1,2},{2,1},{3,0},{4,7},{5,6},{6,5},{7,4},{8,11},{9,10},{10,... | collective-permute-start | bytes 393224 | tf_op jit(solution)/shard_map/ppermute | solution.py:314
  310.0 2.0 copy-start.25
  310.0 2.0 copy-start.27
  310.0 2.0 copy-start.29
  313.6 1.9 copy-start.13
  313.6 2.0 copy-start.15
  313.6 2.0 copy-start.17
  315.6 2.0 copy-start.3
  315.6 2.0 copy-start.5
  315.6 2.7 copy-start.7
  318.3 2.6 copy-start.1
  323.1 7.9 %copy-start.19 = (bf16[2,160,1024]{2,1,0:T(8,128)(2,1)S(1)}, bf16[2,160,1024]{2,1,0:T(8,128)(2,1)}, u32[]{:S(2)}) copy-start(bf16[2,160,1024]{2,1,0:T(8,128)(2,1)} %copy-done.18) | copy-start | bytes 1966084
  (20 other events, 19.9 us)

commit v4 on v3

--- a/solution.py
+++ b/solution.py
@@ -12,7 +12,7 @@
 MIB = 1024 * 1024
 ANY = pl.BlockSpec(memory_space=pl.ANY)
 VMEM = pl.BlockSpec(memory_space=pltpu.VMEM)
-STAGES = ((1, 3, 5), (10, 15), (24, 34, 44, 49, 50))
+STAGES = ((1, 5, 10, 15), (24, 34, 44, 49, 50))
 
 
 def block_rows(quota, count):
@@ -56,17 +56,18 @@
                 put(d, e, cut, (x[e, j, :, cut] * inverse).astype(jnp.bfloat16))
 
 
-def head(n, rows, x_ref, weight_ref, gain_ref, *refs):
-    sent, (own_ref, scale_ref, strip) = refs[:n - 1], refs[n - 1:n + 2]
-    (xbuf, acc, mine, peers, weight, gain, load_sem, small_sem, sum_send, sum_recv, strip_send,
-     strip_recv) = refs[n + 2:]
+def head(n, rows, split, end, x_ref, weight_ref, gain_ref, *refs):
+    sent, got = (None,) + refs[:n - 1], (None,) + refs[n - 1:2 * n - 2]
+    own_ref, early_ref, scale_ref, strip = refs[2 * n - 2:2 * n + 2]
+    (xbuf, nbuf, acc, mine, peers, weight, gain, load_sem, small_sem, store_sem, sum_send, sum_recv, strip_send,
+     strip_recv, first_send, first_recv, early_send, early_recv) = refs[2 * n + 2:]
     me = lax.axis_index("rows")
-    blocks, width = xbuf.shape[0], xbuf.shape[-1]
+    known, width = xbuf.shape[0], xbuf.shape[-1]
 
     def load(b):
         return pltpu.make_async_copy(x_ref.at[:, :, pl.ds(b * rows, rows)], xbuf.at[b], load_sem.at[b])
 
-    for b in range(blocks):
+    for b in range(end):
         load(b).start()
     smalls = [pltpu.make_async_copy(weight_ref, weight, small_sem.at[0]),
               pltpu.make_async_copy(gain_ref, gain, small_sem.at[1])]
@@ -87,13 +88,58 @@
             remote(mine.at[pl.ds(lo, hi - lo)], peers.at[d - 1, pl.ds(lo, hi - lo)],
                    sum_send.at[turn, d - 1], sum_recv.at[turn, d - 1], d)
             for d in range(1, n)
-        ]
-
-    load(0).wait()
-    mine[0] = add_block(xbuf.at[0], acc, rows)
+        ] if hi > lo else []
+
+    def some(b):
+        at = b * rows
+        return pl.ds(at if isinstance(b, int) else pl.multiple_of(at, rows), rows)
+
+    def first(d):
+        return remote(nbuf.at[d, :, some(0)], got[d], first_send.at[d - 1], first_recv.at[d - 1], d)
+
+    def early(b):
+        return remote(nbuf.at[2, :, some(b)], early_ref.at[:, some(b - 1)], early_send.at[b - 1],
+                      early_recv.at[b - 1], 2)
+
+    def store(d, b):
+        return pltpu.make_async_copy(nbuf.at[d, :, some(b)], sent[d].at[:, some(b - 1)], store_sem.at[d, b])
+
+    def add(b, carry):
+        load(b).wait()
+        mine[b] = add_block(xbuf.at[b], acc, rows)
+        return carry
+
+    def average(lo, hi):
+        if hi > lo:
+            total = mine[lo:hi]
+            for d in range(1, n):
+                total = total + peers[d - 1, lo:hi]
+            scale_ref[lo:hi] = total / (n * width)
+
+    def scale(b):
+        def put(d, e, cut, value):
+            nbuf[d, e, some(b), cut] = value
+
+        scale_block(xbuf.at[b], scale_ref[b], acc, put, me, n, rows)
+
+    add(0, 0)
+    for b in range(end, known):
+        load(b).start()
     pl.semaphore_wait(barrier, n - 1)
-    turns = [sums(0, 0, 1)] + ([sums(1, 1, blocks)] if blocks > 1 else [])
+    turns = [sums(0, 0, 1), sums(1, 1, end), sums(2, end, known)]
     for copy in turns[0]:
+        copy.start()
+    lax.fori_loop(1, end, add, 0)
+    for copy in turns[1]:
+        copy.start()
+    for copy in turns[0]:
+        copy.wait()
+    average(0, 1)
+    scale(0)
+    for d in reversed(range(1, n)):
+        first(d).start()
+    lax.fori_loop(end, known, add, 0)
+    for copy in turns[2]:
         copy.start()
     for copy in smalls:
         copy.wait()
@@ -102,35 +148,46 @@
               for d in range(1, n)]
     for copy in strips:
         copy.start()
-    for b in range(1, blocks):
-        load(b).wait()
-        mine[b] = add_block(xbuf.at[b], acc, rows)
-    for turn in turns[1:]:
-        for copy in turn:
-            copy.start()
-    for copy in turns[0]:
+    for copy in turns[1]:
         copy.wait()
-
-    def average(b):
-        total = mine[b]
+    average(1, end)
+
+    def step(b, carry):
+        scale(b)
         for d in range(1, n):
-            total = total + peers[d - 1, b]
-        scale_ref[b] = total / (n * width)
-
-    average(0)
-
-    def put(d, e, cut, value):
-        ref = sent[d - 1] if d else own_ref
-        ref[e, :, cut] = value
-
-    scale_block(xbuf.at[0], scale_ref[0], acc, put, me, n, rows)
-    for turn in turns[1:]:
-        for copy in turn:
-            copy.wait()
-    for b in range(1, blocks):
-        average(b)
+            store(d, b).start()
+        if split:
+            @pl.when(lax.rem(me, 2) == 0)
+            def _():
+                early(b).start()
+        return carry
+
+    lax.fori_loop(1, end, step, 0)
+    own = pltpu.make_async_copy(nbuf.at[0], own_ref, store_sem.at[0, 0])
+    own.start()
+    for copy in turns[2]:
+        copy.wait()
+    average(end, known)
     for copy in strips:
         copy.wait()
+
+    def finish(b, carry):
+        for d in range(1, n):
+            store(d, b).wait()
+        return carry
+
+    lax.fori_loop(1, end, finish, 0)
+    own.wait()
+    for d in range(1, n):
+        first(d).wait()
+    if split:
+        @pl.when(lax.rem(me, 2) == 0)
+        def _():
+            def arrive(b, carry):
+                early(b).wait()
+                return carry
+
+            lax.fori_loop(1, end, arrive, 0)
 
 
 def add_up(rows, *refs):
@@ -211,26 +268,43 @@
     scale_block(x_ref, scale, acc, put, me, n, rows)
 
 
-def place(n, spots, *refs):
+def place(n, spots, final, *refs):
     count = len(spots)
-    got, out_ref, bufs = refs[:count], refs[-3 - count], refs[-2 - count:-2]
+    got = refs[:count]
+    out_ref, bufs = (refs[-3], got) if final else (refs[-3 - count], refs[-2 - count:-2])
     load_sem, store_sem = refs[-2:]
     me = lax.axis_index("rows")
-    loads = [pltpu.make_async_copy(got[k], bufs[k], load_sem.at[k]) for k in range(count)]
-    for copy in loads:
-        copy.start()
-    stores = []
-    for k, (lo, d) in enumerate(spots):
+
+    def load(k):
+        return pltpu.make_async_copy(got[k], bufs[k], load_sem.at[k])
+
+    def store(k):
+        lo, d, _ = spots[k]
         _, height, width = got[k].shape
         column = source(me, d, n) if d else me
-        loads[k].wait()
-        stores.append(pltpu.make_async_copy(
+        return pltpu.make_async_copy(
             bufs[k],
             out_ref.at[:, pl.ds(lo, height), pl.ds(pl.multiple_of(column * width, width), width)],
-            store_sem.at[k]))
-        stores[-1].start()
-    for copy in stores:
-        copy.wait()
+            store_sem.at[k])
+
+    def here(k, act):
+        core = spots[k][2]
+        if core is None:
+            act()
+        else:
+            pl.when(lax.rem(me, 2) == core)(act)
+
+    def turn(k):
+        if not final:
+            load(k).wait()
+        store(k).start()
+
+    for k in range(0 if final else count):
+        here(k, lambda: load(k).start())
+    for k in range(count):
+        here(k, lambda: turn(k))
+    for k in range(count):
+        here(k, lambda: store(k).wait())
 
 
 def gather(owners, strip_ref, router_ref, send_sem, recv_sem):
@@ -281,16 +355,24 @@
     known = stages[0][-1][1]
     hbm = pl.BlockSpec(memory_space=pltpu.HBM)
 
+    end = stages[0][1][1]
+    split = n > 2 and n & (n - 1) == 0
+    second = ((end - 1) * rows, width)
+
     outs = pl.pallas_call(
-        functools.partial(head, n, rows),
-        out_shape=[pltpu.VMEM((experts, rows, width), bf16)] * n + [
+        functools.partial(head, n, rows, split, end),
+        out_shape=[pltpu.HBM((experts, *second), bf16)] * (n - 1) + [
+            pltpu.HBM((experts, rows, width), bf16)] * (n - 1) + [
+            pltpu.HBM((experts, end * rows, width), bf16),
+            pltpu.HBM((experts, *(second if split else (16, LANES))), bf16),
             jax.ShapeDtypeStruct((known, 1, wide), f32),
             jax.ShapeDtypeStruct((n, mine_e, depth), bf16),
         ],
         in_specs=[hbm, hbm, hbm],
-        out_specs=[VMEM] * (n + 2),
+        out_specs=[ANY] * (2 * n) + [VMEM] * 2,
         scratch_shapes=[
             pltpu.VMEM((known, experts, n, rows, width), f32),
+            pltpu.VMEM((n, experts, end * rows, width), bf16),
             pltpu.VMEM((wide, LANES), f32),
             pltpu.VMEM((known, 1, wide), f32),
             pltpu.VMEM((n - 1, known, 1, wide), f32),
@@ -298,23 +380,28 @@
             pltpu.VMEM((1, depth), f32),
             pltpu.SemaphoreType.DMA((known,)),
             pltpu.SemaphoreType.DMA((2,)),
-            pltpu.SemaphoreType.DMA((2, n - 1)),
-            pltpu.SemaphoreType.DMA((2, n - 1)),
+            pltpu.SemaphoreType.DMA((n, end)),
+            pltpu.SemaphoreType.DMA((3, n - 1)),
+            pltpu.SemaphoreType.DMA((3, n - 1)),
             pltpu.SemaphoreType.DMA((n - 1,)),
             pltpu.SemaphoreType.DMA((n - 1,)),
+            pltpu.SemaphoreType.DMA((n - 1,)),
+            pltpu.SemaphoreType.DMA((n - 1,)),
+            pltpu.SemaphoreType.DMA((end,)),
+            pltpu.SemaphoreType.DMA((end,)),
         ],
         compiler_params=pltpu.CompilerParams(
             collective_id=0, has_side_effects=True, vmem_limit_bytes=62 * MIB),
         name="head",
     )(x, router_weight.T, router_gain[None, :])
-    own, scale, strip = outs[n - 1:]
+    own, early, scale, strip = outs[2 * n - 2:]
     scales, parts, after = [scale], [scale], scale
 
     def move(array, d):
         return lax.ppermute(array, "rows", pairs(d, n))
 
-    def permute(arrays):
-        return [move(arrays[d - 1], d) for d in range(1, n)]
+    def permute(arrays, skip=None):
+        return [move(arrays[d - 1], d) for d in range(1, n) if d != skip]
 
     def sums(lo, hi, after):
         step = max(k for k in (4, 3, 2, 1) if (hi - lo) % k == 0)
@@ -389,14 +476,14 @@
         )(x, *parts, *held)
         return made[:n - 1], made[n - 1], made[n]
 
-    def placed(spots, got, out):
+    def placed(spots, got, out, final):
         count = len(got)
         return pl.pallas_call(
-            functools.partial(place, n, spots),
+            functools.partial(place, n, spots, final),
             out_shape=jax.ShapeDtypeStruct((experts, quota, n * width), bf16),
-            in_specs=[ANY] * (count + 1),
+            in_specs=[VMEM if final else ANY] * count + [ANY],
             out_specs=ANY,
-            scratch_shapes=[pltpu.VMEM(a.shape, bf16) for a in got] + [
+            scratch_shapes=[pltpu.VMEM(a.shape, bf16) for a in got if not final] + [
                 pltpu.SemaphoreType.DMA((count,)),
                 pltpu.SemaphoreType.DMA((count,)),
             ],
@@ -404,48 +491,62 @@
             compiler_params=pltpu.CompilerParams(vmem_limit_bytes=24 * MIB),
         )(*got, out)
 
-    out, got, p, base = None, [], 0, 0
-    sent = list(outs[:n - 1])
+    def finish_small():
+        strips = pl.pallas_call(
+            functools.partial(gather, owners),
+            out_shape=jax.ShapeDtypeStruct((owners, n, mine_e, depth), bf16),
+            in_specs=[VMEM],
+            out_specs=VMEM,
+            scratch_shapes=[pltpu.SemaphoreType.DMA((owners - 1,)), pltpu.SemaphoreType.DMA((owners - 1,))],
+            compiler_params=pltpu.CompilerParams(
+                collective_id=1, has_side_effects=True, vmem_limit_bytes=4 * MIB),
+            name="router",
+        )(strip)
+        serve_router = strips.transpose(0, 2, 1, 3).reshape(owners * mine_e, n * depth).T
+        held = jnp.concatenate(scales, axis=0).reshape(blocks, experts, n, rows)
+        scale_down = lax.dynamic_index_in_dim(held, lax.axis_index("rows"), axis=2, keepdims=False)
+        scale_down = scale_down.transpose(1, 0, 2).reshape(experts, quota)
+        return scale_down, serve_router
+
+    small = None
+    last = sum(len(stage) for stage in stages) - 1
+    out, got, p, base = None, [list(outs[n - 1:2 * n - 2])], 0, 0
     for s, stage in enumerate(stages):
         for k, (lo, hi) in enumerate(stage):
-            if p:
+            if p == last and len(parts) == 1:
+                small = finish_small()
+                parts[0], *small = lax.optimization_barrier((parts[0], *small))
+            if p == 1:
+                sent = outs[:n - 1]
+                if split:
+                    odd = lax.ppermute(sent[1], "rows", [pair for pair in pairs(2, n) if pair[0] % 2])
+            if p > 1:
                 sent, out, after = scaled(lo, hi, base, parts, out, 16 if s else 62)
                 if len(parts) > 1:
                     scales.append(after)
             if k + 1 == len(stage) and s + 1 < len(stages):
-                base, end = hi, stages[s + 1][-1][1]
+                base, stop = hi, stages[s + 1][-1][1]
                 if in_pairs(s, len(stages), n, wide):
-                    finish = sums_pair(base, end, after)
+                    finish = sums_pair(base, stop, after)
                 else:
-                    mine = sums(base, end, after)
+                    mine = sums(base, stop, after)
                     parts = [mine] + permute([mine] * (n - 1))
-            got.append(permute(sent))
+            if p:
+                got.append(permute(sent, 2 if p == 1 and split else None))
             p += 1
         if in_pairs(s, len(stages), n, wide):
             parts = [finish()]
             scales.append(parts[0])
 
-    strips = pl.pallas_call(
-        functools.partial(gather, owners),
-        out_shape=jax.ShapeDtypeStruct((owners, n, mine_e, depth), bf16),
-        in_specs=[VMEM],
-        out_specs=VMEM,
-        scratch_shapes=[pltpu.SemaphoreType.DMA((owners - 1,)), pltpu.SemaphoreType.DMA((owners - 1,))],
-        compiler_params=pltpu.CompilerParams(
-            collective_id=1, has_side_effects=True, vmem_limit_bytes=4 * MIB),
-        name="router",
-    )(strip)
-    serve_router = strips.transpose(0, 2, 1, 3).reshape(owners * mine_e, n * depth).T
-    held = jnp.concatenate(scales, axis=0).reshape(blocks, experts, n, rows)
-    scale_down = lax.dynamic_index_in_dim(held, lax.axis_index("rows"), axis=2, keepdims=False)
-    scale_down = scale_down.transpose(1, 0, 2).reshape(experts, quota)
-
     for p, (lo, _) in enumerate(piece for stage in stages for piece in stage):
-        spots, arrays = [(lo * rows, d) for d in range(1, n)], got[p]
+        spots, arrays = [(lo * rows, d, None) for d in range(1, n)], got[p]
         if p == 0:
-            spots, arrays = spots + [(0, 0)], arrays + [own]
-        out = placed(tuple(spots), arrays, out)
-    return out, scale_down, serve_router
+            spots, arrays = spots + [(0, 0, None)], arrays + [own]
+        if p == 1 and split:
+            spots = [spot for spot in spots if spot[1] != 2] + [(lo * rows, 2, 0), (lo * rows, 2, 1)]
+            arrays = arrays + [early, odd]
+        out = placed(tuple(spots), arrays, out, p == last)
+    return out, *(small or finish_small())
 
 
 def solution(mesh):

time: 341 us -> 325 us (0.953)
  Pallas kernels: 113 us -> 107 us
  starting transfers between devices: 28.8 us -> 24.3 us
    ppermute x34 -> x24, waiting for transfers between devices: 177 us -> 166 us  [move(): return lax.ppermute(array, 'rows', pairs(d, n))]
    ppermute x0 -> x1, waiting for transfers between devices: none -> 10 us  [per_device(): lax.ppermute(sent[1], 'rows', [pair for pair in pairs(2, n) if pair[0] % 2])]
    ppermute x34 -> x24, starting transfers between devices: 28.8 us -> 21.4 us  [move(): return lax.ppermute(array, 'rows', pairs(d, n))]
    pallas_call x9 -> x7, Pallas kernels: 54.4 us -> 50 us  [scaled(): pl.pallas_call(functools.partial(narrow, n, rows, (len(held), len(parts))...]
    pallas_call x13 -> x11, Pallas kernels: 42.4 us -> 40.3 us  [the longest x9 18.6 us: placed(): pl.pallas_call(functools.partial(place, n, spots, final), out_shape=jax.S...]
    unnamed x101 -> x91, local copies, waits for them, and re-layouts: 15.4 us -> 13.5 us
  transfers between devices with their start and end apart: 34 -> 25, of which waited for: 18 -> 13; matrix products, arithmetic and copies ran while one was open for 1% -> 1% of each run, Pallas kernels for 31% -> 27%
where the time goes in v4:
time: 325 us; the launch traced here: 323 us
  waiting for transfers between devices  176 us (54%)
  Pallas kernels  107 us (33%)
  starting transfers between devices  24.3 us (7%)
  local copies, waits for them, and re-layouts  14.5 us (4%)
    ppermute x24, waiting for transfers between devices, move(): return lax.ppermute(array, 'rows', pairs(d, n))  166 us
    pallas_call x7, Pallas kernels, scaled(): pl.pallas_call(functools.partial(narrow, n, rows, (len(held), len(parts))...  50 us
    ppermute x24, starting transfers between devices, move(): return lax.ppermute(array, 'rows', pairs(d, n))  21.4 us
    pallas_call x9, Pallas kernels, placed(): pl.pallas_call(functools.partial(place, n, spots, final), out_shape=jax.S...  18.6 us
    pallas_call x1, Pallas kernels, per_device(): pl.pallas_call(functools.partial(head, n, rows, split, end), out_shape=[p...  14.9 us
    pallas_call x1, Pallas kernels, sums_pair(): pl.pallas_call(functools.partial(add_up_pair, rows, step), grid=((hi - lo...  14.8 us
    unnamed x91, local copies, waits for them, and re-layouts  13.5 us
    ppermute x1, waiting for transfers between devices, per_device(): lax.ppermute(sent[1], 'rows', [pair for pair in pairs(2, n) if pair[0] % 2])  10 us
  transfers between devices with their start and end apart: 25, of which 13 were waited for; matrix products, arithmetic and copies ran while one was open for 1% of the time, Pallas kernels for 27%

profile of v4, /device:TPU:1, one launch (start us, length us, event | category | flops | bytes accessed | tf_op | source)
XLA Modules:
  0.0 323.4 jit_solution(4734751361581175809)
XLA Ops:
  0.6 14.9 %head.1 = (bf16[2,128,1024]{2,1,0:T(8,128)(2,1)}, bf16[2,128,1024]{2,1,0:T(8,128)(2,1)}, bf16[2,128,1024]{2,1,0:T(8,128)(2,1)}, bf16[2,32,1024]{2,1,0:T(8,128)(2...) custom-call(f32[2,4,1600,1024]{3,2,1,0:T(8,128)} %bitcast.15, ...), custom_call_target="tpu_custom_call" | custom-call | tf_op jit(solution)/shard_map/head/pallas_call | solution.py:362
  15.5 5.9 %shard_map.58 = (bf16[2,160,1024]{2,1,0:T(8,128)(2,1)}, bf16[2,160,1024]{2,1,0:T(8,128)(2,1)}, bf16[2,160,1024]{2,1,0:T(8,128)(2,1)}, bf16[2,1600,4096]{2,1,0:T(8,128)(2,1)}, f32[5,1,256]{2,1,0:T(1,128)}) custom-call(f32[2,4,1600,1024]{3,2,1,0:T(8,128)} %bitcast.16, f32[15,1,256]{2,1,0:T(1,128)} %get-tuple-element.45.refs_0_), custom_call_target="tpu_custom_call" | custom-call | tf_op jit(solution)/shard_map/pallas_call | solution.py:460
  21.4 6.1 %collective-permute-start.19 = (bf16[2,160,1024]{2,1,0:T(8,128)(2,1)}, bf16[2,160,1024]{2,1,0:T(8,128)(2,1)S(1)}, u32[]{:S(2)}, u32[]{:S(2)}) collective-permute-start(bf16[2,160,1024]{2,1,0:T(8,128)(2,1)} %get-tuple-element.73), channel_id=1, source_target_pairs={{0,1},{1,0},{2,3},{3,2},{4,5},{5,4},{6,7},{7,6},{8,9},{9,8},{10,11... | collective-permute-start | bytes 1966088 | tf_op jit(solution)/shard_map/ppermute | solution.py:401
  27.6 5.9 %shard_map.59 = (bf16[2,160,1024]{2,1,0:T(8,128)(2,1)}, bf16[2,160,1024]{2,1,0:T(8,128)(2,1)}, bf16[2,160,1024]{2,1,0:T(8,128)(2,1)}, bf16[2,1600,4096]{2,1,0:T(8,128)(2,1)}, f32[5,1,256]{2,1,0:T(1,128)}) custom-call(f32[2,4,1600,1024]{3,2,1,0:T(8,128)} %bitcast.17, f32[15,1,256]{2,1,0:T(1,128)} %get-tuple-element.45.refs_0_, ...), custom_call_target="tpu_custom_call", output_to_operand_aliasing={{3}: (2, {})} | custom-call | tf_op jit(solution)/shard_map/pallas_call | solution.py:460
  33.5 0.7 copy-done.32
  34.2 14.8 %shard_map.60.half_ref = f32[35,1,128]{2,1,0:T(1,128)S(1)} custom-call(f32[2,4,1600,1024]{3,2,1,0:T(8,128)} %bitcast.18, f32[2,4,1600,1024]{3,2,1,0:T(8,128)} %bitcast.19, f32[2,4,1600,1024]{3,2,1,0:T(8,128)} %bitcast.20, f32[2,4,1600,1024]{3,2,1,0:T(8,128)} %bitcast.21, f32[2,4,1600,1024]{3,2,1,0:T(8,128)} %bitcast.22, f32[5,1,256]{2,1,0:T(1,128)S(1)} %copy-done.32), custom_call_target="tpu_custom_call" | custom-call | tf_op jit(solution)/shard_map/pallas_call | solution.py:425
  49.1 1.1 collective-permute-start
  50.2 0.7 collective-permute-start.23
  50.9 3.0 collective-permute-start.24
  53.9 0.5 collective-permute-start.20
  54.4 0.8 copy-done.22
  55.5 8.9 %collective-permute-done.23.refs_1_ = bf16[2,128,1024]{2,1,0:T(8,128)(2,1)S(1)} collective-permute-done((bf16[2,128,1024]{2,1,0:T(8,128)(2,1)S(1)}, bf16[2,128,1024]{2,1,0:T(8,128)(2,1)S(1)}, u32[]{:S(2)}, u32[]{:S(2)}) %collective-permute-start.23) | collective-permute-done | bytes 524320 | tf_op jit(solution)/shard_map/ppermute | solution.py:401
  64.4 0.8 copy-done.24
  65.5 10.0 %collective-permute-done.24.refs_3_ = bf16[2,128,1024]{2,1,0:T(8,128)(2,1)S(1)} collective-permute-done((bf16[2,128,1024]{2,1,0:T(8,128)(2,1)S(1)}, bf16[2,128,1024]{2,1,0:T(8,128)(2,1)S(1)}, u32[]{:S(2)}, u32[]{:S(2)}) %collective-permute-start.24) | collective-permute-done | bytes 524320 | tf_op jit(solution)/shard_map/ppermute | solution.py:522
  75.5 0.8 copy-done.26
  76.3 0.6 collective-permute-start.17
  76.9 2.2 shard_map.61.refs_0_
  79.0 9.4 %shard_map.62 = (bf16[2,288,1024]{2,1,0:T(8,128)(2,1)}, bf16[2,288,1024]{2,1,0:T(8,128)(2,1)}, bf16[2,288,1024]{2,1,0:T(8,128)(2,1)}, bf16[2,1600,4096]{2,1,0:T(8,128)(2,1)}, f32[9,1,256]{2,1,0:T(1,128)}) custom-call(f32[2,4,1600,1024]{3,2,1,0:T(8,128)} %bitcast.23, f32[35,1,256]{2,1,0:T(1,128)S(1)} %shard_map.61.refs_0_, ...), custom_call_target="tpu_custom_call", output_to_operand_aliasing={{3}: (2, {})} | custom-call | tf_op jit(solution)/shard_map/pallas_call | solution.py:460
  88.4 0.8 collective-permute-done.20.refs_1_
  89.2 10.2 %shard_map.63 = (bf16[2,320,1024]{2,1,0:T(8,128)(2,1)}, bf16[2,320,1024]{2,1,0:T(8,128)(2,1)}, bf16[2,320,1024]{2,1,0:T(8,128)(2,1)}, bf16[2,1600,4096]{2,1,0:T(8,128)(2,1)}, f32[10,1,256]{2,1,0:T(1,128)}) custom-call(f32[2,4,1600,1024]{3,2,1,0:T(8,128)} %bitcast.24, f32[35,1,256]{2,1,0:T(1,128)S(1)} %shard_map.61.refs_0_, ...), custom_call_target="tpu_custom_call", output_to_operand_aliasing={{3}: (2, {})} | custom-call | tf_op jit(solution)/shard_map/pallas_call | solution.py:460
  99.4 2.5 collective-permute-done.21.refs_2_
  101.9 0.8 copy-done.11
  102.8 2.0 collective-permute-start.10
  104.8 9.9 %shard_map.64 = (bf16[2,320,1024]{2,1,0:T(8,128)(2,1)}, bf16[2,320,1024]{2,1,0:T(8,128)(2,1)}, bf16[2,320,1024]{2,1,0:T(8,128)(2,1)}, bf16[2,1600,4096]{2,1,0:T(8,128)(2,1)}, f32[10,1,256]{2,1,0:T(1,128)}) custom-call(f32[2,4,1600,1024]{3,2,1,0:T(8,128)} %bitcast.25, f32[35,1,256]{2,1,0:T(1,128)S(1)} %shard_map.61.refs_0_, ...), custom_call_target="tpu_custom_call", output_to_operand_aliasing={{3}: (2, {})} | custom-call | tf_op jit(solution)/shard_map/pallas_call | solution.py:460
  114.8 6.5 %shard_map.65 = (bf16[2,160,1024]{2,1,0:T(8,128)(2,1)}, bf16[2,160,1024]{2,1,0:T(8,128)(2,1)}, bf16[2,160,1024]{2,1,0:T(8,128)(2,1)}, bf16[2,1600,4096]{2,1,0:T(8,128)(2,1)}, f32[5,1,256]{2,1,0:T(1,128)}) custom-call(f32[2,4,1600,1024]{3,2,1,0:T(8,128)} %bitcast.26, f32[35,1,256]{2,1,0:T(1,128)S(1)} %shard_map.61.refs_0_, ...), custom_call_target="tpu_custom_call", output_to_operand_aliasing={{3}: (2, {})} | custom-call | tf_op jit(solution)/shard_map/pallas_call | solution.py:460
  121.3 0.9 copy-done.13
  122.2 0.8 copy-done.15
  123.1 0.6 collective-permute-start.14
  123.6 0.9 collective-permute-done.18.refs_2_
  124.6 0.8 copy-done.17
  125.4 2.5 collective-permute-start.15
  127.9 0.9 copy-done.19
  128.8 1.0 collective-permute-start.11
  129.7 1.0 copy-done.2
  131.0 20.1 %collective-permute-done.14.refs_1_ = bf16[2,288,1024]{2,1,0:T(8,128)(2,1)S(1)} collective-permute-done((bf16[2,288,1024]{2,1,0:T(8,128)(2,1)S(1)}, bf16[2,288,1024]{2,1,0:T(8,128)(2,1)S(1)}, u32[]{:S(2)}, u32[]{:S(2)}) %collective-permute-start.14) | collective-permute-done | bytes 1179680 | tf_op jit(solution)/shard_map/ppermute | solution.py:401
  151.1 1.0 copy-done.4
  152.1 1.3 collective-permute-start.7
  153.4 23.5 %collective-permute-done.15.refs_2_ = bf16[2,288,1024]{2,1,0:T(8,128)(2,1)S(1)} collective-permute-done((bf16[2,288,1024]{2,1,0:T(8,128)(2,1)S(1)}, bf16[2,288,1024]{2,1,0:T(8,128)(2,1)S(1)}, u32[]{:S(2)}, u32[]{:S(2)}) %collective-permute-start.15) | collective-permute-done | bytes 1179680 | tf_op jit(solution)/shard_map/ppermute | solution.py:401
  177.0 1.1 copy-done.6
  178.1 0.6 collective-permute-start.8
  178.7 0.8 collective-permute-start.9
  179.5 25.0 %collective-permute-done.11.refs_1_ = bf16[2,320,1024]{2,1,0:T(8,128)(2,1)S(1)} collective-permute-done((bf16[2,320,1024]{2,1,0:T(8,128)(2,1)S(1)}, bf16[2,320,1024]{2,1,0:T(8,128)(2,1)S(1)}, u32[]{:S(2)}, u32[]{:S(2)}) %collective-permute-start.11) | collective-permute-done | bytes 1310752 | tf_op jit(solution)/shard_map/ppermute | solution.py:401
  204.9 28.3 %collective-permute-done.12.refs_2_ = bf16[2,320,1024]{2,1,0:T(8,128)(2,1)S(1)} collective-permute-done((bf16[2,320,1024]{2,1,0:T(8,128)(2,1)S(1)}, bf16[2,320,1024]{2,1,0:T(8,128)(2,1)S(1)}, u32[]{:S(2)}, u32[]{:S(2)}) %collective-permute-start.12) | collective-permute-done | bytes 1310752 | tf_op jit(solution)/shard_map/ppermute | solution.py:401
  233.2 1.1 copy-done
  234.3 6.8 %router.1 = bf16[8,4,2,1024]{3,2,1,0:T(2,128)(2,1)S(1)} custom-call(bf16[4,2,1024]{2,1,0:T(2,128)(2,1)S(1)} %copy-done.31), custom_call_target="tpu_custom_call" | custom-call | tf_op jit(solution)/shard_map/router/pallas_call | solution.py:495
  241.2 0.7 copy.24
  242.1 0.7 reshape.20
  242.8 2.3 shard_map.66
  245.1 1.8 collective-permute-start.1
  246.9 13.8 %collective-permute-done.8.refs_1_ = bf16[2,320,1024]{2,1,0:T(8,128)(2,1)} collective-permute-done((bf16[2,320,1024]{2,1,0:T(8,128)(2,1)}, bf16[2,320,1024]{2,1,0:T(8,128)(2,1)}, u32[]{:S(2)}, u32[]{:S(2)}) %collective-permute-start.8) | collective-permute-done | bytes 1310752 | tf_op jit(solution)/shard_map/ppermute | solution.py:401
  261.1 28.3 %collective-permute-done.9.refs_2_ = bf16[2,320,1024]{2,1,0:T(8,128)(2,1)} collective-permute-done((bf16[2,320,1024]{2,1,0:T(8,128)(2,1)}, bf16[2,320,1024]{2,1,0:T(8,128)(2,1)}, u32[]{:S(2)}, u32[]{:S(2)}) %collective-permute-start.9) | collective-permute-done | bytes 1310752 | tf_op jit(solution)/shard_map/ppermute | solution.py:401
  289.6 1.8 shard_map.67.refs_4_
  291.4 1.3 shard_map.68.refs_3_
  292.7 0.5 copy-done.12
  293.2 1.9 shard_map.69.refs_3_
  295.2 1.9 shard_map.70.refs_3_
  297.2 0.7 copy-done.7
  297.9 2.6 shard_map.71.refs_3_
  300.5 2.3 shard_map.72.refs_3_
  302.7 3.4 %shard_map.73.refs_3_ = bf16[2,1600,4096]{2,1,0:T(8,128)(2,1)} custom-call(bf16[2,320,1024]{2,1,0:T(8,128)(2,1)} %collective-permute-done.7.refs_0_, bf16[2,320,1024]{2,1,0:T(8,128)(2,1)} %collective-permute-done.8.refs_1_, bf16[2,320,1024]{2,1,0:T(8,128)(2,1)} %collective-permute-done.9.refs_2_, ...), custom_call_target="tpu_custom_call", output_to_operand_aliasing={{}: (3, {})} | custom-call | tf_op jit(solution)/shard_map/pallas_call | solution.py:481
  306.1 11.4 %collective-permute-done.6.refs_2_ = bf16[2,160,1024]{2,1,0:T(8,128)(2,1)} collective-permute-done((bf16[2,160,1024]{2,1,0:T(8,128)(2,1)}, bf16[2,160,1024]{2,1,0:T(8,128)(2,1)}, u32[]{:S(2)}, u32[]{:S(2)}) %collective-permute-start.6) | collective-permute-done | bytes 655392 | tf_op jit(solution)/shard_map/ppermute | solution.py:401
  317.5 2.6 shard_map.74.refs_3_
  320.2 2.4 collective-permute-done.3.refs_2_
  322.6 0.8 shard_map.75
  (103 shorter events, 2.2 us)
Async XLA Ops:
  21.4 55.4 %collective-permute-start.19 = (bf16[2,160,1024]{2,1,0:T(8,128)(2,1)}, bf16[2,160,1024]{2,1,0:T(8,128)(2,1)S(1)}, u32[]{:S(2)}, u32[]{:S(2)}) collective-permute-start(bf16[2,160,1024]{2,1,0:T(8,128)(2,1)} %get-tuple-element.73), channel_id=1, source_target_pairs={{0,1},{1,0},{2,3},{3,2},{4,5},{5,4},{6,7},{7,6},{8,9},{9,8},{10,11... | collective-permute-start | bytes 1966088 | tf_op jit(solution)/shard_map/ppermute | solution.py:401
  27.5 26.8 %collective-permute-start.22 = (bf16[2,128,1024]{2,1,0:T(8,128)(2,1)}, bf16[2,128,1024]{2,1,0:T(8,128)(2,1)S(1)}, u32[]{:S(2)}, u32[]{:S(2)}) collective-permute-start(bf16[2,128,1024]{2,1,0:T(8,128)(2,1)} %get-tuple-element.76), channel_id=1, source_target_pairs={{0,1},{1,0},{2,3},{3,2},{4,5},{5,4},{6,7},{7,6},{8,9},{9,8},{10,11... | collective-permute-start | bytes 1572872 | tf_op jit(solution)/shard_map/ppermute | solution.py:401
  34.2 16.0 %copy-start.44 = (bf16[2,128,1024]{2,1,0:T(8,128)(2,1)S(1)}, bf16[2,128,1024]{2,1,0:T(8,128)(2,1)}, u32[]{:S(2)}) copy-start(bf16[2,128,1024]{2,1,0:T(8,128)(2,1)} %get-tuple-element.77) | copy-start | bytes 1572868
  34.2 16.7 %copy-start.43 = (bf16[2,128,1024]{2,1,0:T(8,128)(2,1)S(1)}, bf16[2,128,1024]{2,1,0:T(8,128)(2,1)}, u32[]{:S(2)}) copy-start(bf16[2,128,1024]{2,1,0:T(8,128)(2,1)} %get-tuple-element.79) | copy-start | bytes 1572868
  34.2 19.7 %copy-start.42 = (bf16[2,160,1024]{2,1,0:T(8,128)(2,1)S(1)}, bf16[2,160,1024]{2,1,0:T(8,128)(2,1)}, u32[]{:S(2)}) copy-start(bf16[2,160,1024]{2,1,0:T(8,128)(2,1)} %get-tuple-element.74) | copy-start | bytes 1966084
  34.2 21.0 %copy-start.41 = (bf16[2,160,1024]{2,1,0:T(8,128)(2,1)S(1)}, bf16[2,160,1024]{2,1,0:T(8,128)(2,1)}, u32[]{:S(2)}) copy-start(bf16[2,160,1024]{2,1,0:T(8,128)(2,1)} %get-tuple-element.75) | copy-start | bytes 1966084
  34.2 31.1 %copy-start.40 = (bf16[2,160,1024]{2,1,0:T(8,128)(2,1)S(1)}, bf16[2,160,1024]{2,1,0:T(8,128)(2,1)}, u32[]{:S(2)}) copy-start(bf16[2,160,1024]{2,1,0:T(8,128)(2,1)} %get-tuple-element.70) | copy-start | bytes 1966084
  34.2 42.1 %copy-start.39 = (bf16[2,160,1024]{2,1,0:T(8,128)(2,1)S(1)}, bf16[2,160,1024]{2,1,0:T(8,128)(2,1)}, u32[]{:S(2)}) copy-start(bf16[2,160,1024]{2,1,0:T(8,128)(2,1)} %get-tuple-element.71) | copy-start | bytes 1966084
  34.2 42.7 %copy-start.38 = (bf16[2,160,1024]{2,1,0:T(8,128)(2,1)S(1)}, bf16[2,160,1024]{2,1,0:T(8,128)(2,1)}, u32[]{:S(2)}) copy-start(bf16[2,160,1024]{2,1,0:T(8,128)(2,1)} %get-tuple-element.72) | copy-start | bytes 1966084
  49.1 4.9 %collective-permute-start = (f32[35,1,128]{2,1,0:T(1,128)S(1)}, f32[35,1,128]{2,1,0:T(1,128)S(1)}, u32[]{:S(2)}, u32[]{:S(2)}) collective-permute-start(f32[35,1,128]{2,1,0:T(1,128)S(1)} %shard_map.60.half_ref), channel_id=1, source_target_pairs={{0,2},{1,3},{2,0},{3,1},{4,6},{5,7},{6,4},{7,5},{8,10},{9,11},{10,... | collective-permute-start | bytes 53768 | tf_op jit(solution)/shard_map/ppermute | solution.py:401
  50.2 14.2 %collective-permute-start.23 = (bf16[2,128,1024]{2,1,0:T(8,128)(2,1)S(1)}, bf16[2,128,1024]{2,1,0:T(8,128)(2,1)S(1)}, u32[]{:S(2)}, u32[]{:S(2)}) collective-permute-start(bf16[2,128,1024]{2,1,0:T(8,128)(2,1)S(1)} %copy-done.44), channel_id=1, source_target_pairs={{0,3},{1,2},{2,1},{3,0},{4,7},{5,6},{6,5},{7,4},{8,11},{9,10},{10,... | collective-permute-start | bytes 1572872 | tf_op jit(solution)/shard_map/ppermute | solution.py:401
  50.9 24.6 %collective-permute-start.24 = (bf16[2,128,1024]{2,1,0:T(8,128)(2,1)S(1)}, bf16[2,128,1024]{2,1,0:T(8,128)(2,1)S(1)}, u32[]{:S(2)}, u32[]{:S(2)}) collective-permute-start(bf16[2,128,1024]{2,1,0:T(8,128)(2,1)S(1)} %copy-done.43), channel_id=1, source_target_pairs={{1,3},{3,1},{5,7},{7,5},{9,11},{11,9},{13,15},{15,13},{17,19},{19,... | collective-permute-start | bytes 1572872 | tf_op jit(solution)/shard_map/ppermute | solution.py:522
  53.9 35.3 %collective-permute-start.20 = (bf16[2,160,1024]{2,1,0:T(8,128)(2,1)S(1)}, bf16[2,160,1024]{2,1,0:T(8,128)(2,1)S(1)}, u32[]{:S(2)}, u32[]{:S(2)}) collective-permute-start(bf16[2,160,1024]{2,1,0:T(8,128)(2,1)S(1)} %copy-done.42), channel_id=1, source_target_pairs={{0,2},{1,3},{2,0},{3,1},{4,6},{5,7},{6,4},{7,5},{8,10},{9,11},{10,... | collective-permute-start | bytes 1966088 | tf_op jit(solution)/shard_map/ppermute | solution.py:401
  55.2 46.8 %collective-permute-start.21 = (bf16[2,160,1024]{2,1,0:T(8,128)(2,1)S(1)}, bf16[2,160,1024]{2,1,0:T(8,128)(2,1)S(1)}, u32[]{:S(2)}, u32[]{:S(2)}) collective-permute-start(bf16[2,160,1024]{2,1,0:T(8,128)(2,1)S(1)} %copy-done.41), channel_id=1, source_target_pairs={{0,3},{1,2},{2,1},{3,0},{4,7},{5,6},{6,5},{7,4},{8,11},{9,10},{10,... | collective-permute-start | bytes 1966088 | tf_op jit(solution)/shard_map/ppermute | solution.py:401
  65.3 56.1 %collective-permute-start.16 = (bf16[2,160,1024]{2,1,0:T(8,128)(2,1)S(1)}, bf16[2,160,1024]{2,1,0:T(8,128)(2,1)S(1)}, u32[]{:S(2)}, u32[]{:S(2)}) collective-permute-start(bf16[2,160,1024]{2,1,0:T(8,128)(2,1)S(1)} %copy-done.40), channel_id=1, source_target_pairs={{0,1},{1,0},{2,3},{3,2},{4,5},{5,4},{6,7},{7,6},{8,9},{9,8},{10,11... | collective-permute-start | bytes 1966088 | tf_op jit(solution)/shard_map/ppermute | solution.py:401
  76.3 45.9 %collective-permute-start.17 = (bf16[2,160,1024]{2,1,0:T(8,128)(2,1)S(1)}, bf16[2,160,1024]{2,1,0:T(8,128)(2,1)S(1)}, u32[]{:S(2)}, u32[]{:S(2)}) collective-permute-start(bf16[2,160,1024]{2,1,0:T(8,128)(2,1)S(1)} %copy-done.39), channel_id=1, source_target_pairs={{0,2},{1,3},{2,0},{3,1},{4,6},{5,7},{6,4},{7,5},{8,10},{9,11},{10,... | collective-permute-start | bytes 1966088 | tf_op jit(solution)/shard_map/ppermute | solution.py:401
  76.9 47.7 %collective-permute-start.18 = (bf16[2,160,1024]{2,1,0:T(8,128)(2,1)S(1)}, bf16[2,160,1024]{2,1,0:T(8,128)(2,1)S(1)}, u32[]{:S(2)}, u32[]{:S(2)}) collective-permute-start(bf16[2,160,1024]{2,1,0:T(8,128)(2,1)S(1)} %copy-done.38), channel_id=1, source_target_pairs={{0,3},{1,2},{2,1},{3,0},{4,7},{5,6},{6,5},{7,4},{8,11},{9,10},{10,... | collective-permute-start | bytes 1966088 | tf_op jit(solution)/shard_map/ppermute | solution.py:401
  89.2 10.2 %copy-start.9 = (bf16[2,160,1024]{2,1,0:T(8,128)(2,1)}, bf16[2,160,1024]{2,1,0:T(8,128)(2,1)S(1)}, u32[]{:S(2)}) copy-start(bf16[2,160,1024]{2,1,0:T(8,128)(2,1)S(1)} %collective-permute-done.20.refs_1_) | copy-start | bytes 1966084
  89.2 40.5 %collective-permute-start.13 = (bf16[2,288,1024]{2,1,0:T(8,128)(2,1)}, bf16[2,288,1024]{2,1,0:T(8,128)(2,1)S(1)}, u32[]{:S(2)}, u32[]{:S(2)}) collective-permute-start(bf16[2,288,1024]{2,1,0:T(8,128)(2,1)} %get-tuple-element.67), channel_id=1, source_target_pairs={{0,1},{1,0},{2,3},{3,2},{4,5},{5,4},{6,7},{7,6},{8,9},{9,8},{10,11... | collective-permute-start | bytes 3538952 | tf_op jit(solution)/shard_map/ppermute | solution.py:401
  102.8 75.9 %collective-permute-start.10 = (bf16[2,320,1024]{2,1,0:T(8,128)(2,1)}, bf16[2,320,1024]{2,1,0:T(8,128)(2,1)S(1)}, u32[]{:S(2)}, u32[]{:S(2)}) collective-permute-start(bf16[2,320,1024]{2,1,0:T(8,128)(2,1)} %get-tuple-element.64), channel_id=1, source_target_pairs={{0,1},{1,0},{2,3},{3,2},{4,5},{5,4},{6,7},{7,6},{8,9},{9,8},{10,11... | collective-permute-start | bytes 3932168 | tf_op jit(solution)/shard_map/ppermute | solution.py:401
  114.7 8.3 %copy-start.37 = (bf16[2,288,1024]{2,1,0:T(8,128)(2,1)S(1)}, bf16[2,288,1024]{2,1,0:T(8,128)(2,1)}, u32[]{:S(2)}) copy-start(bf16[2,288,1024]{2,1,0:T(8,128)(2,1)} %get-tuple-element.68) | copy-start | bytes 3538948
  114.7 10.7 %copy-start.36 = (bf16[2,288,1024]{2,1,0:T(8,128)(2,1)S(1)}, bf16[2,288,1024]{2,1,0:T(8,128)(2,1)}, u32[]{:S(2)}) copy-start(bf16[2,288,1024]{2,1,0:T(8,128)(2,1)} %get-tuple-element.69) | copy-start | bytes 3538948
  114.7 14.0 %copy-start.35 = (bf16[2,320,1024]{2,1,0:T(8,128)(2,1)S(1)}, bf16[2,320,1024]{2,1,0:T(8,128)(2,1)}, u32[]{:S(2)}) copy-start(bf16[2,320,1024]{2,1,0:T(8,128)(2,1)} %get-tuple-element.65) | copy-start | bytes 3932164
  114.7 16.0 %copy-start.34 = (bf16[2,320,1024]{2,1,0:T(8,128)(2,1)S(1)}, bf16[2,320,1024]{2,1,0:T(8,128)(2,1)}, u32[]{:S(2)}) copy-start(bf16[2,320,1024]{2,1,0:T(8,128)(2,1)} %get-tuple-element.66) | copy-start | bytes 3932164
  114.8 119.5 %copy-start.31 = (bf16[4,2,1024]{2,1,0:T(2,128)(2,1)S(1)}, bf16[4,2,1024]{2,1,0:T(2,128)(2,1)}, u32[]{:S(2)}) copy-start(bf16[4,2,1024]{2,1,0:T(2,128)(2,1)} %get-tuple-element.48.strip_ref) | copy-start | bytes 49156
  114.8 127.1 %copy-start.33 = (f32[15,1,256]{2,1,0:T(1,128)S(1)}, f32[15,1,256]{2,1,0:T(1,128)}, u32[]{:S(2)}) copy-start(f32[15,1,256]{2,1,0:T(1,128)} %get-tuple-element.45.refs_0_) | copy-start | bytes 46084
  121.3 0.9 copy-start.13
  122.2 5.7 %collective-permute-start.4 = (bf16[2,160,1024]{2,1,0:T(8,128)(2,1)}, bf16[2,160,1024]{2,1,0:T(8,128)(2,1)S(1)}, u32[]{:S(2)}, u32[]{:S(2)}) collective-permute-start(bf16[2,160,1024]{2,1,0:T(8,128)(2,1)} %get-tuple-element.58), channel_id=1, source_target_pairs={{0,1},{1,0},{2,3},{3,2},{4,5},{5,4},{6,7},{7,6},{8,9},{9,8},{10,11... | collective-permute-start | bytes 1966088 | tf_op jit(solution)/shard_map/ppermute | solution.py:401
  123.1 28.0 %collective-permute-start.14 = (bf16[2,288,1024]{2,1,0:T(8,128)(2,1)S(1)}, bf16[2,288,1024]{2,1,0:T(8,128)(2,1)S(1)}, u32[]{:S(2)}, u32[]{:S(2)}) collective-permute-start(bf16[2,288,1024]{2,1,0:T(8,128)(2,1)S(1)} %copy-done.37), channel_id=1, source_target_pairs={{0,2},{1,3},{2,0},{3,1},{4,6},{5,7},{6,4},{7,5},{8,10},{9,11},{10,... | collective-permute-start | bytes 3538952 | tf_op jit(solution)/shard_map/ppermute | solution.py:401
  124.6 0.9 copy-start.17
  125.4 51.6 %collective-permute-start.15 = (bf16[2,288,1024]{2,1,0:T(8,128)(2,1)S(1)}, bf16[2,288,1024]{2,1,0:T(8,128)(2,1)S(1)}, u32[]{:S(2)}, u32[]{:S(2)}) collective-permute-start(bf16[2,288,1024]{2,1,0:T(8,128)(2,1)S(1)} %copy-done.36), channel_id=1, source_target_pairs={{0,3},{1,2},{2,1},{3,0},{4,7},{5,6},{6,5},{7,4},{8,11},{9,10},{10,... | collective-permute-start | bytes 3538952 | tf_op jit(solution)/shard_map/ppermute | solution.py:401
  127.9 0.9 copy-start.19
  128.8 75.7 %collective-permute-start.11 = (bf16[2,320,1024]{2,1,0:T(8,128)(2,1)S(1)}, bf16[2,320,1024]{2,1,0:T(8,128)(2,1)S(1)}, u32[]{:S(2)}, u32[]{:S(2)}) collective-permute-start(bf16[2,320,1024]{2,1,0:T(8,128)(2,1)S(1)} %copy-done.35), channel_id=1, source_target_pairs={{0,2},{1,3},{2,0},{3,1},{4,6},{5,7},{6,4},{7,5},{8,10},{9,11},{10,... | collective-permute-start | bytes 3932168 | tf_op jit(solution)/shard_map/ppermute | solution.py:401
  129.7 1.0 copy-start.2
  130.8 102.4 %collective-permute-start.12 = (bf16[2,320,1024]{2,1,0:T(8,128)(2,1)S(1)}, bf16[2,320,1024]{2,1,0:T(8,128)(2,1)S(1)}, u32[]{:S(2)}, u32[]{:S(2)}) collective-permute-start(bf16[2,320,1024]{2,1,0:T(8,128)(2,1)S(1)} %copy-done.34), channel_id=1, source_target_pairs={{0,3},{1,2},{2,1},{3,0},{4,7},{5,6},{6,5},{7,4},{8,11},{9,10},{10,... | collective-permute-start | bytes 3932168 | tf_op jit(solution)/shard_map/ppermute | solution.py:401
  151.1 1.0 copy-start.4
  152.1 93.0 %collective-permute-start.7 = (bf16[2,320,1024]{2,1,0:T(8,128)(2,1)}, bf16[2,320,1024]{2,1,0:T(8,128)(2,1)}, u32[]{:S(2)}, u32[]{:S(2)}) collective-permute-start(bf16[2,320,1024]{2,1,0:T(8,128)(2,1)} %get-tuple-element.61), channel_id=1, source_target_pairs={{0,1},{1,0},{2,3},{3,2},{4,5},{5,4},{6,7},{7,6},{8,9},{9,8},{10,11... | collective-permute-start | bytes 3932168 | tf_op jit(solution)/shard_map/ppermute | solution.py:401
  177.0 1.1 copy-start.6
  178.1 82.7 %collective-permute-start.8 = (bf16[2,320,1024]{2,1,0:T(8,128)(2,1)}, bf16[2,320,1024]{2,1,0:T(8,128)(2,1)}, u32[]{:S(2)}, u32[]{:S(2)}) collective-permute-start(bf16[2,320,1024]{2,1,0:T(8,128)(2,1)} %get-tuple-element.62), channel_id=1, source_target_pairs={{0,2},{1,3},{2,0},{3,1},{4,6},{5,7},{6,4},{7,5},{8,10},{9,11},{10,... | collective-permute-start | bytes 3932168 | tf_op jit(solution)/shard_map/ppermute | solution.py:401
  178.7 110.8 %collective-permute-start.9 = (bf16[2,320,1024]{2,1,0:T(8,128)(2,1)}, bf16[2,320,1024]{2,1,0:T(8,128)(2,1)}, u32[]{:S(2)}, u32[]{:S(2)}) collective-permute-start(bf16[2,320,1024]{2,1,0:T(8,128)(2,1)} %get-tuple-element.63), channel_id=1, source_target_pairs={{0,3},{1,2},{2,1},{3,0},{4,7},{5,6},{6,5},{7,4},{8,11},{9,10},{10,... | collective-permute-start | bytes 3932168 | tf_op jit(solution)/shard_map/ppermute | solution.py:401
  204.5 101.6 %collective-permute-start.5 = (bf16[2,160,1024]{2,1,0:T(8,128)(2,1)}, bf16[2,160,1024]{2,1,0:T(8,128)(2,1)}, u32[]{:S(2)}, u32[]{:S(2)}) collective-permute-start(bf16[2,160,1024]{2,1,0:T(8,128)(2,1)} %get-tuple-element.59), channel_id=1, source_target_pairs={{0,2},{1,3},{2,0},{3,1},{4,6},{5,7},{6,4},{7,5},{8,10},{9,11},{10,... | collective-permute-start | bytes 1966088 | tf_op jit(solution)/shard_map/ppermute | solution.py:401
  233.2 1.1 copy-start
  234.2 83.3 %collective-permute-start.6 = (bf16[2,160,1024]{2,1,0:T(8,128)(2,1)}, bf16[2,160,1024]{2,1,0:T(8,128)(2,1)}, u32[]{:S(2)}, u32[]{:S(2)}) collective-permute-start(bf16[2,160,1024]{2,1,0:T(8,128)(2,1)} %get-tuple-element.60), channel_id=1, source_target_pairs={{0,3},{1,2},{2,1},{3,0},{4,7},{5,6},{6,5},{7,4},{8,11},{9,10},{10,... | collective-permute-start | bytes 1966088 | tf_op jit(solution)/shard_map/ppermute | solution.py:401
  242.8 46.7 %copy-start.8 = (bf16[2,160,1024]{2,1,0:T(8,128)(2,1)S(1)}, bf16[2,160,1024]{2,1,0:T(8,128)(2,1)}, u32[]{:S(2)}) copy-start(bf16[2,160,1024]{2,1,0:T(8,128)(2,1)} %get-tuple-element.83.refs_3_) | copy-start | bytes 1966084
  242.8 46.7 %copy-start.28 = (bf16[2,32,1024]{2,1,0:T(8,128)(2,1)S(1)}, bf16[2,32,1024]{2,1,0:T(8,128)(2,1)}, u32[]{:S(2)}) copy-start(bf16[2,32,1024]{2,1,0:T(8,128)(2,1)} %get-tuple-element.80.refs_0_) | copy-start | bytes 393220
  242.8 46.7 %copy-start.29 = (bf16[2,32,1024]{2,1,0:T(8,128)(2,1)S(1)}, bf16[2,32,1024]{2,1,0:T(8,128)(2,1)}, u32[]{:S(2)}) copy-start(bf16[2,32,1024]{2,1,0:T(8,128)(2,1)} %get-tuple-element.81.refs_1_) | copy-start | bytes 393220
  242.8 46.7 %copy-start.30 = (bf16[2,32,1024]{2,1,0:T(8,128)(2,1)S(1)}, bf16[2,32,1024]{2,1,0:T(8,128)(2,1)}, u32[]{:S(2)}) copy-start(bf16[2,32,1024]{2,1,0:T(8,128)(2,1)} %get-tuple-element.82.refs_2_) | copy-start | bytes 393220
  245.1 75.1 %collective-permute-start.1 = (bf16[2,32,1024]{2,1,0:T(8,128)(2,1)}, bf16[2,32,1024]{2,1,0:T(8,128)(2,1)S(1)}, u32[]{:S(2)}, u32[]{:S(2)}) collective-permute-start(bf16[2,32,1024]{2,1,0:T(8,128)(2,1)} %get-tuple-element.55), channel_id=1, source_target_pairs={{0,1},{1,0},{2,3},{3,2},{4,5},{5,4},{6,7},{7,6},{8,9},{9,8},{10,11... | collective-permute-start | bytes 393224 | tf_op jit(solution)/shard_map/ppermute | solution.py:401
  260.8 59.4 %collective-permute-start.2 = (bf16[2,32,1024]{2,1,0:T(8,128)(2,1)}, bf16[2,32,1024]{2,1,0:T(8,128)(2,1)S(1)}, u32[]{:S(2)}, u32[]{:S(2)}) collective-permute-start(bf16[2,32,1024]{2,1,0:T(8,128)(2,1)} %get-tuple-element.56), channel_id=1, source_target_pairs={{0,2},{1,3},{2,0},{3,1},{4,6},{5,7},{6,4},{7,5},{8,10},{9,11},{10,... | collective-permute-start | bytes 393224 | tf_op jit(solution)/shard_map/ppermute | solution.py:401
  289.4 33.2 %collective-permute-start.3 = (bf16[2,32,1024]{2,1,0:T(8,128)(2,1)}, bf16[2,32,1024]{2,1,0:T(8,128)(2,1)S(1)}, u32[]{:S(2)}, u32[]{:S(2)}) collective-permute-start(bf16[2,32,1024]{2,1,0:T(8,128)(2,1)} %get-tuple-element.57), channel_id=1, source_target_pairs={{0,3},{1,2},{2,1},{3,0},{4,7},{5,6},{6,5},{7,4},{8,11},{9,10},{10,... | collective-permute-start | bytes 393224 | tf_op jit(solution)/shard_map/ppermute | solution.py:401
  289.5 1.8 copy-start.21
  289.5 1.8 copy-start.23
  289.5 1.8 copy-start.25
  289.5 1.8 copy-start.27
  291.4 1.4 copy-start.10
  291.4 1.8 copy-start.12
  293.2 1.9 copy-start.14
  293.2 2.0 copy-start.16
  293.2 2.0 copy-start.18
  295.2 2.0 copy-start.3
  295.2 2.0 copy-start.5
  295.2 2.7 copy-start.7
  297.9 2.6 copy-start.1
  302.7 14.8 %copy-start.20 = (bf16[2,160,1024]{2,1,0:T(8,128)(2,1)S(1)}, bf16[2,160,1024]{2,1,0:T(8,128)(2,1)}, u32[]{:S(2)}) copy-start(bf16[2,160,1024]{2,1,0:T(8,128)(2,1)} %copy-done.19) | copy-start | bytes 1966084
  (6 other events, 4.8 us)

commit v5 on v4

--- a/solution.py
+++ b/solution.py
@@ -12,7 +12,7 @@
 MIB = 1024 * 1024
 ANY = pl.BlockSpec(memory_space=pl.ANY)
 VMEM = pl.BlockSpec(memory_space=pltpu.VMEM)
-STAGES = ((1, 5, 10, 15), (24, 34, 44, 49, 50))
+STAGES = ((1, 7, 11, 15), (27, 39, 49, 50))
 
 
 def block_rows(quota, count):
@@ -32,16 +32,16 @@
     return [(i, i ^ d if n & (n - 1) == 0 else (i + d) % n) for i in range(n)]
 
 
-def add_block(x, acc, rows):
+def add_block(x):
     experts, n, _, width = x.shape
+    parts = []
     for e in range(experts):
         for j in range(n):
             part = jnp.abs(x[e, j, :, :LANES])
             for g in range(1, width // LANES):
                 part = part + jnp.abs(x[e, j, :, g * LANES:(g + 1) * LANES])
-            at = (e * n + j) * rows
-            acc[at:at + rows, :] = part
-    return jnp.sum(acc[...].T, axis=0, keepdims=True)
+            parts.append(part)
+    return jnp.sum(jnp.concatenate(parts, axis=0).T, axis=0, keepdims=True)
 
 
 def scale_block(x, total, acc, put, me, n, rows):
@@ -51,16 +51,16 @@
         j = partner(me, d, n)
         for e in range(experts):
             inverse = acc[pl.ds(pl.multiple_of((e * n + j) * rows, rows), rows), :]
-            for g in range(width // LANES):
-                cut = slice(g * LANES, (g + 1) * LANES)
-                put(d, e, cut, (x[e, j, :, cut] * inverse).astype(jnp.bfloat16))
+            inverse = jnp.concatenate([inverse] * (width // LANES), axis=1)
+            put(d, e, (x[e, j] * inverse).astype(jnp.bfloat16))
 
 
 def head(n, rows, split, end, x_ref, weight_ref, gain_ref, *refs):
     sent, got = (None,) + refs[:n - 1], (None,) + refs[n - 1:2 * n - 2]
     own_ref, early_ref, scale_ref, strip = refs[2 * n - 2:2 * n + 2]
     (xbuf, nbuf, acc, mine, peers, weight, gain, load_sem, small_sem, store_sem, sum_send, sum_recv, strip_send,
-     strip_recv, first_send, first_recv, early_send, early_recv) = refs[2 * n + 2:]
+     strip_recv, first_send, first_recv, early_send, early_recv, raw, done, factor, raw_send, raw_recv,
+     rest_send, rest_recv, done_sem) = refs[2 * n + 2:]
     me = lax.axis_index("rows")
     known, width = xbuf.shape[0], xbuf.shape[-1]
 
@@ -94,8 +94,26 @@
         at = b * rows
         return pl.ds(at if isinstance(b, int) else pl.multiple_of(at, rows), rows)
 
+    bare = raw.shape[1]
+    experts = nbuf.shape[1]
+
+    def unscaled(d):
+        return remote(xbuf.at[0, 0, partner(me, d, n), pl.ds(0, bare)], raw.at[d - 1],
+                      raw_send.at[d - 1], raw_recv.at[d - 1], d)
+
     def first(d):
-        return remote(nbuf.at[d, :, some(0)], got[d], first_send.at[d - 1], first_recv.at[d - 1], d)
+        if d == 1:
+            return [remote(nbuf.at[d, :, some(0)], got[d], first_send.at[d - 1], first_recv.at[d - 1], d)]
+        copies = [remote(nbuf.at[d, 0, pl.ds(bare, rows - bare)], got[d].at[0, pl.ds(bare, rows - bare)],
+                         first_send.at[d - 1], first_recv.at[d - 1], d)]
+        if experts > 1:
+            others = pl.ds(1, experts - 1)
+            copies.append(remote(nbuf.at[d, others, some(0)], got[d].at[others],
+                                 rest_send.at[d - 1], rest_recv.at[d - 1], d))
+        return copies
+
+    def finished(d):
+        return pltpu.make_async_copy(done.at[d - 1], got[d].at[0, pl.ds(0, bare)], done_sem.at[d - 1])
 
     def early(b):
         return remote(nbuf.at[2, :, some(b)], early_ref.at[:, some(b - 1)], early_send.at[b - 1],
@@ -106,7 +124,7 @@
 
     def add(b, carry):
         load(b).wait()
-        mine[b] = add_block(xbuf.at[b], acc, rows)
+        mine[b] = add_block(xbuf.at[b])
         return carry
 
     def average(lo, hi):
@@ -117,8 +135,8 @@
             scale_ref[lo:hi] = total / (n * width)
 
     def scale(b):
-        def put(d, e, cut, value):
-            nbuf[d, e, some(b), cut] = value
+        def put(d, e, value):
+            nbuf[d, e, some(b), :] = value
 
         scale_block(xbuf.at[b], scale_ref[b], acc, put, me, n, rows)
 
@@ -129,6 +147,8 @@
     turns = [sums(0, 0, 1), sums(1, 1, end), sums(2, end, known)]
     for copy in turns[0]:
         copy.start()
+    for d in range(2, n):
+        unscaled(d).start()
     lax.fori_loop(1, end, add, 0)
     for copy in turns[1]:
         copy.start()
@@ -136,8 +156,10 @@
         copy.wait()
     average(0, 1)
     scale(0)
+    factor[...] = acc[pl.ds(pl.multiple_of(me * rows, rows), bare), :]
     for d in reversed(range(1, n)):
-        first(d).start()
+        for copy in first(d):
+            copy.start()
     lax.fori_loop(end, known, add, 0)
     for copy in turns[2]:
         copy.start()
@@ -178,8 +200,17 @@
 
     lax.fori_loop(1, end, finish, 0)
     own.wait()
+    for d in range(2, n):
+        unscaled(d).wait()
+        for g in range(width // LANES):
+            cut = slice(g * LANES, (g + 1) * LANES)
+            done[d - 1, :, cut] = (raw[d - 1, :, cut] * factor[...]).astype(jnp.bfloat16)
+        finished(d).start()
+    for d in range(2, n):
+        finished(d).wait()
     for d in range(1, n):
-        first(d).wait()
+        for copy in first(d):
+            copy.wait()
     if split:
         @pl.when(lax.rem(me, 2) == 0)
         def _():
@@ -190,10 +221,10 @@
             lax.fori_loop(1, end, arrive, 0)
 
 
-def add_up(rows, *refs):
-    mine_ref, acc = refs[-2:]
+def add_up(*refs):
+    mine_ref = refs[-1]
     for k in range(mine_ref.shape[0]):
-        mine_ref[k] = add_block(refs[k], acc.at[k], rows)
+        mine_ref[k] = add_block(refs[k])
 
 
 def signal_pair(me):
@@ -210,8 +241,8 @@
     copy.wait()
 
 
-def add_up_pair(rows, step, *refs):
-    half_ref, acc, mine, theirs, send_sem, recv_sem = refs[-6:]
+def add_up_pair(step, *refs):
+    half_ref, mine, theirs, send_sem, recv_sem = refs[-5:]
     me, at = lax.axis_index("rows"), pl.program_id(0)
 
     @pl.when(at == 0)
@@ -219,7 +250,7 @@
         signal_pair(me)
 
     for k in range(step):
-        mine[at * step + k] = add_block(refs[k], acc.at[k], rows)
+        mine[at * step + k] = add_block(refs[k])
 
     @pl.when(at == pl.num_programs(0) - 1)
     def _():
@@ -261,9 +292,9 @@
         scale = scale / (n * x_ref.shape[-1])
     scale_ref[0] = scale
 
-    def put(d, e, cut, value):
+    def put(d, e, value):
         ref = sent[d - 1] if d else out_ref
-        ref[e, :, cut] = value
+        ref[e] = value
 
     scale_block(x_ref, scale, acc, put, me, n, rows)
 
@@ -389,6 +420,14 @@
             pltpu.SemaphoreType.DMA((n - 1,)),
             pltpu.SemaphoreType.DMA((end,)),
             pltpu.SemaphoreType.DMA((end,)),
+            pltpu.VMEM((n - 1, rows // 2, width), f32),
+            pltpu.VMEM((n - 1, rows // 2, width), bf16),
+            pltpu.VMEM((rows // 2, LANES), f32),
+            pltpu.SemaphoreType.DMA((n - 1,)),
+            pltpu.SemaphoreType.DMA((n - 1,)),
+            pltpu.SemaphoreType.DMA((n - 1,)),
+            pltpu.SemaphoreType.DMA((n - 1,)),
+            pltpu.SemaphoreType.DMA((n - 1,)),
         ],
         compiler_params=pltpu.CompilerParams(
             collective_id=0, has_side_effects=True, vmem_limit_bytes=62 * MIB),
@@ -406,7 +445,7 @@
     def sums(lo, hi, after):
         step = max(k for k in (4, 3, 2, 1) if (hi - lo) % k == 0)
         return pl.pallas_call(
-            functools.partial(add_up, rows),
+            add_up,
             grid=((hi - lo) // step,),
             out_shape=jax.ShapeDtypeStruct((hi - lo, 1, wide), f32),
             in_specs=[
@@ -414,7 +453,6 @@
                 for k in range(step)
             ] + [ANY],
             out_specs=pl.BlockSpec((step, 1, wide), lambda b: (b, 0, 0)),
-            scratch_shapes=[pltpu.VMEM((step, wide, LANES), f32)],
             compiler_params=pltpu.CompilerParams(vmem_limit_bytes=24 * MIB),
         )(*[x] * step, after)
 
@@ -423,7 +461,7 @@
         part = (hi - lo, 1, wide // 2)
         sems = [pltpu.SemaphoreType.DMA, pltpu.SemaphoreType.DMA]
         half = pl.pallas_call(
-            functools.partial(add_up_pair, rows, step),
+            functools.partial(add_up_pair, step),
             grid=((hi - lo) // step,),
             out_shape=jax.ShapeDtypeStruct(part, f32),
             in_specs=[
@@ -432,7 +470,6 @@
             ] + [ANY],
             out_specs=pl.BlockSpec(part, lambda b: (0, 0, 0)),
             scratch_shapes=[
-                pltpu.VMEM((step, wide, LANES), f32),
                 pltpu.VMEM((hi - lo, 1, wide), f32),
                 pltpu.VMEM((hi - lo, 1, wide), f32),
             ] + sems,

time: 325 us -> 308 us (0.948)
  Pallas kernels: 107 us -> 98.5 us
  waiting for transfers between devices: 176 us -> 171 us
  local copies, waits for them, and re-layouts: 14.5 us -> 10.9 us
    ppermute x24 -> x21, waiting for transfers between devices: 166 us -> 99 us  [move(): return lax.ppermute(array, 'rows', pairs(d, n))]
    ppermute x1, waiting for transfers between devices: 10 us -> 71.8 us  [per_device(): lax.ppermute(sent[1], 'rows', [pair for pair in pairs(2, n) if pair[0] % 2])]
    pallas_call x7 -> x6, Pallas kernels: 50 us -> 44.8 us  [scaled(): pl.pallas_call(functools.partial(narrow, n, rows, (len(held), len(parts))...]
    unnamed x91 -> x75, local copies, waits for them, and re-layouts: 13.5 us -> 9.97 us
    pallas_call x9 -> x8, Pallas kernels: 18.6 us -> 16.6 us  [placed(): pl.pallas_call(functools.partial(place, n, spots, final), out_shape=jax.S...]
    ppermute x24 -> x21, starting transfers between devices: 21.4 us -> 23 us  [move(): return lax.ppermute(array, 'rows', pairs(d, n))]
  transfers between devices with their start and end apart: 25 -> 22, of which waited for: 13 -> 7; matrix products, arithmetic and copies ran while one was open for 1% -> 1% of each run, Pallas kernels for 27% -> 26%
where the time goes in v5:
time: 308 us; the launch traced here: 307 us
  waiting for transfers between devices  171 us (56%)
  Pallas kernels  98.5 us (32%)
  starting transfers between devices  25.7 us (8%)
  local copies, waits for them, and re-layouts  10.9 us (4%)
    ppermute x21, waiting for transfers between devices, move(): return lax.ppermute(array, 'rows', pairs(d, n))  99 us
    ppermute x1, waiting for transfers between devices, per_device(): lax.ppermute(sent[1], 'rows', [pair for pair in pairs(2, n) if pair[0] % 2])  71.8 us
    pallas_call x6, Pallas kernels, scaled(): pl.pallas_call(functools.partial(narrow, n, rows, (len(held), len(parts))...  44.8 us
    ppermute x21, starting transfers between devices, move(): return lax.ppermute(array, 'rows', pairs(d, n))  23 us
    pallas_call x8, Pallas kernels, placed(): pl.pallas_call(functools.partial(place, n, spots, final), out_shape=jax.S...  16.6 us
    pallas_call x1, Pallas kernels, per_device(): pl.pallas_call(functools.partial(head, n, rows, split, end), out_shape=[p...  14.7 us
    pallas_call x1, Pallas kernels, sums_pair(): pl.pallas_call(functools.partial(add_up_pair, step), grid=((hi - lo) // s...  14.4 us
    unnamed x75, local copies, waits for them, and re-layouts  9.97 us
  transfers between devices with their start and end apart: 22, of which 7 were waited for; matrix products, arithmetic and copies ran while one was open for 1% of the time, Pallas kernels for 26%

profile of v5, /device:TPU:1, one launch (start us, length us, event | category | flops | bytes accessed | tf_op | source)
XLA Modules:
  0.0 306.9 jit_solution(2648650825166864243)
XLA Ops:
  0.6 14.7 %head.1 = (bf16[2,192,1024]{2,1,0:T(8,128)(2,1)}, bf16[2,192,1024]{2,1,0:T(8,128)(2,1)}, bf16[2,192,1024]{2,1,0:T(8,128)(2,1)}, bf16[2,32,1024]{2,1,0:T(8,128)(2...) custom-call(f32[2,4,1600,1024]{3,2,1,0:T(8,128)} %bitcast.15, ...), custom_call_target="tpu_custom_call" | custom-call | tf_op jit(solution)/shard_map/head/pallas_call | solution.py:393
  15.3 4.5 %shard_map.58 = (bf16[2,128,1024]{2,1,0:T(8,128)(2,1)}, bf16[2,128,1024]{2,1,0:T(8,128)(2,1)}, bf16[2,128,1024]{2,1,0:T(8,128)(2,1)}, bf16[2,1600,4096]{2,1,0:T(8,128)(2,1)}, f32[4,1,256]{2,1,0:T(1,128)}) custom-call(f32[2,4,1600,1024]{3,2,1,0:T(8,128)} %bitcast.16, f32[15,1,256]{2,1,0:T(1,128)} %get-tuple-element.41.refs_0_), custom_call_target="tpu_custom_call" | custom-call | tf_op jit(solution)/shard_map/pallas_call | solution.py:497
  19.8 8.3 %collective-permute-start.16 = (bf16[2,128,1024]{2,1,0:T(8,128)(2,1)}, bf16[2,128,1024]{2,1,0:T(8,128)(2,1)S(1)}, u32[]{:S(2)}, u32[]{:S(2)}) collective-permute-start(bf16[2,128,1024]{2,1,0:T(8,128)(2,1)} %get-tuple-element.65), channel_id=1, source_target_pairs={{0,1},{1,0},{2,3},{3,2},{4,5},{5,4},{6,7},{7,6},{8,9},{9,8},{10,11... | collective-permute-start | bytes 1572872 | tf_op jit(solution)/shard_map/ppermute | solution.py:440
  28.1 0.7 collective-permute-start.17
  28.8 1.0 collective-permute-start.18
  29.8 4.4 %shard_map.59 = (bf16[2,128,1024]{2,1,0:T(8,128)(2,1)}, bf16[2,128,1024]{2,1,0:T(8,128)(2,1)}, bf16[2,128,1024]{2,1,0:T(8,128)(2,1)}, bf16[2,1600,4096]{2,1,0:T(8,128)(2,1)}, f32[4,1,256]{2,1,0:T(1,128)}) custom-call(f32[2,4,1600,1024]{3,2,1,0:T(8,128)} %bitcast.17, f32[15,1,256]{2,1,0:T(1,128)} %get-tuple-element.41.refs_0_, ...), custom_call_target="tpu_custom_call", output_to_operand_aliasing={{3}: (2, {})} | custom-call | tf_op jit(solution)/shard_map/pallas_call | solution.py:497
  34.2 0.2 collective-permute-start.13
  34.4 0.7 copy-done.28
  35.1 14.4 %shard_map.60.half_ref = f32[35,1,128]{2,1,0:T(1,128)S(1)} custom-call(f32[2,4,1600,1024]{3,2,1,0:T(8,128)} %bitcast.18, f32[2,4,1600,1024]{3,2,1,0:T(8,128)} %bitcast.19, f32[2,4,1600,1024]{3,2,1,0:T(8,128)} %bitcast.20, f32[2,4,1600,1024]{3,2,1,0:T(8,128)} %bitcast.21, f32[2,4,1600,1024]{3,2,1,0:T(8,128)} %bitcast.22, f32[4,1,256]{2,1,0:T(1,128)S(1)} %copy-done.28), custom_call_target="tpu_custom_call" | custom-call | tf_op jit(solution)/shard_map/pallas_call | solution.py:463
  49.5 0.7 collective-permute-start
  50.3 2.8 collective-permute-done.refs_0_
  53.0 1.2 collective-permute-start.19
  54.3 0.0 collective-permute-done.16.refs_0_
  54.3 0.7 collective-permute-start.14
  55.0 1.0 collective-permute-start.15
  56.1 0.8 collective-permute-start.20
  56.9 1.2 shard_map.61.refs_0_
  58.1 11.7 %shard_map.62 = (bf16[2,384,1024]{2,1,0:T(8,128)(2,1)}, bf16[2,384,1024]{2,1,0:T(8,128)(2,1)}, bf16[2,384,1024]{2,1,0:T(8,128)(2,1)}, bf16[2,1600,4096]{2,1,0:T(8,128)(2,1)}, f32[12,1,256]{2,1,0:T(1,128)}) custom-call(f32[2,4,1600,1024]{3,2,1,0:T(8,128)} %bitcast.23, f32[35,1,256]{2,1,0:T(1,128)S(1)} %shard_map.61.refs_0_, ...), custom_call_target="tpu_custom_call", output_to_operand_aliasing={{3}: (2, {})} | custom-call | tf_op jit(solution)/shard_map/pallas_call | solution.py:497
  69.9 0.4 collective-permute-start.10
  70.3 11.6 %shard_map.63 = (bf16[2,384,1024]{2,1,0:T(8,128)(2,1)}, bf16[2,384,1024]{2,1,0:T(8,128)(2,1)}, bf16[2,384,1024]{2,1,0:T(8,128)(2,1)}, bf16[2,1600,4096]{2,1,0:T(8,128)(2,1)}, f32[12,1,256]{2,1,0:T(1,128)}) custom-call(f32[2,4,1600,1024]{3,2,1,0:T(8,128)} %bitcast.24, f32[35,1,256]{2,1,0:T(1,128)S(1)} %shard_map.61.refs_0_, ...), custom_call_target="tpu_custom_call", output_to_operand_aliasing={{3}: (2, {})} | custom-call | tf_op jit(solution)/shard_map/pallas_call | solution.py:497
  81.9 10.3 %shard_map.64 = (bf16[2,320,1024]{2,1,0:T(8,128)(2,1)}, bf16[2,320,1024]{2,1,0:T(8,128)(2,1)}, bf16[2,320,1024]{2,1,0:T(8,128)(2,1)}, bf16[2,1600,4096]{2,1,0:T(8,128)(2,1)}, f32[10,1,256]{2,1,0:T(1,128)}) custom-call(f32[2,4,1600,1024]{3,2,1,0:T(8,128)} %bitcast.25, f32[35,1,256]{2,1,0:T(1,128)S(1)} %shard_map.61.refs_0_, ...), custom_call_target="tpu_custom_call", output_to_operand_aliasing={{3}: (2, {})} | custom-call | tf_op jit(solution)/shard_map/pallas_call | solution.py:497
  92.2 0.8 copy-done.20
  93.0 0.2 collective-permute-start.4
  93.2 0.8 copy-done.22
  94.1 0.7 collective-permute-start.11
  94.8 0.9 copy-done.6
  95.7 1.2 collective-permute-start.12
  96.9 0.9 copy-done.8
  97.8 2.7 collective-permute-start.21
  100.5 71.8 %collective-permute-done.21.refs_3_ = bf16[2,192,1024]{2,1,0:T(8,128)(2,1)S(1)} collective-permute-done((bf16[2,192,1024]{2,1,0:T(8,128)(2,1)S(1)}, bf16[2,192,1024]{2,1,0:T(8,128)(2,1)S(1)}, u32[]{:S(2)}, u32[]{:S(2)}) %collective-permute-start.21) | collective-permute-done | bytes 786464 | tf_op jit(solution)/shard_map/ppermute | solution.py:559
  172.3 0.9 copy-done.10
  173.2 1.1 copy-done.2
  174.3 0.7 collective-permute-start.8
  175.0 1.4 collective-permute-start.9
  176.5 0.7 collective-permute-start.5
  177.2 1.1 copy-done
  178.3 0.6 collective-permute-start.6
  179.0 6.8 %router.1 = bf16[8,4,2,1024]{3,2,1,0:T(2,128)(2,1)S(1)} custom-call(bf16[4,2,1024]{2,1,0:T(2,128)(2,1)S(1)} %copy-done.27), custom_call_target="tpu_custom_call" | custom-call | tf_op jit(solution)/shard_map/router/pallas_call | solution.py:532
  185.8 0.1 copy.21
  185.8 0.7 copy.22
  186.6 0.1 copy.19
  186.7 0.1 copy.20
  186.8 0.7 reshape.20
  187.5 2.3 shard_map.65
  189.8 1.5 collective-permute-start.1
  191.3 18.7 %collective-permute-done.8.refs_1_ = bf16[2,384,1024]{2,1,0:T(8,128)(2,1)} collective-permute-done((bf16[2,384,1024]{2,1,0:T(8,128)(2,1)}, bf16[2,384,1024]{2,1,0:T(8,128)(2,1)}, u32[]{:S(2)}, u32[]{:S(2)}) %collective-permute-start.8) | collective-permute-done | bytes 1572896 | tf_op jit(solution)/shard_map/ppermute | solution.py:440
  210.1 0.7 collective-permute-start.2
  210.8 34.6 %collective-permute-done.9.refs_2_ = bf16[2,384,1024]{2,1,0:T(8,128)(2,1)} collective-permute-done((bf16[2,384,1024]{2,1,0:T(8,128)(2,1)}, bf16[2,384,1024]{2,1,0:T(8,128)(2,1)}, u32[]{:S(2)}, u32[]{:S(2)}) %collective-permute-start.9) | collective-permute-done | bytes 1572896 | tf_op jit(solution)/shard_map/ppermute | solution.py:440
  245.5 1.9 shard_map.66.refs_4_
  247.4 0.3 copy-done.11
  247.7 1.6 shard_map.67.refs_3_
  249.3 0.4 copy-done.17
  249.7 1.3 shard_map.68.refs_3_
  251.0 0.3 copy-done.21
  251.3 0.3 copy-done.23
  251.6 1.3 shard_map.69.refs_3_
  252.9 0.7 copy-done.1
  253.6 2.5 shard_map.70.refs_3_
  256.2 3.7 %shard_map.71.refs_3_ = bf16[2,1600,4096]{2,1,0:T(8,128)(2,1)} custom-call(bf16[2,384,1024]{2,1,0:T(8,128)(2,1)} %collective-permute-done.7.refs_0_, bf16[2,384,1024]{2,1,0:T(8,128)(2,1)} %collective-permute-done.8.refs_1_, bf16[2,384,1024]{2,1,0:T(8,128)(2,1)} %collective-permute-done.9.refs_2_, ...), custom_call_target="tpu_custom_call", output_to_operand_aliasing={{}: (3, {})} | custom-call | tf_op jit(solution)/shard_map/pallas_call | solution.py:518
  259.9 11.9 %collective-permute-done.5.refs_1_ = bf16[2,320,1024]{2,1,0:T(8,128)(2,1)} collective-permute-done((bf16[2,320,1024]{2,1,0:T(8,128)(2,1)}, bf16[2,320,1024]{2,1,0:T(8,128)(2,1)}, u32[]{:S(2)}, u32[]{:S(2)}) %collective-permute-start.5) | collective-permute-done | bytes 1310752 | tf_op jit(solution)/shard_map/ppermute | solution.py:440
  271.9 29.7 %collective-permute-done.6.refs_2_ = bf16[2,320,1024]{2,1,0:T(8,128)(2,1)} collective-permute-done((bf16[2,320,1024]{2,1,0:T(8,128)(2,1)}, bf16[2,320,1024]{2,1,0:T(8,128)(2,1)}, u32[]{:S(2)}, u32[]{:S(2)}) %collective-permute-start.6) | collective-permute-done | bytes 1310752 | tf_op jit(solution)/shard_map/ppermute | solution.py:440
  301.6 3.4 %shard_map.72.refs_3_ = bf16[2,1600,4096]{2,1,0:T(8,128)(2,1)} custom-call(bf16[2,320,1024]{2,1,0:T(8,128)(2,1)S(1)} %copy-done.3, bf16[2,320,1024]{2,1,0:T(8,128)(2,1)} %collective-permute-done.5.refs_1_, bf16[2,320,1024]{2,1,0:T(8,128)(2,1)} %collective-permute-done.6.refs_2_, bf16[2,1600,4096]{2,1,0:T(8,128)(2,1)} %shard_map.71.refs_3_), custom_call_target="tpu_custom_call", output_to_operand_aliasing={{}: (3, {})} | custom-call | tf_op jit(solution)/shard_map/pallas_call | solution.py:518
  305.0 1.1 collective-permute-done.3.refs_2_
  306.1 0.8 shard_map.73
  (79 shorter events, 0.2 us)
Async XLA Ops:
  19.8 34.5 %collective-permute-start.16 = (bf16[2,128,1024]{2,1,0:T(8,128)(2,1)}, bf16[2,128,1024]{2,1,0:T(8,128)(2,1)S(1)}, u32[]{:S(2)}, u32[]{:S(2)}) collective-permute-start(bf16[2,128,1024]{2,1,0:T(8,128)(2,1)} %get-tuple-element.65), channel_id=1, source_target_pairs={{0,1},{1,0},{2,3},{3,2},{4,5},{5,4},{6,7},{7,6},{8,9},{9,8},{10,11... | collective-permute-start | bytes 1572872 | tf_op jit(solution)/shard_map/ppermute | solution.py:440
  28.1 26.9 %collective-permute-start.17 = (bf16[2,128,1024]{2,1,0:T(8,128)(2,1)}, bf16[2,128,1024]{2,1,0:T(8,128)(2,1)S(1)}, u32[]{:S(2)}, u32[]{:S(2)}) collective-permute-start(bf16[2,128,1024]{2,1,0:T(8,128)(2,1)} %get-tuple-element.66), channel_id=1, source_target_pairs={{0,2},{1,3},{2,0},{3,1},{4,6},{5,7},{6,4},{7,5},{8,10},{9,11},{10,... | collective-permute-start | bytes 1572872 | tf_op jit(solution)/shard_map/ppermute | solution.py:440
  28.8 27.3 %collective-permute-start.18 = (bf16[2,128,1024]{2,1,0:T(8,128)(2,1)}, bf16[2,128,1024]{2,1,0:T(8,128)(2,1)S(1)}, u32[]{:S(2)}, u32[]{:S(2)}) collective-permute-start(bf16[2,128,1024]{2,1,0:T(8,128)(2,1)} %get-tuple-element.67), channel_id=1, source_target_pairs={{0,3},{1,2},{2,1},{3,0},{4,7},{5,6},{6,5},{7,4},{8,11},{9,10},{10,... | collective-permute-start | bytes 1572872 | tf_op jit(solution)/shard_map/ppermute | solution.py:440
  34.2 35.7 %collective-permute-start.13 = (bf16[2,128,1024]{2,1,0:T(8,128)(2,1)}, bf16[2,128,1024]{2,1,0:T(8,128)(2,1)S(1)}, u32[]{:S(2)}, u32[]{:S(2)}) collective-permute-start(bf16[2,128,1024]{2,1,0:T(8,128)(2,1)} %get-tuple-element.62), channel_id=1, source_target_pairs={{0,1},{1,0},{2,3},{3,2},{4,5},{5,4},{6,7},{7,6},{8,9},{9,8},{10,11... | collective-permute-start | bytes 1572872 | tf_op jit(solution)/shard_map/ppermute | solution.py:440
  34.4 0.7 copy-start.28
  35.1 17.9 %copy-start.34 = (bf16[2,192,1024]{2,1,0:T(8,128)(2,1)S(1)}, bf16[2,192,1024]{2,1,0:T(8,128)(2,1)}, u32[]{:S(2)}) copy-start(bf16[2,192,1024]{2,1,0:T(8,128)(2,1)} %get-tuple-element.68) | copy-start | bytes 2359300
  35.1 19.2 %copy-start.36 = (bf16[2,128,1024]{2,1,0:T(8,128)(2,1)S(1)}, bf16[2,128,1024]{2,1,0:T(8,128)(2,1)}, u32[]{:S(2)}) copy-start(bf16[2,128,1024]{2,1,0:T(8,128)(2,1)} %get-tuple-element.63) | copy-start | bytes 1572868
  35.1 19.9 %copy-start.35 = (bf16[2,128,1024]{2,1,0:T(8,128)(2,1)S(1)}, bf16[2,128,1024]{2,1,0:T(8,128)(2,1)}, u32[]{:S(2)}) copy-start(bf16[2,128,1024]{2,1,0:T(8,128)(2,1)} %get-tuple-element.64) | copy-start | bytes 1572868
  35.1 21.0 %copy-start.33 = (bf16[2,192,1024]{2,1,0:T(8,128)(2,1)S(1)}, bf16[2,192,1024]{2,1,0:T(8,128)(2,1)}, u32[]{:S(2)}) copy-start(bf16[2,192,1024]{2,1,0:T(8,128)(2,1)} %get-tuple-element.69) | copy-start | bytes 2359300
  49.5 3.5 %collective-permute-start = (f32[35,1,128]{2,1,0:T(1,128)S(1)}, f32[35,1,128]{2,1,0:T(1,128)S(1)}, u32[]{:S(2)}, u32[]{:S(2)}) collective-permute-start(f32[35,1,128]{2,1,0:T(1,128)S(1)} %shard_map.60.half_ref), channel_id=1, source_target_pairs={{0,2},{1,3},{2,0},{3,1},{4,6},{5,7},{6,4},{7,5},{8,10},{9,11},{10,... | collective-permute-start | bytes 53768 | tf_op jit(solution)/shard_map/ppermute | solution.py:440
  53.0 41.7 %collective-permute-start.19 = (bf16[2,192,1024]{2,1,0:T(8,128)(2,1)S(1)}, bf16[2,192,1024]{2,1,0:T(8,128)(2,1)S(1)}, u32[]{:S(2)}, u32[]{:S(2)}) collective-permute-start(bf16[2,192,1024]{2,1,0:T(8,128)(2,1)S(1)} %copy-done.34), channel_id=1, source_target_pairs={{0,1},{1,0},{2,3},{3,2},{4,5},{5,4},{6,7},{7,6},{8,9},{9,8},{10,11... | collective-permute-start | bytes 2359304 | tf_op jit(solution)/shard_map/ppermute | solution.py:440
  54.3 15.6 %copy-start.12 = (bf16[2,128,1024]{2,1,0:T(8,128)(2,1)}, bf16[2,128,1024]{2,1,0:T(8,128)(2,1)S(1)}, u32[]{:S(2)}) copy-start(bf16[2,128,1024]{2,1,0:T(8,128)(2,1)S(1)} %collective-permute-done.16.refs_0_) | copy-start | bytes 1572868
  54.3 37.9 %collective-permute-start.14 = (bf16[2,128,1024]{2,1,0:T(8,128)(2,1)S(1)}, bf16[2,128,1024]{2,1,0:T(8,128)(2,1)S(1)}, u32[]{:S(2)}, u32[]{:S(2)}) collective-permute-start(bf16[2,128,1024]{2,1,0:T(8,128)(2,1)S(1)} %copy-done.36), channel_id=1, source_target_pairs={{0,2},{1,3},{2,0},{3,1},{4,6},{5,7},{6,4},{7,5},{8,10},{9,11},{10,... | collective-permute-start | bytes 1572872 | tf_op jit(solution)/shard_map/ppermute | solution.py:440
  55.0 14.9 %copy-start.14 = (bf16[2,128,1024]{2,1,0:T(8,128)(2,1)}, bf16[2,128,1024]{2,1,0:T(8,128)(2,1)S(1)}, u32[]{:S(2)}) copy-start(bf16[2,128,1024]{2,1,0:T(8,128)(2,1)S(1)} %collective-permute-done.17.refs_1_) | copy-start | bytes 1572868
  55.0 38.2 %collective-permute-start.15 = (bf16[2,128,1024]{2,1,0:T(8,128)(2,1)S(1)}, bf16[2,128,1024]{2,1,0:T(8,128)(2,1)S(1)}, u32[]{:S(2)}, u32[]{:S(2)}) collective-permute-start(bf16[2,128,1024]{2,1,0:T(8,128)(2,1)S(1)} %copy-done.35), channel_id=1, source_target_pairs={{0,3},{1,2},{2,1},{3,0},{4,7},{5,6},{6,5},{7,4},{8,11},{9,10},{10,... | collective-permute-start | bytes 1572872 | tf_op jit(solution)/shard_map/ppermute | solution.py:440
  56.1 13.8 %copy-start.16 = (bf16[2,128,1024]{2,1,0:T(8,128)(2,1)}, bf16[2,128,1024]{2,1,0:T(8,128)(2,1)S(1)}, u32[]{:S(2)}) copy-start(bf16[2,128,1024]{2,1,0:T(8,128)(2,1)S(1)} %collective-permute-done.18.refs_2_) | copy-start | bytes 1572868
  56.1 40.8 %collective-permute-start.20 = (bf16[2,192,1024]{2,1,0:T(8,128)(2,1)S(1)}, bf16[2,192,1024]{2,1,0:T(8,128)(2,1)S(1)}, u32[]{:S(2)}, u32[]{:S(2)}) collective-permute-start(bf16[2,192,1024]{2,1,0:T(8,128)(2,1)S(1)} %copy-done.33), channel_id=1, source_target_pairs={{0,3},{1,2},{2,1},{3,0},{4,7},{5,6},{6,5},{7,4},{8,11},{9,10},{10,... | collective-permute-start | bytes 2359304 | tf_op jit(solution)/shard_map/ppermute | solution.py:440
  69.9 12.0 %copy-start.18 = (bf16[2,128,1024]{2,1,0:T(8,128)(2,1)}, bf16[2,128,1024]{2,1,0:T(8,128)(2,1)S(1)}, u32[]{:S(2)}) copy-start(bf16[2,128,1024]{2,1,0:T(8,128)(2,1)S(1)} %collective-permute-done.13.refs_0_) | copy-start | bytes 1572868
  69.9 105.1 %collective-permute-start.10 = (bf16[2,384,1024]{2,1,0:T(8,128)(2,1)}, bf16[2,384,1024]{2,1,0:T(8,128)(2,1)S(1)}, u32[]{:S(2)}, u32[]{:S(2)}) collective-permute-start(bf16[2,384,1024]{2,1,0:T(8,128)(2,1)} %get-tuple-element.59), channel_id=1, source_target_pairs={{0,1},{1,0},{2,3},{3,2},{4,5},{5,4},{6,7},{7,6},{8,9},{9,8},{10,11... | collective-permute-start | bytes 4718600 | tf_op jit(solution)/shard_map/ppermute | solution.py:440
  81.9 12.2 %copy-start.31 = (bf16[2,384,1024]{2,1,0:T(8,128)(2,1)S(1)}, bf16[2,384,1024]{2,1,0:T(8,128)(2,1)}, u32[]{:S(2)}) copy-start(bf16[2,384,1024]{2,1,0:T(8,128)(2,1)} %get-tuple-element.60) | copy-start | bytes 4718596
  81.9 13.8 %copy-start.30 = (bf16[2,384,1024]{2,1,0:T(8,128)(2,1)S(1)}, bf16[2,384,1024]{2,1,0:T(8,128)(2,1)}, u32[]{:S(2)}) copy-start(bf16[2,384,1024]{2,1,0:T(8,128)(2,1)} %get-tuple-element.61) | copy-start | bytes 4718596
  81.9 15.9 %copy-start.32 = (bf16[2,192,1024]{2,1,0:T(8,128)(2,1)S(1)}, bf16[2,192,1024]{2,1,0:T(8,128)(2,1)}, u32[]{:S(2)}) copy-start(bf16[2,192,1024]{2,1,0:T(8,128)(2,1)} %get-tuple-element.71) | copy-start | bytes 2359300
  81.9 97.1 %copy-start.27 = (bf16[4,2,1024]{2,1,0:T(2,128)(2,1)S(1)}, bf16[4,2,1024]{2,1,0:T(2,128)(2,1)}, u32[]{:S(2)}) copy-start(bf16[4,2,1024]{2,1,0:T(2,128)(2,1)} %get-tuple-element.44.strip_ref) | copy-start | bytes 49156
  81.9 104.7 %copy-start.29 = (f32[15,1,256]{2,1,0:T(1,128)S(1)}, f32[15,1,256]{2,1,0:T(1,128)}, u32[]{:S(2)}) copy-start(f32[15,1,256]{2,1,0:T(1,128)} %get-tuple-element.41.refs_0_) | copy-start | bytes 46084
  92.2 0.8 copy-start.20
  93.0 80.2 %collective-permute-start.4 = (bf16[2,320,1024]{2,1,0:T(8,128)(2,1)}, bf16[2,320,1024]{2,1,0:T(8,128)(2,1)S(1)}, u32[]{:S(2)}, u32[]{:S(2)}) collective-permute-start(bf16[2,320,1024]{2,1,0:T(8,128)(2,1)} %get-tuple-element.53), channel_id=1, source_target_pairs={{0,1},{1,0},{2,3},{3,2},{4,5},{5,4},{6,7},{7,6},{8,9},{9,8},{10,11... | collective-permute-start | bytes 3932168 | tf_op jit(solution)/shard_map/ppermute | solution.py:440
  93.2 0.8 copy-start.22
  94.1 82.4 %collective-permute-start.11 = (bf16[2,384,1024]{2,1,0:T(8,128)(2,1)S(1)}, bf16[2,384,1024]{2,1,0:T(8,128)(2,1)S(1)}, u32[]{:S(2)}, u32[]{:S(2)}) collective-permute-start(bf16[2,384,1024]{2,1,0:T(8,128)(2,1)S(1)} %copy-done.31), channel_id=1, source_target_pairs={{0,2},{1,3},{2,0},{3,1},{4,6},{5,7},{6,4},{7,5},{8,10},{9,11},{10,... | collective-permute-start | bytes 4718600 | tf_op jit(solution)/shard_map/ppermute | solution.py:440
  94.8 0.9 copy-start.6
  95.7 81.5 %collective-permute-start.12 = (bf16[2,384,1024]{2,1,0:T(8,128)(2,1)S(1)}, bf16[2,384,1024]{2,1,0:T(8,128)(2,1)S(1)}, u32[]{:S(2)}, u32[]{:S(2)}) collective-permute-start(bf16[2,384,1024]{2,1,0:T(8,128)(2,1)S(1)} %copy-done.30), channel_id=1, source_target_pairs={{0,3},{1,2},{2,1},{3,0},{4,7},{5,6},{6,5},{7,4},{8,11},{9,10},{10,... | collective-permute-start | bytes 4718600 | tf_op jit(solution)/shard_map/ppermute | solution.py:440
  96.9 0.9 copy-start.8
  97.8 74.5 %collective-permute-start.21 = (bf16[2,192,1024]{2,1,0:T(8,128)(2,1)S(1)}, bf16[2,192,1024]{2,1,0:T(8,128)(2,1)S(1)}, u32[]{:S(2)}, u32[]{:S(2)}) collective-permute-start(bf16[2,192,1024]{2,1,0:T(8,128)(2,1)S(1)} %copy-done.32), channel_id=1, source_target_pairs={{1,3},{3,1},{5,7},{7,5},{9,11},{11,9},{13,15},{15,13},{17,19},{19,... | collective-permute-start | bytes 2359304 | tf_op jit(solution)/shard_map/ppermute | solution.py:559
  172.3 0.9 copy-start.10
  173.2 16.6 %collective-permute-start.7 = (bf16[2,384,1024]{2,1,0:T(8,128)(2,1)}, bf16[2,384,1024]{2,1,0:T(8,128)(2,1)}, u32[]{:S(2)}, u32[]{:S(2)}) collective-permute-start(bf16[2,384,1024]{2,1,0:T(8,128)(2,1)} %get-tuple-element.56), channel_id=1, source_target_pairs={{0,1},{1,0},{2,3},{3,2},{4,5},{5,4},{6,7},{7,6},{8,9},{9,8},{10,11... | collective-permute-start | bytes 4718600 | tf_op jit(solution)/shard_map/ppermute | solution.py:440
  173.2 1.1 copy-start.2
  174.3 35.8 %collective-permute-start.8 = (bf16[2,384,1024]{2,1,0:T(8,128)(2,1)}, bf16[2,384,1024]{2,1,0:T(8,128)(2,1)}, u32[]{:S(2)}, u32[]{:S(2)}) collective-permute-start(bf16[2,384,1024]{2,1,0:T(8,128)(2,1)} %get-tuple-element.57), channel_id=1, source_target_pairs={{0,2},{1,3},{2,0},{3,1},{4,6},{5,7},{6,4},{7,5},{8,10},{9,11},{10,... | collective-permute-start | bytes 4718600 | tf_op jit(solution)/shard_map/ppermute | solution.py:440
  175.0 70.4 %collective-permute-start.9 = (bf16[2,384,1024]{2,1,0:T(8,128)(2,1)}, bf16[2,384,1024]{2,1,0:T(8,128)(2,1)}, u32[]{:S(2)}, u32[]{:S(2)}) collective-permute-start(bf16[2,384,1024]{2,1,0:T(8,128)(2,1)} %get-tuple-element.58), channel_id=1, source_target_pairs={{0,3},{1,2},{2,1},{3,0},{4,7},{5,6},{6,5},{7,4},{8,11},{9,10},{10,... | collective-permute-start | bytes 4718600 | tf_op jit(solution)/shard_map/ppermute | solution.py:440
  176.5 95.4 %collective-permute-start.5 = (bf16[2,320,1024]{2,1,0:T(8,128)(2,1)}, bf16[2,320,1024]{2,1,0:T(8,128)(2,1)}, u32[]{:S(2)}, u32[]{:S(2)}) collective-permute-start(bf16[2,320,1024]{2,1,0:T(8,128)(2,1)} %get-tuple-element.54), channel_id=1, source_target_pairs={{0,2},{1,3},{2,0},{3,1},{4,6},{5,7},{6,4},{7,5},{8,10},{9,11},{10,... | collective-permute-start | bytes 3932168 | tf_op jit(solution)/shard_map/ppermute | solution.py:440
  177.2 1.1 copy-start
  178.3 123.3 %collective-permute-start.6 = (bf16[2,320,1024]{2,1,0:T(8,128)(2,1)}, bf16[2,320,1024]{2,1,0:T(8,128)(2,1)}, u32[]{:S(2)}, u32[]{:S(2)}) collective-permute-start(bf16[2,320,1024]{2,1,0:T(8,128)(2,1)} %get-tuple-element.55), channel_id=1, source_target_pairs={{0,3},{1,2},{2,1},{3,0},{4,7},{5,6},{6,5},{7,4},{8,11},{9,10},{10,... | collective-permute-start | bytes 3932168 | tf_op jit(solution)/shard_map/ppermute | solution.py:440
  187.5 57.9 %copy-start.4 = (bf16[2,224,1024]{2,1,0:T(8,128)(2,1)S(1)}, bf16[2,224,1024]{2,1,0:T(8,128)(2,1)}, u32[]{:S(2)}) copy-start(bf16[2,224,1024]{2,1,0:T(8,128)(2,1)} %get-tuple-element.75.refs_3_) | copy-start | bytes 2752516
  187.5 57.9 %copy-start.24 = (bf16[2,32,1024]{2,1,0:T(8,128)(2,1)S(1)}, bf16[2,32,1024]{2,1,0:T(8,128)(2,1)}, u32[]{:S(2)}) copy-start(bf16[2,32,1024]{2,1,0:T(8,128)(2,1)} %get-tuple-element.72.refs_0_) | copy-start | bytes 393220
  187.5 57.9 %copy-start.25 = (bf16[2,32,1024]{2,1,0:T(8,128)(2,1)S(1)}, bf16[2,32,1024]{2,1,0:T(8,128)(2,1)}, u32[]{:S(2)}) copy-start(bf16[2,32,1024]{2,1,0:T(8,128)(2,1)} %get-tuple-element.73.refs_1_) | copy-start | bytes 393220
  187.5 57.9 %copy-start.26 = (bf16[2,32,1024]{2,1,0:T(8,128)(2,1)S(1)}, bf16[2,32,1024]{2,1,0:T(8,128)(2,1)}, u32[]{:S(2)}) copy-start(bf16[2,32,1024]{2,1,0:T(8,128)(2,1)} %get-tuple-element.74.refs_2_) | copy-start | bytes 393220
  189.8 115.2 %collective-permute-start.1 = (bf16[2,32,1024]{2,1,0:T(8,128)(2,1)}, bf16[2,32,1024]{2,1,0:T(8,128)(2,1)S(1)}, u32[]{:S(2)}, u32[]{:S(2)}) collective-permute-start(bf16[2,32,1024]{2,1,0:T(8,128)(2,1)} %get-tuple-element.50), channel_id=1, source_target_pairs={{0,1},{1,0},{2,3},{3,2},{4,5},{5,4},{6,7},{7,6},{8,9},{9,8},{10,11... | collective-permute-start | bytes 393224 | tf_op jit(solution)/shard_map/ppermute | solution.py:440
  210.1 95.0 %collective-permute-start.2 = (bf16[2,32,1024]{2,1,0:T(8,128)(2,1)}, bf16[2,32,1024]{2,1,0:T(8,128)(2,1)S(1)}, u32[]{:S(2)}, u32[]{:S(2)}) collective-permute-start(bf16[2,32,1024]{2,1,0:T(8,128)(2,1)} %get-tuple-element.51), channel_id=1, source_target_pairs={{0,2},{1,3},{2,0},{3,1},{4,6},{5,7},{6,4},{7,5},{8,10},{9,11},{10,... | collective-permute-start | bytes 393224 | tf_op jit(solution)/shard_map/ppermute | solution.py:440
  245.4 60.7 %collective-permute-start.3 = (bf16[2,32,1024]{2,1,0:T(8,128)(2,1)}, bf16[2,32,1024]{2,1,0:T(8,128)(2,1)S(1)}, u32[]{:S(2)}, u32[]{:S(2)}) collective-permute-start(bf16[2,32,1024]{2,1,0:T(8,128)(2,1)} %get-tuple-element.52), channel_id=1, source_target_pairs={{0,3},{1,2},{2,1},{3,0},{4,7},{5,6},{6,5},{7,4},{8,11},{9,10},{10,... | collective-permute-start | bytes 393224 | tf_op jit(solution)/shard_map/ppermute | solution.py:440
  245.4 1.9 copy-start.5
  245.5 1.9 copy-start.7
  245.5 1.9 copy-start.9
  245.5 2.2 copy-start.11
  247.7 1.7 copy-start.13
  247.7 1.7 copy-start.15
  247.7 2.0 copy-start.17
  249.7 1.3 copy-start.19
  249.7 1.6 copy-start.21
  249.7 1.9 copy-start.23
  251.6 2.0 copy-start.1
  256.2 45.4 %copy-start.3 = (bf16[2,320,1024]{2,1,0:T(8,128)(2,1)S(1)}, bf16[2,320,1024]{2,1,0:T(8,128)(2,1)}, u32[]{:S(2)}) copy-start(bf16[2,320,1024]{2,1,0:T(8,128)(2,1)} %copy-done.2) | copy-start | bytes 3932164
